TPU v7x, 32 devices: a whole 2x2x4 slice. The times are simulated.
32 devices in a mesh: slab: 8 (over y, x, core), chan: 4 (over z).
Axes of the slice: x: 2, y: 2, z: 4, core: 2. Of those that a mesh axis runs over, the one named last changes fastest.
Arguments:
- features: bfloat16 [96, 16384], P('chan', 'slab'), may hold values from -1 to 3
- coords: bfloat16 [3, 16384], P(None, 'slab'), may hold values from 0 to 1
- send_rows: int32 [2, 8192], P(None, 'slab'), may hold values from 0 to 2047
- send_count: int32 [2, 8], P(None, 'slab'), may hold values from 1 to 1024, as said below
- neighbours: int32 [1024, 128], P('slab'), may hold values from 0 to 4095, as said below
- neighbour_count: int32 [1024], P('slab'), may hold values from 32 to 128
- geom_weight: bfloat16 [80, 6], replicated, may hold values from -3.5 to 3.5
- feat_weight: bfloat16 [80, 96], replicated, may hold values from -0.625 to 0.625
- bias_one: float32 [80], replicated, may hold values from -3 to 3
- hidden_weight: bfloat16 [80, 80], replicated, may hold values from -1 to 1
- bias_two: float32 [80], replicated, may hold values from -3 to 3
- out_weight: bfloat16 [96, 80], replicated, may hold values from -1 to 1
- bias_three: float32 [96], replicated, may hold values from -3 to 3
Outputs:
- latent: float32 [96, 1024], P('chan', 'slab')
Inputs may be any that keep to these rules, and one draw needn't show every extreme that they name: `send_count`: every slab has at least one live slot in each direction; some slab has all 1024 slots of its lower list live. `neighbours`: entries index the slab's point table: below 2048 own points, then 1024 slots from the slab below, then 1024 from the slab above; slot 0 of every node is an own point; nodes of the lower plane of a slab use the slots from below, those of the upper plane the slots from above, and may name dead slots.
All inputs are finite; a program needn't handle non-finite values.
Results may differ from a plain program's by a relative error of at most 0.0013.
Values may be sent and summed in bfloat16 or wider, within the bound.
No kernel may reach another device: no remote copies, remote signals or barrier semaphores. Data moves between devices by JAX's collectives and lax.ppermute only.
A program may use at most 64 MiB of HBM per device.

v0:
```python
import jax
import jax.numpy as jnp
from jax import lax
from jax.sharding import PartitionSpec as P

ZD = 2
GX = 16
GY = 4


def padded(block, sides, width):
    for axis, dim in sides:
        count = lax.axis_size(axis)
        forward = [(i, i + 1) for i in range(count - 1)]
        backward = [(target, source) for source, target in forward]
        low = lax.ppermute(
            lax.slice_in_dim(block, block.shape[dim] - width, None, axis=dim), axis, forward
        )
        high = lax.ppermute(lax.slice_in_dim(block, 0, width, axis=dim), axis, backward)
        block = jnp.concatenate([low, block, high], axis=dim)
    return block


def node_term(geom_weight, bias_one, node_ids, depth):
    along_x = ((node_ids % GX).astype(jnp.float32) + 0.5) / GX
    along_y = ((node_ids // GX % GY).astype(jnp.float32) + 0.5) / GY
    along_z = ((node_ids // (GX * GY)).astype(jnp.float32) + 0.5) / depth
    geom = geom_weight[:, 0:3].astype(jnp.float32)
    return (
        geom[:, 0:1] * along_x[None, :]
        + geom[:, 1:2] * along_y[None, :]
        + geom[:, 2:3] * along_z[None, :]
        + bias_one[:, None]
    )


def kernel_block(
    pre_table,
    value_table,
    flag_table,
    nbr,
    counts,
    node_pre,
    hidden_weight,
    bias_two,
    out_rows,
    bias_rows,
):
    nodes, slots = nbr.shape
    hidden = pre_table.shape[0]
    flat = nbr.reshape(-1)
    gathered = jnp.take(pre_table, flat, axis=1).astype(jnp.float32).reshape(hidden, nodes, slots)
    first = (
        jax.nn.gelu(gathered + node_pre[:, :, None])
        .reshape(hidden, nodes * slots)
        .astype(jnp.bfloat16)
    )
    second = jax.nn.gelu(
        jnp.dot(hidden_weight, first, preferred_element_type=jnp.float32) + bias_two[:, None]
    ).astype(jnp.bfloat16)
    kappa = jnp.dot(out_rows, second, preferred_element_type=jnp.float32) + bias_rows[:, None]
    values = jnp.take(value_table, flat, axis=1).astype(jnp.float32)
    used = (jnp.arange(slots, dtype=jnp.int32)[None, :] < counts[:, None]).astype(jnp.float32)
    flags = jnp.take(flag_table, flat).astype(jnp.float32) * used.reshape(-1)
    total = (kappa * values * flags[None, :]).reshape(out_rows.shape[0], nodes, slots).sum(axis=2)
    weight = flags.reshape(nodes, slots).sum(axis=1)
    return total / weight[None, :]


def encode(
    pre_table,
    value_table,
    flag_table,
    nbr,
    counts,
    first_id,
    depth,
    geom_weight,
    bias_one,
    hidden_weight,
    bias_two,
    out_rows,
    bias_rows,
):
    nodes = nbr.shape[0]
    block = min(128, nodes)
    blocks = nodes // block

    def one_block(index):
        start = index * block
        ids = first_id + start + jnp.arange(block, dtype=jnp.int32)
        node_pre = node_term(geom_weight, bias_one, ids, depth)
        return kernel_block(
            pre_table,
            value_table,
            flag_table,
            nbr,
            counts,
            node_pre,
            hidden_weight,
            bias_two,
            out_rows,
            bias_rows,
        )

    result = lax.map(one_block, jnp.arange(blocks, dtype=jnp.int32))
    return result.transpose(1, 0, 2).reshape(out_rows.shape[0], nodes)


def shards(
    features,
    coords,
    send_rows,
    send_count,
    neighbours,
    neighbour_count,
    geom_weight,
    feat_weight,
    bias_one,
    hidden_weight,
    bias_two,
    out_weight,
    bias_three,
):
    groups = lax.axis_size("chan")
    member = lax.axis_index("chan")
    slab_id = lax.axis_index("slab")
    depth = ZD * lax.axis_size("slab")
    own_full = lax.all_gather(features, "chan", axis=0, tiled=True)
    pre_own = (
        jnp.dot(feat_weight, own_full, preferred_element_type=jnp.float32)
        + jnp.dot(geom_weight[:, 3:6], coords, preferred_element_type=jnp.float32)
    ).astype(jnp.bfloat16)
    send = send_rows.shape[1]
    points = features.shape[1]
    hidden = pre_own.shape[0]
    chans = own_full.shape[0]
    columns = send_rows.reshape(-1)
    live = (
        (jnp.arange(send, dtype=jnp.int32)[None, :] < send_count)
        .astype(jnp.bfloat16)
        .reshape(1, 2 * send)
    )
    pre_sel = jnp.take(pre_own, columns, axis=1)
    val_sel = jnp.take(own_full, columns, axis=1)
    ones_row = jnp.ones((1, 2 * send), jnp.bfloat16)
    payload = jnp.concatenate([pre_sel, val_sel, ones_row], axis=0) * live
    extended = padded(payload, (("slab", 1),), send)
    below = extended[:, :send]
    above = extended[:, 3 * send :]
    below_pre = below[:hidden]
    above_pre = above[:hidden]
    below_vals = below[hidden : hidden + chans]
    above_vals = above[hidden : hidden + chans]
    below_flag = below[hidden + chans]
    above_flag = above[hidden + chans]
    pre_table = jnp.concatenate([pre_own, below_pre, above_pre], axis=1)
    value_table = jnp.concatenate([own_full, below_vals, above_vals], axis=1)
    flag_table = jnp.concatenate(
        [jnp.ones((points,), jnp.bfloat16), below_flag, above_flag], axis=0
    )
    per_slab = neighbours.shape[0]
    share = per_slab // groups
    start = member * share
    part_nbr = lax.dynamic_slice_in_dim(neighbours, start, share, 0)
    part_cnt = lax.dynamic_slice_in_dim(neighbour_count, start, share, 0)
    partial_value = encode(
        pre_table,
        value_table,
        flag_table,
        part_nbr,
        part_cnt,
        slab_id * per_slab + start,
        depth,
        geom_weight,
        bias_one,
        hidden_weight,
        bias_two,
        out_weight,
        bias_three,
    )
    return lax.all_to_all(partial_value, "chan", split_axis=0, concat_axis=1, tiled=True)


def solution(mesh):
    placed = (
        P("chan", "slab"),
        P(None, "slab"),
        P(None, "slab"),
        P(None, "slab"),
        P("slab", None),
        P("slab"),
        P(),
        P(),
        P(),
        P(),
        P(),
        P(),
        P(),
    )
    return jax.shard_map(
        shards, mesh=mesh, in_specs=placed, out_specs=P("chan", "slab"), check_vma=False
    )
```

profile of v0, /device:TPU:1, one launch (start us, length us, event | category | flops | bytes accessed | tf_op | source)
XLA Modules:
  0.0 116.7 jit_solution(4114827480123415698)
XLA Ops:
  0.0 0.0 copy-start
  0.0 0.0 copy-start.5
  0.0 0.7 compare_and_fusion.1
  0.8 0.7 fusion.37
  1.5 0.7 copy.71
  2.2 14.1 %all_gather.3 = bf16[96,2048]{1,0:T(8,128)(2,1)S(1)} all-gather(bf16[24,2048]{1,0:T(8,128)(2,1)} %param.13), channel_id=1, replica_groups=mesh['slab'=8,'chan'=4] {'chan'}, dimensions={0}, use_global_device_ids=true | all-gather | bytes 491520 | tf_op jit(solution)/shard_map/all_gather | solution.py:129
  16.3 0.3 copy.57
  16.6 0.0 copy-done.4
  16.6 0.2 fusion.59
  16.8 0.0 copy-done.6
  16.9 0.0 copy-done.5
  16.9 0.3 fusion.3
  17.2 0.3 copy.55
  17.4 6.2 %gather_fusion = bf16[2048,80]{1,0:T(8,128)(2,1)S(1)} fusion(bf16[80,2048]{0,1:T(8,128)(2,1)S(1)} %copy.55, s32[2048]{0:T(1024)S(1)} %broadcast_clamp_fusion.1), kind=kCustom, calls=%fused_computation | custom fusion | bytes 663552 | tf_op jit(solution)/shard_map/jit(_take)/gather | solution.py:144
  23.6 0.2 copy.56
  23.9 6.2 %gather_fusion.1 = bf16[2048,96]{1,0:T(8,128)(2,1)S(1)} fusion(bf16[96,2048]{0,1:T(8,128)(2,1)S(1)} %copy.57, s32[2048]{0:T(1024)S(1)} %broadcast_clamp_fusion.1), kind=kCustom, calls=%fused_computation.1 | custom fusion | bytes 794624 | tf_op jit(solution)/shard_map/jit(_take)/gather | solution.py:145
  30.0 0.2 copy.58
  30.4 0.1 pad.11.clone
  30.4 0.2 maximum_multiply_fusion
  30.7 0.1 fusion.58
  30.7 5.4 %collective-permute-start = (bf16[177,1024]{1,0:T(8,128)(2,1)S(1)}, bf16[177,1024]{1,0:T(8,128)(2,1)S(1)}, u32[]{:S(2)}, u32[]{:S(2)}) collective-permute-start(bf16[177,1024]{1,0:T(8,128)(2,1)S(1)} %get-tuple-element.33), channel_id=1, source_target_pairs={{0,4},{4,8},{8,12},{12,16},{16,20},{20,24},{24,28},{1,5},{5,9},{9,... | collective-permute-start | bytes 1087496 | tf_op jit(solution)/shard_map/ppermute | solution.py:16
  36.2 1.9 %collective-permute-start.1 = (bf16[177,1024]{1,0:T(8,128)(2,1)S(1)}, bf16[177,1024]{1,0:T(8,128)(2,1)S(1)}, u32[]{:S(2)}, u32[]{:S(2)}) collective-permute-start(bf16[177,1024]{1,0:T(8,128)(2,1)S(1)} %get-tuple-element.34), channel_id=1, source_target_pairs={{4,0},{8,4},{12,8},{16,12},{20,16},{24,20},{28,24},{5,1},{9,5},{13... | collective-permute-start | bytes 1087496 | tf_op jit(solution)/shard_map/ppermute | solution.py:19
  38.2 0.0 copy-done.3
  38.2 0.0 copy-done.7
  38.2 0.1 add_add_fusion
  38.3 0.0 copy-done.9
  38.3 0.1 dynamic_slice.10
  38.4 0.1 copy.61
  38.5 2.2 %collective-permute-done = bf16[177,1024]{1,0:T(8,128)(2,1)S(1)} collective-permute-done((bf16[177,1024]{1,0:T(8,128)(2,1)S(1)}, bf16[177,1024]{1,0:T(8,128)(2,1)S(1)}, u32[]{:S(2)}, u32[]{:S(2)}) %collective-permute-start) | collective-permute-done | bytes 362528 | tf_op jit(solution)/shard_map/ppermute | solution.py:16
  40.7 5.7 %collective-permute-done.1 = bf16[177,1024]{1,0:T(8,128)(2,1)S(1)} collective-permute-done((bf16[177,1024]{1,0:T(8,128)(2,1)S(1)}, bf16[177,1024]{1,0:T(8,128)(2,1)S(1)}, u32[]{:S(2)}, u32[]{:S(2)}) %collective-permute-start.1) | collective-permute-done | bytes 362528 | tf_op jit(solution)/shard_map/ppermute | solution.py:19
  46.4 25.6 %gather_fusion.4 = bf16[4096]{0:T(1024)(128)(2,1)S(1)} fusion(bf16[4096]{0:T(1024)(128)(2,1)S(1)} %pad_maximum_fusion.2, s32[4096]{0:T(1024)S(1)} %broadcast_clamp_fusion), kind=kCustom, calls=%fused_computation.4 | custom fusion | bytes 32768 | tf_op jit(solution)/shard_map/while/body/eval_jaxpr/jit(_take)/gather | solution.py:64
  72.1 0.2 select_reduce_fusion
  72.3 0.1 convert_select_fusion
  72.3 0.0 copy-done.1
  72.3 0.2 copy.63
  72.5 0.0 copy-done.2
  72.6 0.2 copy.64
  72.7 0.2 pad_maximum_fusion
  72.9 12.1 %gather_fusion.3 = bf16[4096,96]{1,0:T(8,128)(2,1)S(1)} fusion(bf16[96,4096]{0,1:T(8,128)(2,1)S(1)} %pad_maximum_fusion, s32[4096]{0:T(1024)S(1)} %broadcast_clamp_fusion), kind=kCustom, calls=%fused_computation.3 | custom fusion | bytes 1589248 | tf_op jit(solution)/shard_map/while/body/eval_jaxpr/jit(_take)/gather | solution.py:62
  85.1 0.0 slice-start
  85.1 0.0 slice-start.1
  85.1 1.2 %copy.65 = bf16[4096,96]{0,1:T(8,128)(2,1)} copy(bf16[4096,96]{1,0:T(8,128)(2,1)S(1)} %gather_fusion.3) | data formatting | bytes 1572864 | tf_op jit(solution)/shard_map/while/body/eval_jaxpr/jit(_take)/gather | solution.py:62
  86.4 0.0 slice-done
  86.4 0.0 slice-done.1
  86.4 0.6 copy.59
  87.1 12.1 %gather_fusion.2 = bf16[4096,80]{1,0:T(8,128)(2,1)S(1)} fusion(bf16[80,4096]{0,1:T(8,128)(2,1)S(1)} %copy.59, s32[4096]{0:T(1024)S(1)} %broadcast_clamp_fusion), kind=kCustom, calls=%fused_computation.2 | custom fusion | bytes 1327104 | tf_op jit(solution)/shard_map/while/body/eval_jaxpr/jit(_take)/gather | solution.py:52
  99.2 0.0 copy-start.8
  99.2 0.0 copy-start.10
  99.2 0.0 copy-start.11
  99.2 1.3 %copy.60 = bf16[4096,80]{0,1:T(8,128)(2,1)} copy(bf16[4096,80]{1,0:T(8,128)(2,1)S(1)} %gather_fusion.2) | data formatting | bytes 1310720 | tf_op jit(solution)/shard_map/while/body/eval_jaxpr/jit(_take)/gather | solution.py:52
  100.5 0.4 add.268
  100.9 0.0 copy-done
  100.9 3.2 %fusion.4 = f32[12,8,32,128]{3,1,2,0:T(8,128)S(1)} fusion(bf16[96,80]{0,1:T(8,128)(2,1)S(1)} %copy-done, bf16[80,80]{1,0:T(8,128)(2,1)S(1)} %copy-done.8, f32[4096]{0:T(1024)S(1)} %get-tuple-element.31, bf16[4096,96]{0,1:T(8,128)(2,1)} %copy.65, f32[96]{0:T(128)S(1)} %copy-done.10, pred[4096]{0:T(1024)(128)(4,1)S(1)} %get-tuple-element.32, ...), kind=kOutput, calls=%fused_computation.14 | convolution fusion | flops 124518400 | bytes 4374720 | tf_op jit(solution)/shard_map/while/body/eval_jaxpr/dot_general | solution.py:61
  104.2 0.3 copy.74
  104.5 0.5 reduce_sum.22
  105.0 0.1 copy.69
  105.0 0.1 broadcast_divide_fusion
  105.2 0.1 copy.67
  105.2 0.1 reshape.384
  105.3 9.3 %all_to_all.16 = f32[4,1,768]{2,1,0:T(1,128)S(1)} all-to-all(f32[4,1,768]{2,1,0:T(1,128)S(1)} %reshape.384), channel_id=1, replica_groups=mesh['slab'=8,'chan'=4] {'chan'}, dimensions={0} | all-to-all | bytes 24576 | tf_op jit(solution)/shard_map/all_to_all | solution.py:182
  114.7 0.5 broadcast.479
  115.2 0.7 reduce.4
  115.9 0.1 reshape.385
  116.0 0.7 all_to_all.14
  (30 shorter events, 0.3 us)
Async XLA Ops:
  0.0 100.9 %copy-start = (bf16[96,80]{0,1:T(8,128)(2,1)S(1)}, bf16[96,80]{0,1:T(8,128)(2,1)}, u32[]{:S(2)}) copy-start(bf16[96,80]{0,1:T(8,128)(2,1)} %param.24) | copy-start | bytes 46084
  0.0 16.6 %copy-start.4 = (bf16[80,96]{1,0:T(8,128)(2,1)S(1)}, bf16[80,96]{1,0:T(8,128)(2,1)}, u32[]{:S(2)}) copy-start(bf16[80,96]{1,0:T(8,128)(2,1)} %param.20) | copy-start | bytes 46084
  0.0 16.8 %copy-start.6 = (bf16[80,6]{0,1:T(8,128)(2,1)S(1)}, bf16[80,6]{0,1:T(8,128)(2,1)}, u32[]{:S(2)}) copy-start(bf16[80,6]{0,1:T(8,128)(2,1)} %param.19) | copy-start | bytes 2884
  0.0 16.8 %copy-start.5 = (bf16[3,2048]{1,0:T(4,128)(2,1)S(1)}, bf16[3,2048]{1,0:T(4,128)(2,1)}, u32[]{:S(2)}) copy-start(bf16[3,2048]{1,0:T(4,128)(2,1)} %param.14) | copy-start | bytes 36868
  30.4 7.7 %copy-start.3 = (s32[128,128]{1,0:T(8,128)S(1)}, s32[128,128]{1,0:T(8,128)}, u32[]{:S(2)}) copy-start(s32[128,128]{1,0:T(8,128)} %param.17) | copy-start | bytes 196612
  30.4 7.8 %copy-start.7 = (f32[80]{0:T(128)S(1)}, f32[80]{0:T(128)}, u32[]{:S(2)}) copy-start(f32[80]{0:T(128)} %param.21) | copy-start | bytes 964
  30.4 7.9 %copy-start.9 = (s32[128]{0:T(128)S(1)}, s32[128]{0:T(128)}, u32[]{:S(2)}) copy-start(s32[128]{0:T(128)} %param.18) | copy-start | bytes 1540
  30.7 9.9 %collective-permute-start = (bf16[177,1024]{1,0:T(8,128)(2,1)S(1)}, bf16[177,1024]{1,0:T(8,128)(2,1)S(1)}, u32[]{:S(2)}, u32[]{:S(2)}) collective-permute-start(bf16[177,1024]{1,0:T(8,128)(2,1)S(1)} %get-tuple-element.33), channel_id=1, source_target_pairs={{0,4},{4,8},{8,12},{12,16},{16,20},{20,24},{24,28},{1,5},{5,9},{9,... | collective-permute-start | bytes 1087496 | tf_op jit(solution)/shard_map/ppermute | solution.py:16
  36.2 10.2 %collective-permute-start.1 = (bf16[177,1024]{1,0:T(8,128)(2,1)S(1)}, bf16[177,1024]{1,0:T(8,128)(2,1)S(1)}, u32[]{:S(2)}, u32[]{:S(2)}) collective-permute-start(bf16[177,1024]{1,0:T(8,128)(2,1)S(1)} %get-tuple-element.34), channel_id=1, source_target_pairs={{4,0},{8,4},{12,8},{16,12},{20,16},{24,20},{28,24},{5,1},{9,5},{13... | collective-permute-start | bytes 1087496 | tf_op jit(solution)/shard_map/ppermute | solution.py:19
  40.7 31.6 %copy-start.1 = (bf16[177,1024]{1,0:T(8,128)(2,1)}, bf16[177,1024]{1,0:T(8,128)(2,1)S(1)}, u32[]{:S(2)}) copy-start(bf16[177,1024]{1,0:T(8,128)(2,1)S(1)} %collective-permute-done) | copy-start | bytes 1087492
  46.4 26.1 %copy-start.2 = (bf16[177,1024]{1,0:T(8,128)(2,1)}, bf16[177,1024]{1,0:T(8,128)(2,1)S(1)}, u32[]{:S(2)}) copy-start(bf16[177,1024]{1,0:T(8,128)(2,1)S(1)} %collective-permute-done.1) | copy-start | bytes 1087492
  85.1 1.3 %slice-start = ((bf16[177,1024]{1,0:T(8,128)(2,1)}), bf16[80,1024]{1,0:T(8,128)(2,1)S(1)}, s32[]{:S(2)}) async-start(bf16[177,1024]{1,0:T(8,128)(2,1)} %copy-done.1), calls=%async_computation.1 | async-start | bytes 327680 | tf_op jit(solution)/shard_map/slice | solution.py:151
  85.1 1.3 %slice-start.1 = ((bf16[177,1024]{1,0:T(8,128)(2,1)}), bf16[80,1024]{1,0:T(8,128)(2,1)S(1)}, s32[]{:S(2)}) async-start(bf16[177,1024]{1,0:T(8,128)(2,1)} %copy-done.2), calls=%async_computation.2 | async-start | bytes 327680 | tf_op jit(solution)/shard_map/slice | solution.py:152
  99.2 1.7 %copy-start.8 = (bf16[80,80]{1,0:T(8,128)(2,1)S(1)}, bf16[80,80]{1,0:T(8,128)(2,1)}, u32[]{:S(2)}) copy-start(bf16[80,80]{1,0:T(8,128)(2,1)} %param.22) | copy-start | bytes 38404
  99.2 1.7 %copy-start.10 = (f32[96]{0:T(128)S(1)}, f32[96]{0:T(128)}, u32[]{:S(2)}) copy-start(f32[96]{0:T(128)} %param.25) | copy-start | bytes 1156
  99.2 1.7 %copy-start.11 = (f32[80]{0:T(128)S(1)}, f32[80]{0:T(128)}, u32[]{:S(2)}) copy-start(f32[80]{0:T(128)} %param.23) | copy-start | bytes 964
where the time goes:
time: 117 us
  local copies, waits for them, and re-layouts  70.1 us (60%)
  blocking collectives  23.4 us (20%)
  waiting for transfers between devices  7.85 us (7%)
  starting transfers between devices  7.34 us (6%)
  matrix products  3.76 us (3%)
  other arithmetic  3.72 us (3%)
    gather x1, local copies, waits for them, and re-layouts, kernel_block(): flags = jnp.take(flag_table, flat).astype(jnp.float32) * used.reshape(-1)  25.6 us
    all_gather x1, blocking collectives, shards(): own_full = lax.all_gather(features, 'chan', axis=0, tiled=True)  14.1 us
    gather x2, local copies, waits for them, and re-layouts, kernel_block(): jnp.take(pre_table, flat, axis=1).astype(jnp.float32)  13.4 us
    gather x2, local copies, waits for them, and re-layouts, kernel_block(): values = jnp.take(value_table, flat, axis=1).astype(jnp.float32)  13.4 us
    all_to_all x1, blocking collectives, shards(): lax.all_to_all(partial_value, 'chan', split_axis=0, concat_axis=1, tiled=...  9.35 us
    gather x2, local copies, waits for them, and re-layouts, shards(): val_sel = jnp.take(own_full, columns, axis=1)  6.4 us
    gather x2, local copies, waits for them, and re-layouts, shards(): pre_sel = jnp.take(pre_own, columns, axis=1)  6.4 us
    ppermute x1, waiting for transfers between devices, padded(): lax.ppermute(lax.slice_in_dim(block, 0, width, axis=dim), axis, backward)  5.66 us
  transfers between devices with their start and end apart: 2, of which 2 were waited for; matrix products, arithmetic and copies ran while one was open for 0% of the time, Pallas kernels for 0%

commit v1 on v0

v1 whole, which is shorter than its diff:
```python
import jax
import jax.numpy as jnp
from jax import lax
from jax.experimental import pallas as pl
from jax.experimental.pallas import tpu as pltpu
from jax.sharding import PartitionSpec as P

ZD = 2
GX = 16
GY = 4
LANES = 128


def node_term(geom, bias, ids, depth):
    along_x = ((ids % GX).astype(jnp.float32) + 0.5) / GX
    along_y = ((ids // GX % GY).astype(jnp.float32) + 0.5) / GY
    along_z = ((ids // (GX * GY)).astype(jnp.float32) + 0.5) / depth
    return geom[0:1] * along_x + geom[1:2] * along_y + geom[2:3] * along_z + bias


def select_points(blocks, coords, send_rows, send_count, place):
    groups = len(blocks)
    chans, points = blocks[0].shape
    width = LANES // groups
    send = send_rows.shape[1]
    unroll = 16

    def kernel(*refs):
        block_refs = refs[:groups]
        coords_ref, rows_ref, count_ref, place_ref = refs[groups : groups + 4]
        own_ref, sent_ref, stack, table, picked = refs[groups + 4 :]
        member = place_ref[0]
        side = place_ref[1]
        for step in range(groups):
            base = pl.multiple_of((member ^ step) * width, width)
            empty = jnp.zeros((width - chans, points), jnp.bfloat16)
            stack[pl.ds(base, width), :] = jnp.concatenate([block_refs[step][...], empty], axis=0)
        stack[chans : chans + 3, :] = coords_ref[...]
        stack[chans + 3 : chans + 4, :] = jnp.ones((1, points), jnp.bfloat16)
        own = stack[...].T
        own_ref[...] = own
        table[...] = own.astype(jnp.float32)

        def gather(step, carry):
            base = step * unroll
            rows = [table[pl.ds(rows_ref[side, base + j], 1), :] for j in range(unroll)]
            for j in range(unroll):
                picked[pl.ds(base + j, 1), :] = rows[j]
            return carry

        lax.fori_loop(0, send // unroll, gather, 0)
        slot = lax.broadcasted_iota(jnp.int32, (send, LANES), 0)
        sent_ref[...] = jnp.where(slot < count_ref[side, 0], picked[...], 0.0).astype(jnp.bfloat16)

    smem = pl.BlockSpec(memory_space=pltpu.SMEM)
    vmem = pl.BlockSpec(memory_space=pltpu.VMEM)
    return pl.pallas_call(
        kernel,
        out_shape=(
            jax.ShapeDtypeStruct((points, LANES), jnp.bfloat16),
            jax.ShapeDtypeStruct((send, LANES), jnp.bfloat16),
        ),
        in_specs=[vmem] * (groups + 1) + [smem] * 3,
        out_specs=(vmem, vmem),
        scratch_shapes=[
            pltpu.VMEM((LANES, points), jnp.bfloat16),
            pltpu.VMEM((points, LANES), jnp.float32),
            pltpu.VMEM((send, LANES), jnp.float32),
        ],
        name="select_points",
    )(*blocks, coords, send_rows, send_count, place)


def encode(own, other, rows, place, table_weight, hidden_weight, out_weight, vectors, groups, chans, per_slab, depth):
    points = own.shape[0]
    send = other.shape[0]
    nodes, slots = rows.shape
    total_rows = points + send
    width = LANES // groups
    unroll = 16
    group_nodes = 8
    pairs = group_nodes * slots

    def kernel(own_ref, other_ref, rows_ref, place_ref, table_w, hidden_w, out_w, vec_ref, *rest):
        outs = rest[:groups]
        table, picked, acc, turned = rest[groups:]
        member = place_ref[0]
        first_id = place_ref[2]

        def fill(source, start, count):
            step = 256
            for at in range(0, count, step):
                both = jnp.dot(source[pl.ds(at, step), :], table_w[...], preferred_element_type=jnp.float32)
                pre = both[:, :LANES].astype(jnp.bfloat16).astype(jnp.float32)
                table[pl.ds(2 * (start + at), step, stride=2), :] = pre
                table[pl.ds(2 * (start + at) + 1, step, stride=2), :] = both[:, LANES:]

        fill(own_ref, 0, points)
        fill(other_ref, points, send)
        table[pl.ds(2 * total_rows, 8), :] = jnp.zeros((8, LANES), jnp.float32)

        acc[...] = jnp.zeros((LANES, LANES), jnp.float32)
        vec = vec_ref[...]
        bias_two = vec[4:5]
        bias_three = vec[5:6]

        def one_group(index, carry):
            start = index * group_nodes

            def gather(step, inner):
                node = step // (slots // unroll)
                slot = (step % (slots // unroll)) * unroll
                got = [
                    table[pl.ds(rows_ref[start + node, slot + j], 2), :] for j in range(unroll)
                ]
                for j in range(unroll):
                    picked[pl.ds(2 * (step * unroll + j), 2), :] = got[j]
                return inner

            lax.fori_loop(0, pairs // unroll, gather, 0)
            ids = first_id + start + lax.broadcasted_iota(jnp.int32, (group_nodes, 1), 0)
            node_pre = node_term(vec[0:3], vec[3:4], ids, depth)
            for node in range(group_nodes):
                pre = picked[pl.ds(2 * node * slots, slots, stride=2), :]
                val = picked[pl.ds(2 * node * slots + 1, slots, stride=2), :]
                first = jax.nn.gelu(pre + node_pre[node : node + 1]).astype(jnp.bfloat16)
                second = jnp.dot(first, hidden_w[...], preferred_element_type=jnp.float32)
                second = jax.nn.gelu(second + bias_two).astype(jnp.bfloat16)
                kappa = jnp.dot(second, out_w[...], preferred_element_type=jnp.float32) + bias_three
                total = jnp.sum(kappa * val, axis=0, keepdims=True)
                acc[pl.ds(member * nodes + start + node, 1), :] = total
            return carry

        lax.fori_loop(0, nodes // group_nodes, one_group, 0)
        flag_lane = chans + 3
        sums = acc[...]
        weight = sums[:, flag_lane : flag_lane + 1]
        here = lax.broadcasted_iota(jnp.int32, (LANES, 1), 0)
        mine = (here >= member * nodes) & (here < (member + 1) * nodes)
        scaled = sums / jnp.where(mine, weight, 1.0)
        turned[...] = scaled.T
        for step in range(groups):
            base = pl.multiple_of((member ^ step) * width, width)
            outs[step][...] = turned[pl.ds(base, chans), :]

    smem = pl.BlockSpec(memory_space=pltpu.SMEM)
    vmem = pl.BlockSpec(memory_space=pltpu.VMEM)
    return pl.pallas_call(
        kernel,
        out_shape=tuple(jax.ShapeDtypeStruct((chans, per_slab), jnp.float32) for _ in range(groups)),
        in_specs=[vmem, vmem, smem, smem] + [vmem] * 4,
        out_specs=(vmem,) * groups,
        scratch_shapes=[
            pltpu.VMEM((2 * total_rows + 8, LANES), jnp.float32),
            pltpu.VMEM((2 * pairs, LANES), jnp.float32),
            pltpu.VMEM((LANES, LANES), jnp.float32),
            pltpu.VMEM((LANES, LANES), jnp.float32),
        ],
        name="encode",
    )(own, other, rows, place, table_weight, hidden_weight, out_weight, vectors)


def shards(
    features,
    coords,
    send_rows,
    send_count,
    neighbours,
    neighbour_count,
    geom_weight,
    feat_weight,
    bias_one,
    hidden_weight,
    bias_two,
    out_weight,
    bias_three,
):
    groups = lax.axis_size("chan")
    slabs = lax.axis_size("slab")
    member = lax.axis_index("chan")
    slab_id = lax.axis_index("slab")
    depth = ZD * slabs
    chans, points = features.shape
    send = send_rows.shape[1]
    per_slab, slots = neighbours.shape
    hidden = hidden_weight.shape[0]
    share = per_slab // groups
    width = LANES // groups
    half = groups // ZD

    blocks = [features]
    for step in range(1, groups):
        blocks.append(lax.ppermute(features, "chan", [(i, i ^ step) for i in range(groups)]))

    upper = (member < half).astype(jnp.int32)
    first_id = slab_id * per_slab + member * share
    place = jnp.stack([member, upper, first_id]).astype(jnp.int32)
    own, sent = select_points(blocks, coords, send_rows, send_count, place)
    pairs = []
    for slab in range(slabs):
        for who in range(groups):
            target = slab + 1 if who < half else slab - 1
            if 0 <= target < slabs:
                pairs.append((slab * groups + who, target * groups + who))
    other = lax.ppermute(sent, ("slab", "chan"), pairs)

    part_nbr = lax.dynamic_slice_in_dim(neighbours, member * share, share, 0)
    part_cnt = lax.dynamic_slice_in_dim(neighbour_count, member * share, share, 0)
    row = jnp.where(part_nbr >= points + send, part_nbr - send, part_nbr)
    slot = lax.broadcasted_iota(jnp.int32, (share, slots), 1)
    rows = 2 * jnp.where(slot < part_cnt[:, None], row, points + send)

    def lanes_of(weight):
        lead = weight.shape[:-1]
        split = weight.reshape(lead + (groups, chans))
        return jnp.pad(split, [(0, 0)] * len(lead) + [(0, 0), (0, width - chans)]).reshape(lead + (LANES,))

    feat_rows = lanes_of(feat_weight)
    spot = jnp.arange(LANES)
    geom = jnp.pad(geom_weight[:, 3:6], ((0, 0), (chans, LANES - chans - 3)))
    pre_weight = jnp.pad((feat_rows + geom).T, ((0, 0), (0, LANES - hidden)))
    table_weight = jnp.concatenate([pre_weight, jnp.eye(LANES, dtype=jnp.bfloat16)], axis=1)
    hidden_t = jnp.pad(hidden_weight.T, ((0, LANES - hidden), (0, LANES - hidden)))
    out_t = jnp.pad(lanes_of(out_weight.T), ((0, LANES - hidden), (0, 0)))
    tail = (0, LANES - hidden)
    vectors = jnp.concatenate(
        [
            jnp.pad(geom_weight[:, 0:3].astype(jnp.float32).T, ((0, 0), tail)),
            jnp.pad(bias_one, tail)[None],
            jnp.pad(bias_two, tail)[None],
            (lanes_of(bias_three) + (spot == chans + 3))[None],
            jnp.zeros((2, LANES), jnp.float32),
        ],
        axis=0,
    )
    pieces = encode(
        own, other, rows, place, table_weight, hidden_t, out_t, vectors, groups, chans, per_slab, depth
    )
    result = pieces[0]
    for step in range(1, groups):
        result = result + lax.ppermute(pieces[step], "chan", [(i, i ^ step) for i in range(groups)])
    return result


def solution(mesh):
    placed = (
        P("chan", "slab"),
        P(None, "slab"),
        P(None, "slab"),
        P(None, "slab"),
        P("slab", None),
        P("slab"),
        P(),
        P(),
        P(),
        P(),
        P(),
        P(),
        P(),
    )
    return jax.shard_map(
        shards, mesh=mesh, in_specs=placed, out_specs=P("chan", "slab"), check_vma=False
    )
```

time: 117 us -> 52.5 us (0.45)
  the two profiles are of different devices: /device:TPU:1 before, /device:TPU:12 now
where the time goes in v1:
time: 52.5 us; the launch traced here: 52.1 us
  Pallas kernels  20.9 us (40%)
  waiting for transfers between devices  10.9 us (21%)
  starting transfers between devices  9.01 us (17%)
  local copies, waits for them, and re-layouts  7.15 us (14%)
  other arithmetic  3.95 us (8%)
    pallas_call x1, Pallas kernels, encode(): pl.pallas_call(kernel, out_shape=tuple((jax.ShapeDtypeStruct((chans, per_...  15.9 us
    pallas_call x1, Pallas kernels, select_points(): pl.pallas_call(kernel, out_shape=(jax.ShapeDtypeStruct((points, LANES), j...  5.02 us
    unnamed x30, local copies, waits for them, and re-layouts  4.93 us
    ppermute x3, waiting for transfers between devices, shards(): lax.ppermute(features, 'chan', [(i, i ^ step) for i in range(groups)])  4.68 us
    ppermute x3, waiting for transfers between devices, shards(): lax.ppermute(pieces[step], 'chan', [(i, i ^ step) for i in range(groups)])  3.81 us
    ppermute x3, starting transfers between devices, shards(): lax.ppermute(features, 'chan', [(i, i ^ step) for i in range(groups)])  3.49 us
    ppermute x3, starting transfers between devices, shards(): lax.ppermute(pieces[step], 'chan', [(i, i ^ step) for i in range(groups)])  3.48 us
    ppermute x1, waiting for transfers between devices, shards(): other = lax.ppermute(sent, ('slab', 'chan'), pairs)  2.41 us
  transfers between devices with their start and end apart: 7, of which 6 were waited for; matrix products, arithmetic and copies ran while one was open for 11% of the time, Pallas kernels for 0%

profile of v1, /device:TPU:12, one launch (start us, length us, event | category | flops | bytes accessed | tf_op | source)
XLA Modules:
  0.0 52.1 jit_solution(10574946185082658966)
XLA Ops:
  0.0 0.4 collective-permute-start
  0.5 2.6 %collective-permute-start.1 = (bf16[24,2048]{1,0:T(8,128)(2,1)}, bf16[24,2048]{1,0:T(8,128)(2,1)S(1)}, u32[]{:S(2)}, u32[]{:S(2)}) collective-permute-start(bf16[24,2048]{1,0:T(8,128)(2,1)} %refs_0_.1), channel_id=1, source_target_pairs={{0,2},{1,3},{2,0},{3,1},{4,6},{5,7},{6,4},{7,5},{8,10},{9,11},{10,... | collective-permute-start | bytes 294920 | tf_op jit(solution)/shard_map/ppermute | solution.py:193
  3.0 0.5 collective-permute-start.2
  3.5 0.0 copy-start.11
  3.5 0.0 copy-start.4
  3.5 0.6 %copy-done.11 = s32[2,1]{0,1:T(1,128)S(1)} copy-done((s32[2,1]{0,1:T(1,128)S(1)}, s32[2,1]{0,1:T(1,128)}, u32[]{:S(2)}) %copy-start.11) | copy-done | bytes 32
  4.1 0.6 %copy.17.refs_6_ = s32[2,1]{1,0:T(2,128)} copy(s32[2,1]{0,1:T(1,128)S(1)} %copy-done.11) | data formatting | bytes 16 | tf_op args[3]
  4.8 0.0 copy-done.4
  4.8 0.0 copy-start.7
  4.8 0.1 copy.18
  4.9 0.6 %copy-done.7 = bf16[80,6]{0,1:T(8,128)(2,1)S(1)} copy-done((bf16[80,6]{0,1:T(8,128)(2,1)S(1)}, bf16[80,6]{0,1:T(8,128)(2,1)}, u32[]{:S(2)}) %copy-start.7) | copy-done | bytes 984
  5.5 0.0 copy-start.8
  5.5 0.6 %copy-done.8 = f32[96]{0:T(128)S(1)} copy-done((f32[96]{0:T(128)S(1)}, f32[96]{0:T(128)}, u32[]{:S(2)}) %copy-start.8) | copy-done | bytes 408
  6.1 0.1 reshape.43
  6.2 0.1 reshape.44
  6.4 0.6 %fusion.1.table_w = bf16[128,256]{1,0:T(8,128)(2,1)} fusion(bf16[128,80]{1,0:T(8,128)(2,1)S(1)} %bitcast.19, bf16[128,128]{1,0:T(8,128)(2,1)S(1)} %fusion.2), kind=kLoop, calls=%fused_computation.2 | loop fusion | flops 196608 | bytes 118784 | tf_op jit(solution)/shard_map/concatenate | solution.py:222
  7.0 0.6 %pad_add_fusion.refs_7_.place_ref = s32[3]{0:T(128)} fusion(s32[1]{0:T(128)} %bitcast.2, s32[1]{0:T(128)} %bitcast.1, s32[1]{0:T(128)} %bitcast), kind=kLoop, calls=%fused_computation.15 | loop fusion | flops 6 | bytes 24 | tf_op jit(solution)/shard_map/stack | solution.py:197
  7.6 0.0 collective-permute-done.refs_1_
  7.6 0.0 copy-start.1
  7.6 2.8 %collective-permute-done.1.refs_2_ = bf16[24,2048]{1,0:T(8,128)(2,1)S(1)} collective-permute-done((bf16[24,2048]{1,0:T(8,128)(2,1)}, bf16[24,2048]{1,0:T(8,128)(2,1)S(1)}, u32[]{:S(2)}, u32[]{:S(2)}) %collective-permute-start.1) | collective-permute-done | bytes 98336 | tf_op jit(solution)/shard_map/ppermute | solution.py:193
  10.4 0.0 copy-start.2
  10.4 1.9 %collective-permute-done.2.refs_3_ = bf16[24,2048]{1,0:T(8,128)(2,1)S(1)} collective-permute-done((bf16[24,2048]{1,0:T(8,128)(2,1)}, bf16[24,2048]{1,0:T(8,128)(2,1)S(1)}, u32[]{:S(2)}, u32[]{:S(2)}) %collective-permute-start.2) | collective-permute-done | bytes 98336 | tf_op jit(solution)/shard_map/ppermute | solution.py:193
  12.3 0.0 copy-done.1
  12.3 0.0 copy-done.2
  12.3 0.0 copy-start.3
  12.3 0.6 %copy-done.3 = bf16[24,2048]{1,0:T(8,128)(2,1)} copy-done((bf16[24,2048]{1,0:T(8,128)(2,1)}, bf16[24,2048]{1,0:T(8,128)(2,1)S(1)}, u32[]{:S(2)}) %copy-start.3) | copy-done | bytes 98328
  12.9 0.0 copy-start.5
  12.9 5.0 %select_points.1 = (bf16[2048,128]{1,0:T(8,128)(2,1)}, bf16[1024,128]{1,0:T(8,128)(2,1)}) custom-call(bf16[24,2048]{1,0:T(8,128)(2,1)} %refs_0_.1, bf16[24,2048]{1,0:T(8,128)(2,1)} %copy-done.1, bf16[24,2048]{1,0:T(8,128)(2,1)} %copy-done.2, bf16[24,2048]{1,0:T(8,128)(2,1)} %copy-done.3, bf16[3,2048]{1,0:T(4,128)(2,1)} %refs_4_.1, s32[2,1024]{1,0:T(2,128)} %refs_5_.1, ...), custom_call_target="tpu_custom_call" | custom-call | tf_op jit(solution)/shard_map/select_points/pallas_call | solution.py:57
  17.9 0.0 copy-start.9
  17.9 0.0 copy-start.10
  17.9 2.0 %collective-permute-start.3 = (bf16[1024,128]{1,0:T(8,128)(2,1)}, bf16[1024,128]{1,0:T(8,128)(2,1)S(1)}, u32[]{:S(2)}, u32[]{:S(2)}) collective-permute-start(bf16[1024,128]{1,0:T(8,128)(2,1)} %get-tuple-element.12), channel_id=1, source_target_pairs={{0,4},{1,5},{4,8},{5,9},{6,2},{7,3},{8,12},{9,13},{10,6},{11,7},{1... | collective-permute-start | bytes 786440 | tf_op jit(solution)/shard_map/ppermute | solution.py:205
  20.0 0.0 copy-done.9
  20.0 0.0 copy-done.10
  20.0 0.0 copy-done.5
  20.0 0.1 copy.19
  20.1 0.0 copy-start.6
  20.1 0.6 %pad.44.hidden_w = bf16[128,128]{1,0:T(8,128)(2,1)} pad(bf16[80,80]{1,0:T(8,128)(2,1)S(1)} %bitcast.22, bf16[]{:T(256)} %constant.29.clone.1), padding=0_48x0_48 | pad | bytes 45570 | tf_op jit(solution)/shard_map/jit(_pad)/pad | solution.py:223
  20.7 0.1 copy-done.6
  20.9 0.1 copy.20
  21.0 0.1 copy.21
  21.1 0.6 %pad.46.out_w = bf16[128,128]{1,0:T(8,128)(2,1)} pad(bf16[80,128]{1,0:T(8,128)(2,1)S(1)} %copy.21, bf16[]{:T(256)} %constant.29.clone.1), padding=0_48x0_0 | pad | bytes 53250 | tf_op jit(solution)/shard_map/jit(_pad)/pad | solution.py:224
  21.7 0.0 copy-start.12
  21.7 0.7 %copy-done.12 = s32[128]{0:T(128)S(1)} copy-done((s32[128]{0:T(128)S(1)}, s32[128]{0:T(128)}, u32[]{:S(2)}) %copy-start.12) | copy-done | bytes 536
  22.4 0.1 dynamic_slice.6
  22.4 0.6 %concatenate.7.vec_ref = f32[8,128]{1,0:T(8,128)} concatenate(f32[3,128]{1,0:T(4,128)S(1)} %pad_convert_fusion, f32[1,128]{1,0:T(1,128)S(1)} %get-tuple-element.20, f32[1,128]{1,0:T(1,128)S(1)} %get-tuple-element.19, f32[1,128]{1,0:T(1,128)S(1)} %fusion.5, f32[2,128]{1,0:T(2,128)S(1)} %broadcast_in_dim.15), dimensions={0} | concatenate | bytes 8192 | tf_op jit(solution)/shard_map/concatenate | solution.py:226
  23.1 1.4 %fusion.4.rows_ref = s32[32,128]{1,0:T(8,128)} fusion(s32[128,128]{1,0:T(8,128)} %param.17, s32[]{:T(128)S(6)} %select_n.12, s32[32]{0:T(128)S(1)} %dynamic_slice.6), kind=kLoop, calls=%fused_computation.8 | loop fusion | flops 24576 | bytes 32900 | tf_op jit(solution)/shard_map/mul | solution.py:211
  24.4 2.4 %collective-permute-done.3.other_ref = bf16[1024,128]{1,0:T(8,128)(2,1)S(1)} collective-permute-done((bf16[1024,128]{1,0:T(8,128)(2,1)}, bf16[1024,128]{1,0:T(8,128)(2,1)S(1)}, u32[]{:S(2)}, u32[]{:S(2)}) %collective-permute-start.3) | collective-permute-done | bytes 262176 | tf_op jit(solution)/shard_map/ppermute | solution.py:205
  26.9 0.0 copy-start
  26.9 0.7 %copy-done = bf16[1024,128]{1,0:T(8,128)(2,1)} copy-done((bf16[1024,128]{1,0:T(8,128)(2,1)}, bf16[1024,128]{1,0:T(8,128)(2,1)S(1)}, u32[]{:S(2)}) %copy-start) | copy-done | bytes 262168
  27.5 15.9 %encode.1 = (f32[24,128]{1,0:T(8,128)}, f32[24,128]{1,0:T(8,128)}, f32[24,128]{1,0:T(8,128)}, f32[24,128]{1,0:T(8,128)}) custom-call(bf16[2048,128]{1,0:T(8,128)(2,1)} %get-tuple-element.11.own_ref, bf16[1024,128]{1,0:T(8,128)(2,1)} %copy-done, s32[32,128]{1,0:T(8,128)} %fusion.4.rows_ref, s32[3]{0:T(128)} %pad_add_fusion.refs_7_.place_ref, ...), custom_call_target="tpu_custom_call" | custom-call | tf_op jit(solution)/shard_map/encode/pallas_call | solution.py:148
  43.4 0.0 collective-permute-start.6
  43.4 3.4 %collective-permute-start.5 = (f32[24,128]{1,0:T(8,128)}, f32[24,128]{1,0:T(8,128)S(1)}, u32[]{:S(2)}, u32[]{:S(2)}) collective-permute-start(f32[24,128]{1,0:T(8,128)} %get-tuple-element.15), channel_id=1, source_target_pairs={{0,2},{1,3},{2,0},{3,1},{4,6},{5,7},{6,4},{7,5},{8,10},{9,11},{10,... | collective-permute-start | bytes 36872 | tf_op jit(solution)/shard_map/ppermute | solution.py:241
  46.8 0.1 collective-permute-start.4
  46.9 0.4 collective-permute-done.6
  47.3 1.5 %collective-permute-done.5 = f32[24,128]{1,0:T(8,128)S(1)} collective-permute-done((f32[24,128]{1,0:T(8,128)}, f32[24,128]{1,0:T(8,128)S(1)}, u32[]{:S(2)}, u32[]{:S(2)}) %collective-permute-start.5) | collective-permute-done | bytes 12320 | tf_op jit(solution)/shard_map/ppermute | solution.py:241
  48.8 1.9 %collective-permute-done.4 = f32[24,128]{1,0:T(8,128)S(1)} collective-permute-done((f32[24,128]{1,0:T(8,128)}, f32[24,128]{1,0:T(8,128)S(1)}, u32[]{:S(2)}, u32[]{:S(2)}) %collective-permute-start.4) | collective-permute-done | bytes 12320 | tf_op jit(solution)/shard_map/ppermute | solution.py:241
  50.7 1.3 %add_add_fusion = f32[24,128]{1,0:T(8,128)} fusion(f32[24,128]{1,0:T(8,128)S(1)} %collective-permute-done.6, f32[24,128]{1,0:T(8,128)S(1)} %collective-permute-done.5, f32[24,128]{1,0:T(8,128)} %get-tuple-element.13, f32[24,128]{1,0:T(8,128)S(1)} %collective-permute-done.4), kind=kLoop, calls=%fused_computation.10 | loop fusion | flops 9216 | bytes 61440 | tf_op jit(solution)/shard_map/add | solution.py:241
  (10 shorter events, 0.1 us)
Async XLA Ops:
  0.0 7.6 %collective-permute-start = (bf16[24,2048]{1,0:T(8,128)(2,1)}, bf16[24,2048]{1,0:T(8,128)(2,1)S(1)}, u32[]{:S(2)}, u32[]{:S(2)}) collective-permute-start(bf16[24,2048]{1,0:T(8,128)(2,1)} %refs_0_.1), channel_id=1, source_target_pairs={{0,1},{1,0},{2,3},{3,2},{4,5},{5,4},{6,7},{7,6},{8,9},{9,8},{10,11... | collective-permute-start | bytes 294920 | tf_op jit(solution)/shard_map/ppermute | solution.py:193
  0.5 9.9 %collective-permute-start.1 = (bf16[24,2048]{1,0:T(8,128)(2,1)}, bf16[24,2048]{1,0:T(8,128)(2,1)S(1)}, u32[]{:S(2)}, u32[]{:S(2)}) collective-permute-start(bf16[24,2048]{1,0:T(8,128)(2,1)} %refs_0_.1), channel_id=1, source_target_pairs={{0,2},{1,3},{2,0},{3,1},{4,6},{5,7},{6,4},{7,5},{8,10},{9,11},{10,... | collective-permute-start | bytes 294920 | tf_op jit(solution)/shard_map/ppermute | solution.py:193
  3.0 9.2 %collective-permute-start.2 = (bf16[24,2048]{1,0:T(8,128)(2,1)}, bf16[24,2048]{1,0:T(8,128)(2,1)S(1)}, u32[]{:S(2)}, u32[]{:S(2)}) collective-permute-start(bf16[24,2048]{1,0:T(8,128)(2,1)} %refs_0_.1), channel_id=1, source_target_pairs={{0,3},{1,2},{2,1},{3,0},{4,7},{5,6},{6,5},{7,4},{8,11},{9,10},{10,... | collective-permute-start | bytes 294920 | tf_op jit(solution)/shard_map/ppermute | solution.py:193
  3.5 0.7 %copy-start.11 = (s32[2,1]{0,1:T(1,128)S(1)}, s32[2,1]{0,1:T(1,128)}, u32[]{:S(2)}) copy-start(s32[2,1]{0,1:T(1,128)} %param.16) | copy-start | bytes 28
  3.5 1.3 %copy-start.4 = (bf16[80,96]{1,0:T(8,128)(2,1)S(1)}, bf16[80,96]{1,0:T(8,128)(2,1)}, u32[]{:S(2)}) copy-start(bf16[80,96]{1,0:T(8,128)(2,1)} %param.20) | copy-start | bytes 46084
  4.8 0.7 %copy-start.7 = (bf16[80,6]{0,1:T(8,128)(2,1)S(1)}, bf16[80,6]{0,1:T(8,128)(2,1)}, u32[]{:S(2)}) copy-start(bf16[80,6]{0,1:T(8,128)(2,1)} %param.19) | copy-start | bytes 2884
  5.5 0.7 %copy-start.8 = (f32[96]{0:T(128)S(1)}, f32[96]{0:T(128)}, u32[]{:S(2)}) copy-start(f32[96]{0:T(128)} %param.25) | copy-start | bytes 1156
  7.6 4.7 %copy-start.1 = (bf16[24,2048]{1,0:T(8,128)(2,1)}, bf16[24,2048]{1,0:T(8,128)(2,1)S(1)}, u32[]{:S(2)}) copy-start(bf16[24,2048]{1,0:T(8,128)(2,1)S(1)} %collective-permute-done.refs_1_) | copy-start | bytes 294916
  10.4 1.9 %copy-start.2 = (bf16[24,2048]{1,0:T(8,128)(2,1)}, bf16[24,2048]{1,0:T(8,128)(2,1)S(1)}, u32[]{:S(2)}) copy-start(bf16[24,2048]{1,0:T(8,128)(2,1)S(1)} %collective-permute-done.1.refs_2_) | copy-start | bytes 294916
  12.3 0.6 %copy-start.3 = (bf16[24,2048]{1,0:T(8,128)(2,1)}, bf16[24,2048]{1,0:T(8,128)(2,1)S(1)}, u32[]{:S(2)}) copy-start(bf16[24,2048]{1,0:T(8,128)(2,1)S(1)} %collective-permute-done.2.refs_3_) | copy-start | bytes 294916
  12.9 7.1 %copy-start.5 = (bf16[80,80]{1,0:T(8,128)(2,1)S(1)}, bf16[80,80]{1,0:T(8,128)(2,1)}, u32[]{:S(2)}) copy-start(bf16[80,80]{1,0:T(8,128)(2,1)} %param.22) | copy-start | bytes 38404
  17.9 2.1 %copy-start.9 = (f32[80]{0:T(128)S(1)}, f32[80]{0:T(128)}, u32[]{:S(2)}) copy-start(f32[80]{0:T(128)} %param.23) | copy-start | bytes 964
  17.9 2.1 %copy-start.10 = (f32[80]{0:T(128)S(1)}, f32[80]{0:T(128)}, u32[]{:S(2)}) copy-start(f32[80]{0:T(128)} %param.21) | copy-start | bytes 964
  17.9 8.9 %collective-permute-start.3 = (bf16[1024,128]{1,0:T(8,128)(2,1)}, bf16[1024,128]{1,0:T(8,128)(2,1)S(1)}, u32[]{:S(2)}, u32[]{:S(2)}) collective-permute-start(bf16[1024,128]{1,0:T(8,128)(2,1)} %get-tuple-element.12), channel_id=1, source_target_pairs={{0,4},{1,5},{4,8},{5,9},{6,2},{7,3},{8,12},{9,13},{10,6},{11,7},{1... | collective-permute-start | bytes 786440 | tf_op jit(solution)/shard_map/ppermute | solution.py:205
  20.1 0.7 %copy-start.6 = (bf16[96,80]{0,1:T(8,128)(2,1)S(1)}, bf16[96,80]{0,1:T(8,128)(2,1)}, u32[]{:S(2)}) copy-start(bf16[96,80]{0,1:T(8,128)(2,1)} %param.24) | copy-start | bytes 46084
  21.7 0.7 %copy-start.12 = (s32[128]{0:T(128)S(1)}, s32[128]{0:T(128)}, u32[]{:S(2)}) copy-start(s32[128]{0:T(128)} %param.18) | copy-start | bytes 1540
  26.9 0.7 %copy-start = (bf16[1024,128]{1,0:T(8,128)(2,1)}, bf16[1024,128]{1,0:T(8,128)(2,1)S(1)}, u32[]{:S(2)}) copy-start(bf16[1024,128]{1,0:T(8,128)(2,1)S(1)} %collective-permute-done.3.other_ref) | copy-start | bytes 786436
  43.4 3.9 %collective-permute-start.6 = (f32[24,128]{1,0:T(8,128)}, f32[24,128]{1,0:T(8,128)S(1)}, u32[]{:S(2)}, u32[]{:S(2)}) collective-permute-start(f32[24,128]{1,0:T(8,128)} %get-tuple-element.16), channel_id=1, source_target_pairs={{0,3},{1,2},{2,1},{3,0},{4,7},{5,6},{6,5},{7,4},{8,11},{9,10},{10,... | collective-permute-start | bytes 36872 | tf_op jit(solution)/shard_map/ppermute | solution.py:241
  43.4 5.4 %collective-permute-start.5 = (f32[24,128]{1,0:T(8,128)}, f32[24,128]{1,0:T(8,128)S(1)}, u32[]{:S(2)}, u32[]{:S(2)}) collective-permute-start(f32[24,128]{1,0:T(8,128)} %get-tuple-element.15), channel_id=1, source_target_pairs={{0,2},{1,3},{2,0},{3,1},{4,6},{5,7},{6,4},{7,5},{8,10},{9,11},{10,... | collective-permute-start | bytes 36872 | tf_op jit(solution)/shard_map/ppermute | solution.py:241
  46.8 3.9 %collective-permute-start.4 = (f32[24,128]{1,0:T(8,128)}, f32[24,128]{1,0:T(8,128)S(1)}, u32[]{:S(2)}, u32[]{:S(2)}) collective-permute-start(f32[24,128]{1,0:T(8,128)} %get-tuple-element.14), channel_id=1, source_target_pairs={{0,1},{1,0},{2,3},{3,2},{4,5},{5,4},{6,7},{7,6},{8,9},{9,8},{10,11... | collective-permute-start | bytes 36872 | tf_op jit(solution)/shard_map/ppermute | solution.py:241

commit v2 on v1

v2 whole, which is shorter than its diff:
```python
import jax
import jax.numpy as jnp
from jax import lax
from jax.experimental import pallas as pl
from jax.experimental.pallas import tpu as pltpu
from jax.sharding import PartitionSpec as P

ZD = 2
GX = 16
GY = 4
LANES = 128
CHUNK = 16
BLOCK = 64

SMEM = pl.BlockSpec(memory_space=pltpu.SMEM)
VMEM = pl.BlockSpec(memory_space=pltpu.VMEM)
ANY = pl.BlockSpec(memory_space=pl.ANY)


def node_term(geom, bias, ids, depth):
    along_x = ((ids % GX).astype(jnp.float32) + 0.5) / GX
    along_y = ((ids // GX % GY).astype(jnp.float32) + 0.5) / GY
    along_z = ((ids // (GX * GY)).astype(jnp.float32) + 0.5) / depth
    return geom[0:1] * along_x + geom[1:2] * along_y + geom[2:3] * along_z + bias


def plan_pairs(neighbours, neighbour_count, place, nodes, points, send):
    slots = neighbours.shape[1]
    per_node = slots // CHUNK
    most = nodes * per_node
    nothing = 2 * (points + send)

    def kernel(nbr_ref, count_ref, place_ref, rows_ref, list_ref, total_ref):
        start = place_ref[3]
        lane = lax.broadcasted_iota(jnp.int32, (1, slots), 1)

        def one_node(node, at):
            count = count_ref[start + node]
            row = nbr_ref[pl.ds(start + node, 1), :]
            row = jnp.where(row >= points + send, row - send, row)
            rows_ref[pl.ds(node, 1), :] = jnp.where(lane < count, 2 * row, nothing)
            for piece in range(per_node):
                list_ref[at + piece] = node * per_node + piece
            return at + (count + CHUNK - 1) // CHUNK

        used = lax.fori_loop(0, nodes, one_node, 0)
        rows_ref[pl.ds(nodes, 8), :] = jnp.full((8, slots), nothing, jnp.int32)
        total_ref[0] = (used + BLOCK - 1) // BLOCK

        def fill(step, carry):
            list_ref[used + step] = most
            return carry

        lax.fori_loop(0, BLOCK, fill, 0)

    return pl.pallas_call(
        kernel,
        out_shape=(
            jax.ShapeDtypeStruct((nodes + 8, slots), jnp.int32),
            jax.ShapeDtypeStruct((most + BLOCK,), jnp.int32),
            jax.ShapeDtypeStruct((1,), jnp.int32),
        ),
        in_specs=[VMEM, SMEM, SMEM],
        out_specs=(VMEM, SMEM, SMEM),
        name="plan_pairs",
    )(neighbours, neighbour_count, place)


def select_points(blocks, coords, send_rows, send_count, place, after):
    groups = len(blocks)
    chans, points = blocks[0].shape
    width = LANES // groups
    send = send_rows.shape[0] // 2
    unroll = 32

    def kernel(*refs):
        block_refs = refs[:groups]
        coords_ref, rows_ref, count_ref, place_ref = refs[groups : groups + 4]
        own_ref, sent_ref, stack, table, picked = refs[groups + 4 + len(after) :]
        member = place_ref[0]
        side = place_ref[1]
        for step in range(groups):
            base = pl.multiple_of((member ^ step) * width, width)
            empty = jnp.zeros((width - chans, points), jnp.bfloat16)
            stack[pl.ds(base, width), :] = jnp.concatenate([block_refs[step][...], empty], axis=0)
        stack[chans : chans + 3, :] = coords_ref[...]
        stack[chans + 3 : chans + 4, :] = jnp.ones((1, points), jnp.bfloat16)
        own = stack[...].T
        own_ref[...] = own
        table[...] = own.astype(jnp.float32)

        def gather(step, carry):
            base = step * unroll
            first = side * send + base
            rows = [table[pl.ds(rows_ref[first + j], 1), :] for j in range(unroll)]
            for j in range(unroll):
                picked[pl.ds(base + j, 1), :] = rows[j]
            return carry

        lax.fori_loop(0, send // unroll, gather, 0)
        slot = lax.broadcasted_iota(jnp.int32, (send, LANES), 0)
        sent_ref[...] = jnp.where(slot < count_ref[side, 0], picked[...], 0.0).astype(jnp.bfloat16)

    return pl.pallas_call(
        kernel,
        out_shape=(
            jax.ShapeDtypeStruct((points, LANES), jnp.bfloat16),
            jax.ShapeDtypeStruct((send, LANES), jnp.bfloat16),
        ),
        in_specs=[VMEM] * (groups + 1) + [SMEM] * 3 + [ANY] * len(after),
        out_specs=(VMEM, VMEM),
        scratch_shapes=[
            pltpu.VMEM((LANES, points), jnp.bfloat16),
            pltpu.VMEM((points, LANES), jnp.float32),
            pltpu.VMEM((send, LANES), jnp.float32),
        ],
        name="select_points",
    )(*blocks, coords, send_rows, send_count, place, *after)


def encode(own, other, plan, place, weights, chans, width, depth):
    rows, chunks, total = plan
    table_weight, hidden_weight, out_weight, vectors = weights
    points = own.shape[0]
    send = other.shape[0]
    nodes = rows.shape[0] - 8
    slots = rows.shape[1]
    shift = (slots // CHUNK).bit_length() - 1
    total_rows = points + send
    pairs = BLOCK * CHUNK
    all_nodes = ZD * nodes

    def kernel(
        own_ref, other_ref, rows_ref, list_ref, total_ref, place_ref, table_w, hidden_w, out_w,
        vec_ref, keep_ref, give_ref, table, picked, node_pre, acc, turned,
    ):
        parity = place_ref[1]
        first_id = place_ref[2]

        def fill(source, start, count):
            step = 256
            for at in range(0, count, step):
                both = jnp.dot(source[pl.ds(at, step), :], table_w[...], preferred_element_type=jnp.float32)
                pre = both[:, :LANES].astype(jnp.bfloat16).astype(jnp.float32)
                table[pl.ds(2 * (start + at), step, stride=2), :] = pre
                table[pl.ds(2 * (start + at) + 1, step, stride=2), :] = both[:, LANES:]

        fill(own_ref, 0, points)
        fill(other_ref, points, send)
        table[pl.ds(2 * total_rows, 8), :] = jnp.zeros((8, LANES), jnp.float32)

        vec = vec_ref[...]
        bias_two = vec[4:5]
        bias_three = vec[5:6]
        ids = first_id + lax.broadcasted_iota(jnp.int32, (nodes + 8, 1), 0)
        node_pre[...] = node_term(vec[0:3], vec[3:4], ids, depth)
        acc[...] = jnp.zeros((nodes + 8, LANES), jnp.float32)

        def one_block(index, carry):
            names = [list_ref[index * BLOCK + piece] for piece in range(BLOCK)]
            for piece in range(BLOCK):
                at = names[piece] * CHUNK
                got = [table[pl.ds(rows_ref[at + j], 2), :] for j in range(CHUNK)]
                for j in range(CHUNK):
                    picked[pl.ds(2 * (piece * CHUNK + j), 2), :] = got[j]
            step = 8
            for group in range(BLOCK // step):
                base = group * step * CHUNK
                offset = jnp.concatenate(
                    [
                        jnp.broadcast_to(
                            node_pre[pl.ds(names[group * step + i] >> shift, 1), :], (CHUNK, LANES)
                        )
                        for i in range(step)
                    ],
                    axis=0,
                )
                pre = picked[pl.ds(2 * base, step * CHUNK, stride=2), :]
                val = picked[pl.ds(2 * base + 1, step * CHUNK, stride=2), :]
                first = jax.nn.gelu(pre + offset).astype(jnp.bfloat16)
                second = jnp.dot(first, hidden_w[...], preferred_element_type=jnp.float32)
                second = jax.nn.gelu(second + bias_two).astype(jnp.bfloat16)
                kappa = jnp.dot(second, out_w[...], preferred_element_type=jnp.float32) + bias_three
                product = kappa * val
                for i in range(step):
                    part = jnp.sum(product[i * CHUNK : (i + 1) * CHUNK], axis=0, keepdims=True)
                    spot = pl.ds(names[group * step + i] >> shift, 1)
                    acc[spot, :] = acc[spot, :] + part
            return carry

        lax.fori_loop(0, total_ref[0], one_block, 0)
        sums = acc[0:nodes]
        means = (sums / sums[:, LANES - 1 :]).T
        blank = jnp.zeros((LANES, nodes), jnp.float32)
        low = jnp.where(parity == 1, means, blank)
        turned[...] = jnp.concatenate([low, means - low], axis=1)
        mine = pl.multiple_of((1 - parity) * width, width)
        theirs = pl.multiple_of(parity * width, width)
        keep_ref[...] = turned[pl.ds(mine, chans), :]
        give_ref[...] = turned[pl.ds(theirs, chans), :]

    piece = jax.ShapeDtypeStruct((chans, all_nodes), jnp.float32)
    return pl.pallas_call(
        kernel,
        out_shape=(piece, piece),
        in_specs=[VMEM, VMEM] + [SMEM] * 4 + [VMEM] * 4,
        out_specs=(VMEM, VMEM),
        scratch_shapes=[
            pltpu.VMEM((2 * total_rows + 8, LANES), jnp.float32),
            pltpu.VMEM((2 * pairs, LANES), jnp.float32),
            pltpu.VMEM((nodes + 8, LANES), jnp.float32),
            pltpu.VMEM((nodes + 8, LANES), jnp.float32),
            pltpu.VMEM((LANES, all_nodes), jnp.float32),
        ],
        name="encode",
    )(
        own, other, rows.reshape(-1), chunks, total, place, table_weight, hidden_weight, out_weight,
        vectors,
    )


def shards(
    features,
    coords,
    send_rows,
    send_count,
    neighbours,
    neighbour_count,
    geom_weight,
    feat_weight,
    bias_one,
    hidden_weight,
    bias_two,
    out_weight,
    bias_three,
):
    groups = lax.axis_size("chan")
    slabs = lax.axis_size("slab")
    member = lax.axis_index("chan")
    slab_id = lax.axis_index("slab")
    depth = ZD * slabs
    chans, points = features.shape
    send = send_rows.shape[1]
    per_slab = neighbours.shape[0]
    hidden = hidden_weight.shape[0]
    nodes = per_slab // ZD
    width = LANES // groups

    blocks = [features]
    for step in range(1, groups):
        blocks.append(lax.ppermute(features, "chan", [(i, i ^ step) for i in range(groups)]))

    plane = member % 2
    start = plane * nodes
    upper = 1 - plane
    place = jnp.stack([member, upper, slab_id * per_slab + start, start]).astype(jnp.int32)
    plan = plan_pairs(neighbours, neighbour_count, place, nodes, points, send)

    def lanes_of(weight):
        lead = weight.shape[:-1]
        split = weight.reshape(lead + (groups, chans))
        return jnp.pad(split, [(0, 0)] * len(lead) + [(0, 0), (0, width - chans)]).reshape(lead + (LANES,))

    first_lane = (member // 2) * 2 * width

    def pair_of(weight):
        part = lax.dynamic_slice_in_dim(lanes_of(weight), first_lane, 2 * width, weight.ndim - 1)
        return jnp.pad(part, [(0, 0)] * (weight.ndim - 1) + [(0, LANES - 2 * width)])

    row = jnp.arange(LANES)[:, None]
    lane = jnp.arange(LANES)[None, :]
    take = ((row == first_lane + lane) & (lane < 2 * width)) | ((row == chans + 3) & (lane == LANES - 1))
    geom = jnp.pad(geom_weight[:, 3:6], ((0, 0), (chans, LANES - chans - 3)))
    pre_weight = jnp.pad((lanes_of(feat_weight) + geom).T, ((0, 0), (0, LANES - hidden)))
    table_weight = jnp.concatenate([pre_weight, take.astype(jnp.bfloat16)], axis=1)
    hidden_t = jnp.pad(hidden_weight.T, ((0, LANES - hidden), (0, LANES - hidden)))
    out_t = jnp.pad(pair_of(out_weight.T), ((0, LANES - hidden), (0, 0)))
    tail = (0, LANES - hidden)
    vectors = jnp.concatenate(
        [
            jnp.pad(geom_weight[:, 0:3].astype(jnp.float32).T, ((0, 0), tail)),
            jnp.pad(bias_one, tail)[None],
            jnp.pad(bias_two, tail)[None],
            pair_of(bias_three)[None] + (lane == LANES - 1),
            jnp.zeros((2, LANES), jnp.float32),
        ],
        axis=0,
    )
    weights = (table_weight, hidden_t, out_t, vectors)

    own, sent = select_points(
        blocks, coords, send_rows.reshape(-1), send_count, place, plan + weights
    )
    moves = []
    for slab in range(slabs):
        for who in range(groups):
            target = slab + 1 if who % 2 == 0 else slab - 1
            if 0 <= target < slabs:
                moves.append((slab * groups + who, target * groups + who))
    other = lax.ppermute(sent, ("slab", "chan"), moves)
    keep, give = encode(own, other, plan, place, weights, chans, width, depth)
    return keep + lax.ppermute(give, "chan", [(i, i ^ 1) for i in range(groups)])


def solution(mesh):
    placed = (
        P("chan", "slab"),
        P(None, "slab"),
        P(None, "slab"),
        P(None, "slab"),
        P("slab", None),
        P("slab"),
        P(),
        P(),
        P(),
        P(),
        P(),
        P(),
        P(),
    )
    return jax.shard_map(
        shards, mesh=mesh, in_specs=placed, out_specs=P("chan", "slab"), check_vma=False
    )
```

time: 52.5 us -> 47.4 us (0.903)
  the two profiles are of different devices: /device:TPU:12 before, /device:TPU:4 now
where the time goes in v2:
time: 47.4 us; the launch traced here: 46.9 us
  Pallas kernels  19.2 us (41%)
  waiting for transfers between devices  10.8 us (23%)
  local copies, waits for them, and re-layouts  7.81 us (16%)
  starting transfers between devices  6.3 us (13%)
  other arithmetic  2.68 us (6%)
    pallas_call x1, Pallas kernels, encode(): pl.pallas_call(kernel, out_shape=(piece, piece), in_specs=[VMEM, VMEM] +...  12.4 us
    ppermute x1, waiting for transfers between devices, shards(): other = lax.ppermute(sent, ('slab', 'chan'), moves)  6.87 us
    unnamed x32, local copies, waits for them, and re-layouts  5.66 us
    ppermute x3, starting transfers between devices, shards(): lax.ppermute(features, 'chan', [(i, i ^ step) for i in range(groups)])  4.39 us
    ppermute x1, waiting for transfers between devices, shards(): lax.ppermute(give, 'chan', [(i, i ^ 1) for i in range(groups)])  3.9 us
    pallas_call x1, Pallas kernels, select_points(): pl.pallas_call(kernel, out_shape=(jax.ShapeDtypeStruct((points, LANES), j...  3.85 us
    pallas_call x1, Pallas kernels, plan_pairs(): pl.pallas_call(kernel, out_shape=(jax.ShapeDtypeStruct((nodes + 8, slots)...  2.95 us
    ppermute x1, starting transfers between devices, shards(): other = lax.ppermute(sent, ('slab', 'chan'), moves)  1.91 us
  transfers between devices with their start and end apart: 5, of which 2 were waited for; matrix products, arithmetic and copies ran while one was open for 11% of the time, Pallas kernels for 6%

profile of v2, /device:TPU:4, one launch (start us, length us, event | category | flops | bytes accessed | tf_op | source)
XLA Modules:
  0.0 46.9 jit_solution(1292732898940092567)
XLA Ops:
  0.0 2.6 %collective-permute-start.1 = (bf16[24,2048]{1,0:T(8,128)(2,1)}, bf16[24,2048]{1,0:T(8,128)(2,1)S(1)}, u32[]{:S(2)}, u32[]{:S(2)}) collective-permute-start(bf16[24,2048]{1,0:T(8,128)(2,1)} %refs_0_.1), channel_id=1, source_target_pairs={{0,2},{1,3},{2,0},{3,1},{4,6},{5,7},{6,4},{7,5},{8,10},{9,11},{10,... | collective-permute-start | bytes 294920 | tf_op jit(solution)/shard_map/ppermute | solution.py:251
  2.6 1.6 %collective-permute-start = (bf16[24,2048]{1,0:T(8,128)(2,1)}, bf16[24,2048]{1,0:T(8,128)(2,1)S(1)}, u32[]{:S(2)}, u32[]{:S(2)}) collective-permute-start(bf16[24,2048]{1,0:T(8,128)(2,1)} %refs_0_.1), channel_id=1, source_target_pairs={{0,1},{1,0},{2,3},{3,2},{4,5},{5,4},{6,7},{7,6},{8,9},{9,8},{10,11... | collective-permute-start | bytes 294920 | tf_op jit(solution)/shard_map/ppermute | solution.py:251
  4.2 0.2 collective-permute-start.2
  4.4 0.0 copy-start.11
  4.4 0.0 copy-start.12
  4.4 0.0 copy-start.9
  4.4 0.0 copy-start.8
  4.5 0.0 copy-start.7
  4.5 0.6 %copy-done.11 = f32[80]{0:T(128)S(1)} copy-done((f32[80]{0:T(128)S(1)}, f32[80]{0:T(128)}, u32[]{:S(2)}) %copy-start.11) | copy-done | bytes 344
  5.1 0.0 copy-start.4
  5.1 0.0 copy-done.12
  5.1 0.7 %copy.21.refs_6_ = s32[2,1]{1,0:T(2,128)} copy(s32[2,1]{0,1:T(1,128)S(1)} %copy-done.12) | data formatting | bytes 16 | tf_op args[3]
  5.7 0.0 copy-done.9
  5.7 0.1 reshape.51
  5.8 0.1 reshape.52
  5.9 0.0 copy-done.8
  5.9 0.0 copy-done.7
  6.0 0.6 %copy.25 = s32[1,8,2,128]{3,1,2,0:T(8,128)} copy(s32[1,8,2,128]{3,2,1,0:T(2,128)S(1)} %bitcast.33) | data formatting | bytes 16384
  6.6 0.0 copy-done.4
  6.6 0.0 copy-start.5
  6.6 0.1 copy.18
  6.7 0.6 %copy-done.5 = bf16[80,96]{1,0:T(8,128)(2,1)S(1)} copy-done((bf16[80,96]{1,0:T(8,128)(2,1)S(1)}, bf16[80,96]{1,0:T(8,128)(2,1)}, u32[]{:S(2)}) %copy-start.5) | copy-done | bytes 15384
  7.3 0.1 copy.17
  7.4 0.6 %pad.52.refs_12_.hidden_w = bf16[128,128]{1,0:T(8,128)(2,1)} pad(bf16[80,80]{1,0:T(8,128)(2,1)S(1)} %bitcast.30, bf16[]{:T(256)} %constant.47.clone.1), padding=0_48x0_48 | pad | bytes 45570 | tf_op jit(solution)/shard_map/jit(_pad)/pad | solution.py:276
  8.0 0.0 copy-start.6
  8.0 0.7 %copy-done.6 = bf16[96,80]{0,1:T(8,128)(2,1)S(1)} copy-done((bf16[96,80]{0,1:T(8,128)(2,1)S(1)}, bf16[96,80]{0,1:T(8,128)(2,1)}, u32[]{:S(2)}) %copy-start.6) | copy-done | bytes 15384
  8.7 0.1 copy.19
  8.9 0.1 dynamic_slice.7
  9.0 0.1 copy.22
  9.1 0.6 %pad.69.refs_13_.out_w = bf16[128,128]{1,0:T(8,128)(2,1)} pad(bf16[80,64]{1,0:T(8,128)(2,1)S(1)} %copy.22, bf16[]{:T(256)} %constant.47.clone.1), padding=0_48x0_64 | pad | bytes 43010 | tf_op jit(solution)/shard_map/jit(_pad)/pad | solution.py:277
  9.7 0.0 copy-start.10
  9.7 0.7 %copy-done.10 = f32[80]{0:T(128)S(1)} copy-done((f32[80]{0:T(128)S(1)}, f32[80]{0:T(128)}, u32[]{:S(2)}) %copy-start.10) | copy-done | bytes 344
  10.4 0.6 %pad_add_fusion.place_ref.refs_7_ = s32[4]{0:T(128)} fusion(s32[1]{0:T(128)} %bitcast.3, s32[1]{0:T(128)} %bitcast.2, s32[1]{0:T(128)} %bitcast.1, s32[1]{0:T(128)} %bitcast), kind=kLoop, calls=%fused_computation.11 | loop fusion | flops 12 | bytes 32 | tf_op jit(solution)/shard_map/stack | solution.py:256
  11.0 3.0 %plan_pairs.1 = (s32[72,128]{1,0:T(8,128)}, s32[576]{0:T(1024)}, s32[1]{0:T(128)}) custom-call(s32[128,128]{1,0:T(8,128)} %nbr_ref.1, s32[128]{0:T(128)} %count_ref.1, s32[4]{0:T(128)} %pad_add_fusion.place_ref.refs_7_), custom_call_target="tpu_custom_call" | custom-call | tf_op jit(solution)/shard_map/plan_pairs/pallas_call | solution.py:56
  13.9 0.1 fusion.4
  14.0 0.6 %concatenate.7.refs_14_.vec_ref = f32[8,128]{1,0:T(8,128)} concatenate(f32[3,128]{1,0:T(4,128)S(1)} %pad_convert_fusion, f32[1,128]{1,0:T(1,128)S(1)} %pad_bitcast_fusion.1, f32[1,128]{1,0:T(1,128)S(1)} %get-tuple-element.24, f32[1,128]{1,0:T(1,128)S(1)} %get-tuple-element.23, f32[2,128]{1,0:T(2,128)S(1)} %broadcast_in_dim.14), dimensions={0} | concatenate | bytes 8192 | tf_op jit(solution)/shard_map/concatenate | solution.py:279
  14.6 0.6 %fusion.1.refs_11_.table_w = bf16[128,256]{1,0:T(8,128)(2,1)} fusion(bf16[128,80]{1,0:T(8,128)(2,1)S(1)} %bitcast.27, bf16[128,128]{1,0:T(8,128)(2,1)S(1)} %fusion.4), kind=kLoop, calls=%fused_computation.2 | loop fusion | flops 196608 | bytes 118784 | tf_op jit(solution)/shard_map/concatenate | solution.py:275
  15.3 0.0 collective-permute-done.1.refs_2_
  15.3 0.0 copy-start.1
  15.3 0.0 collective-permute-done.refs_1_
  15.3 0.0 copy-start.2
  15.3 0.0 collective-permute-done.2.refs_3_
  15.3 0.0 copy-start.3
  15.3 0.6 %copy-done.1 = bf16[24,2048]{1,0:T(8,128)(2,1)} copy-done((bf16[24,2048]{1,0:T(8,128)(2,1)}, bf16[24,2048]{1,0:T(8,128)(2,1)S(1)}, u32[]{:S(2)}) %copy-start.1) | copy-done | bytes 98328
  15.9 0.0 copy-done.2
  15.9 0.0 copy-done.3
  16.0 3.9 %select_points.1 = (bf16[2048,128]{1,0:T(8,128)(2,1)}, bf16[1024,128]{1,0:T(8,128)(2,1)}) custom-call(bf16[24,2048]{1,0:T(8,128)(2,1)} %refs_0_.1, bf16[24,2048]{1,0:T(8,128)(2,1)} %copy-done.2, bf16[24,2048]{1,0:T(8,128)(2,1)} %copy-done.1, bf16[24,2048]{1,0:T(8,128)(2,1)} %copy-done.3, bf16[3,2048]{1,0:T(4,128)(2,1)} %refs_4_.1, s32[2048]{0:T(1024)} %bitcast.32, ...), custom_call_target="tpu_custom_call" | custom-call | tf_op jit(solution)/shard_map/select_points/pallas_call | solution.py:104
  19.8 1.9 %collective-permute-start.3 = (bf16[1024,128]{1,0:T(8,128)(2,1)}, bf16[1024,128]{1,0:T(8,128)(2,1)S(1)}, u32[]{:S(2)}, u32[]{:S(2)}) collective-permute-start(bf16[1024,128]{1,0:T(8,128)(2,1)} %get-tuple-element.16), channel_id=1, source_target_pairs={{0,4},{2,6},{4,8},{5,1},{6,10},{7,3},{8,12},{9,5},{10,14},{11,7},{... | collective-permute-start | bytes 786440 | tf_op jit(solution)/shard_map/ppermute | solution.py:300
  21.8 6.9 %collective-permute-done.3.other_ref = bf16[1024,128]{1,0:T(8,128)(2,1)S(1)} collective-permute-done((bf16[1024,128]{1,0:T(8,128)(2,1)}, bf16[1024,128]{1,0:T(8,128)(2,1)S(1)}, u32[]{:S(2)}, u32[]{:S(2)}) %collective-permute-start.3) | collective-permute-done | bytes 262176 | tf_op jit(solution)/shard_map/ppermute | solution.py:300
  28.6 0.0 copy-start
  28.6 0.7 %copy-done = bf16[1024,128]{1,0:T(8,128)(2,1)} copy-done((bf16[1024,128]{1,0:T(8,128)(2,1)}, bf16[1024,128]{1,0:T(8,128)(2,1)S(1)}, u32[]{:S(2)}) %copy-start) | copy-done | bytes 262168
  29.3 12.4 %encode.1 = (f32[24,128]{1,0:T(8,128)}, f32[24,128]{1,0:T(8,128)}) custom-call(bf16[2048,128]{1,0:T(8,128)(2,1)} %get-tuple-element.15.own_ref, bf16[1024,128]{1,0:T(8,128)(2,1)} %copy-done, s32[9216]{0:T(1024)} %bitcast.26, s32[576]{0:T(1024)} %get-tuple-element.13.refs_9_.list_ref, s32[1]{0:T(128)} %get-tuple-element.14.refs_10_.total_ref, ...), custom_call_target="tpu_custom_call" | custom-call | tf_op jit(solution)/shard_map/encode/pallas_call | solution.py:203
  41.7 0.0 collective-permute-start.4
  41.7 3.9 %collective-permute-done.4 = f32[24,128]{1,0:T(8,128)S(1)} collective-permute-done((f32[24,128]{1,0:T(8,128)}, f32[24,128]{1,0:T(8,128)S(1)}, u32[]{:S(2)}, u32[]{:S(2)}) %collective-permute-start.4) | collective-permute-done | bytes 12320 | tf_op jit(solution)/shard_map/ppermute | solution.py:302
  45.6 1.3 %add.67 = f32[24,128]{1,0:T(8,128)} add(f32[24,128]{1,0:T(8,128)} %get-tuple-element.17, f32[24,128]{1,0:T(8,128)S(1)} %collective-permute-done.4) | non-fusion elementwise | flops 3072 | bytes 36864 | tf_op jit(solution)/shard_map/add | solution.py:302
  (13 shorter events, 0.1 us)
Async XLA Ops:
  0.0 15.3 %collective-permute-start.1 = (bf16[24,2048]{1,0:T(8,128)(2,1)}, bf16[24,2048]{1,0:T(8,128)(2,1)S(1)}, u32[]{:S(2)}, u32[]{:S(2)}) collective-permute-start(bf16[24,2048]{1,0:T(8,128)(2,1)} %refs_0_.1), channel_id=1, source_target_pairs={{0,2},{1,3},{2,0},{3,1},{4,6},{5,7},{6,4},{7,5},{8,10},{9,11},{10,... | collective-permute-start | bytes 294920 | tf_op jit(solution)/shard_map/ppermute | solution.py:251
  2.6 12.7 %collective-permute-start = (bf16[24,2048]{1,0:T(8,128)(2,1)}, bf16[24,2048]{1,0:T(8,128)(2,1)S(1)}, u32[]{:S(2)}, u32[]{:S(2)}) collective-permute-start(bf16[24,2048]{1,0:T(8,128)(2,1)} %refs_0_.1), channel_id=1, source_target_pairs={{0,1},{1,0},{2,3},{3,2},{4,5},{5,4},{6,7},{7,6},{8,9},{9,8},{10,11... | collective-permute-start | bytes 294920 | tf_op jit(solution)/shard_map/ppermute | solution.py:251
  4.2 11.1 %collective-permute-start.2 = (bf16[24,2048]{1,0:T(8,128)(2,1)}, bf16[24,2048]{1,0:T(8,128)(2,1)S(1)}, u32[]{:S(2)}, u32[]{:S(2)}) collective-permute-start(bf16[24,2048]{1,0:T(8,128)(2,1)} %refs_0_.1), channel_id=1, source_target_pairs={{0,3},{1,2},{2,1},{3,0},{4,7},{5,6},{6,5},{7,4},{8,11},{9,10},{10,... | collective-permute-start | bytes 294920 | tf_op jit(solution)/shard_map/ppermute | solution.py:251
  4.4 0.7 %copy-start.11 = (f32[80]{0:T(128)S(1)}, f32[80]{0:T(128)}, u32[]{:S(2)}) copy-start(f32[80]{0:T(128)} %param.21) | copy-start | bytes 964
  4.4 0.7 %copy-start.12 = (s32[2,1]{0,1:T(1,128)S(1)}, s32[2,1]{0,1:T(1,128)}, u32[]{:S(2)}) copy-start(s32[2,1]{0,1:T(1,128)} %param.16) | copy-start | bytes 28
  4.4 1.3 %copy-start.9 = (f32[96]{0:T(128)S(1)}, f32[96]{0:T(128)}, u32[]{:S(2)}) copy-start(f32[96]{0:T(128)} %param.25) | copy-start | bytes 1156
  4.4 1.5 %copy-start.8 = (bf16[80,6]{0,1:T(8,128)(2,1)S(1)}, bf16[80,6]{0,1:T(8,128)(2,1)}, u32[]{:S(2)}) copy-start(bf16[80,6]{0,1:T(8,128)(2,1)} %param.19) | copy-start | bytes 2884
  4.5 1.5 %copy-start.7 = (s32[2,1024]{1,0:T(2,128)S(1)}, s32[2,1024]{1,0:T(2,128)}, u32[]{:S(2)}) copy-start(s32[2,1024]{1,0:T(2,128)} %param.15) | copy-start | bytes 24580
  5.1 1.5 %copy-start.4 = (bf16[80,80]{1,0:T(8,128)(2,1)S(1)}, bf16[80,80]{1,0:T(8,128)(2,1)}, u32[]{:S(2)}) copy-start(bf16[80,80]{1,0:T(8,128)(2,1)} %param.22) | copy-start | bytes 38404
  6.6 0.7 %copy-start.5 = (bf16[80,96]{1,0:T(8,128)(2,1)S(1)}, bf16[80,96]{1,0:T(8,128)(2,1)}, u32[]{:S(2)}) copy-start(bf16[80,96]{1,0:T(8,128)(2,1)} %param.20) | copy-start | bytes 46084
  8.0 0.7 %copy-start.6 = (bf16[96,80]{0,1:T(8,128)(2,1)S(1)}, bf16[96,80]{0,1:T(8,128)(2,1)}, u32[]{:S(2)}) copy-start(bf16[96,80]{0,1:T(8,128)(2,1)} %param.24) | copy-start | bytes 46084
  9.7 0.7 %copy-start.10 = (f32[80]{0:T(128)S(1)}, f32[80]{0:T(128)}, u32[]{:S(2)}) copy-start(f32[80]{0:T(128)} %param.23) | copy-start | bytes 964
  15.3 0.6 %copy-start.1 = (bf16[24,2048]{1,0:T(8,128)(2,1)}, bf16[24,2048]{1,0:T(8,128)(2,1)S(1)}, u32[]{:S(2)}) copy-start(bf16[24,2048]{1,0:T(8,128)(2,1)S(1)} %collective-permute-done.1.refs_2_) | copy-start | bytes 294916
  15.3 0.7 %copy-start.2 = (bf16[24,2048]{1,0:T(8,128)(2,1)}, bf16[24,2048]{1,0:T(8,128)(2,1)S(1)}, u32[]{:S(2)}) copy-start(bf16[24,2048]{1,0:T(8,128)(2,1)S(1)} %collective-permute-done.refs_1_) | copy-start | bytes 294916
  15.3 0.7 %copy-start.3 = (bf16[24,2048]{1,0:T(8,128)(2,1)}, bf16[24,2048]{1,0:T(8,128)(2,1)S(1)}, u32[]{:S(2)}) copy-start(bf16[24,2048]{1,0:T(8,128)(2,1)S(1)} %collective-permute-done.2.refs_3_) | copy-start | bytes 294916
  19.8 8.8 %collective-permute-start.3 = (bf16[1024,128]{1,0:T(8,128)(2,1)}, bf16[1024,128]{1,0:T(8,128)(2,1)S(1)}, u32[]{:S(2)}, u32[]{:S(2)}) collective-permute-start(bf16[1024,128]{1,0:T(8,128)(2,1)} %get-tuple-element.16), channel_id=1, source_target_pairs={{0,4},{2,6},{4,8},{5,1},{6,10},{7,3},{8,12},{9,5},{10,14},{11,7},{... | collective-permute-start | bytes 786440 | tf_op jit(solution)/shard_map/ppermute | solution.py:300
  28.6 0.7 %copy-start = (bf16[1024,128]{1,0:T(8,128)(2,1)}, bf16[1024,128]{1,0:T(8,128)(2,1)S(1)}, u32[]{:S(2)}) copy-start(bf16[1024,128]{1,0:T(8,128)(2,1)S(1)} %collective-permute-done.3.other_ref) | copy-start | bytes 786436
  41.7 3.9 %collective-permute-start.4 = (f32[24,128]{1,0:T(8,128)}, f32[24,128]{1,0:T(8,128)S(1)}, u32[]{:S(2)}, u32[]{:S(2)}) collective-permute-start(f32[24,128]{1,0:T(8,128)} %get-tuple-element.18), channel_id=1, source_target_pairs={{0,1},{1,0},{2,3},{3,2},{4,5},{5,4},{6,7},{7,6},{8,9},{9,8},{10,11... | collective-permute-start | bytes 36872 | tf_op jit(solution)/shard_map/ppermute | solution.py:302

commit v3 on v2

--- a/solution.py
+++ b/solution.py
@@ -62,6 +62,7 @@
         ),
         in_specs=[VMEM, SMEM, SMEM],
         out_specs=(VMEM, SMEM, SMEM),
+        compiler_params=pltpu.CompilerParams(vmem_limit_bytes=2 << 20),
         name="plan_pairs",
     )(neighbours, neighbour_count, place)
 
@@ -114,6 +115,7 @@
             pltpu.VMEM((points, LANES), jnp.float32),
             pltpu.VMEM((send, LANES), jnp.float32),
         ],
+        compiler_params=pltpu.CompilerParams(vmem_limit_bytes=12 << 20),
         name="select_points",
     )(*blocks, coords, send_rows, send_count, place, *after)
 
@@ -212,6 +214,7 @@
             pltpu.VMEM((nodes + 8, LANES), jnp.float32),
             pltpu.VMEM((LANES, all_nodes), jnp.float32),
         ],
+        compiler_params=pltpu.CompilerParams(vmem_limit_bytes=16 << 20),
         name="encode",
     )(
         own, other, rows.reshape(-1), chunks, total, place, table_weight, hidden_weight, out_weight,

time: 47.4 us -> 40 us (0.84)
  local copies, waits for them, and re-layouts: 7.81 us -> 4.99 us
  Pallas kernels: 19.2 us -> 16.7 us
  other arithmetic: 2.68 us -> 0.82 us
    pallas_call x1, Pallas kernels: 3.85 us -> 2.61 us  [select_points(): pl.pallas_call(kernel, out_shape=(jax.ShapeDtypeStruct((points, LANES), j...]
    unnamed x32, local copies, waits for them, and re-layouts: 5.66 us -> 4.65 us
    pallas_call x1, Pallas kernels: 12.4 us -> 11.5 us  [encode(): pl.pallas_call(kernel, out_shape=(piece, piece), in_specs=[VMEM, VMEM] +...]
    add x1, other arithmetic: 1.31 us -> 0.6 us  [shards(): keep + lax.ppermute(give, 'chan', [(i, i ^ 1) for i in range(groups)])]
    concatenate x1, other arithmetic: 0.63 us -> 0.01 us  [shards(): jnp.concatenate([pre_weight, take.astype(jnp.bfloat16)], axis=1)]
    pad x1, local copies, waits for them, and re-layouts: 0.62 us -> 0.01 us  [shards(): out_t = jnp.pad(pair_of(out_weight.T), ((0, LANES - hidden), (0, 0)))]
    pad x1, local copies, waits for them, and re-layouts: 0.63 us -> 0.02 us  [shards(): jnp.pad(hidden_weight.T, ((0, LANES - hidden), (0, LANES - hidden)))]
    concatenate x1, local copies, waits for them, and re-layouts: 0.61 us -> 0.02 us  [shards(): jnp.concatenate([jnp.pad(geom_weight[:, 0:3].astype(jnp.float32).T, ((0,...]
  transfers between devices with their start and end apart: 5 -> 5, of which waited for: 2 -> 2; matrix products, arithmetic and copies ran while one was open for 11% -> 3% of each run, Pallas kernels for 6% -> 7%
where the time goes in v3:
time: 40 us; the launch traced here: 39.6 us
  Pallas kernels  16.7 us (42%)
  waiting for transfers between devices  10.4 us (26%)
  starting transfers between devices  6.38 us (16%)
  local copies, waits for them, and re-layouts  4.99 us (12%)
  other arithmetic  0.82 us (2%)
    pallas_call x1, Pallas kernels, encode(): pl.pallas_call(kernel, out_shape=(piece, piece), in_specs=[VMEM, VMEM] +...  11.5 us
    ppermute x1, waiting for transfers between devices, shards(): other = lax.ppermute(sent, ('slab', 'chan'), moves)  6.66 us
    unnamed x32, local copies, waits for them, and re-layouts  4.65 us
    ppermute x3, starting transfers between devices, shards(): lax.ppermute(features, 'chan', [(i, i ^ step) for i in range(groups)])  4.39 us
    ppermute x1, waiting for transfers between devices, shards(): lax.ppermute(give, 'chan', [(i, i ^ 1) for i in range(groups)])  3.68 us
    pallas_call x1, Pallas kernels, plan_pairs(): pl.pallas_call(kernel, out_shape=(jax.ShapeDtypeStruct((nodes + 8, slots)...  2.66 us
    pallas_call x1, Pallas kernels, select_points(): pl.pallas_call(kernel, out_shape=(jax.ShapeDtypeStruct((points, LANES), j...  2.61 us
    ppermute x1, starting transfers between devices, shards(): other = lax.ppermute(sent, ('slab', 'chan'), moves)  1.92 us
  transfers between devices with their start and end apart: 5, of which 2 were waited for; matrix products, arithmetic and copies ran while one was open for 3% of the time, Pallas kernels for 7%

profile of v3, /device:TPU:4, one launch (start us, length us, event | category | flops | bytes accessed | tf_op | source)
XLA Modules:
  0.0 39.6 jit_solution(15638872396408836109)
XLA Ops:
  0.0 2.6 %collective-permute-start.1 = (bf16[24,2048]{1,0:T(8,128)(2,1)}, bf16[24,2048]{1,0:T(8,128)(2,1)S(1)}, u32[]{:S(2)}, u32[]{:S(2)}) collective-permute-start(bf16[24,2048]{1,0:T(8,128)(2,1)} %refs_0_.1), channel_id=1, source_target_pairs={{0,2},{1,3},{2,0},{3,1},{4,6},{5,7},{6,4},{7,5},{8,10},{9,11},{10,... | collective-permute-start | bytes 294920 | tf_op jit(solution)/shard_map/ppermute | solution.py:254
  2.6 1.6 %collective-permute-start = (bf16[24,2048]{1,0:T(8,128)(2,1)}, bf16[24,2048]{1,0:T(8,128)(2,1)S(1)}, u32[]{:S(2)}, u32[]{:S(2)}) collective-permute-start(bf16[24,2048]{1,0:T(8,128)(2,1)} %refs_0_.1), channel_id=1, source_target_pairs={{0,1},{1,0},{2,3},{3,2},{4,5},{5,4},{6,7},{7,6},{8,9},{9,8},{10,11... | collective-permute-start | bytes 294920 | tf_op jit(solution)/shard_map/ppermute | solution.py:254
  4.2 0.2 collective-permute-start.2
  4.4 0.0 copy-start.11
  4.4 0.0 copy-start.12
  4.4 0.0 copy-start.9
  4.4 0.0 copy-start.8
  4.5 0.0 copy-start.7
  4.5 0.6 %copy-done.11 = f32[80]{0:T(128)S(1)} copy-done((f32[80]{0:T(128)S(1)}, f32[80]{0:T(128)}, u32[]{:S(2)}) %copy-start.11) | copy-done | bytes 344
  5.1 0.0 copy-start.4
  5.1 0.0 copy-done.12
  5.1 0.1 copy.21.refs_6_
  5.2 0.0 copy-done.9
  5.2 0.1 reshape.51
  5.3 0.1 reshape.52
  5.4 0.0 copy-done.8
  5.4 0.0 copy-done.7
  5.4 0.4 %copy-done.4 = bf16[80,80]{1,0:T(8,128)(2,1)S(1)} copy-done((bf16[80,80]{1,0:T(8,128)(2,1)S(1)}, bf16[80,80]{1,0:T(8,128)(2,1)}, u32[]{:S(2)}) %copy-start.4) | copy-done | bytes 12824
  5.8 0.0 copy-start.5
  5.8 0.1 copy.18
  5.9 0.6 %copy-done.5 = bf16[80,96]{1,0:T(8,128)(2,1)S(1)} copy-done((bf16[80,96]{1,0:T(8,128)(2,1)S(1)}, bf16[80,96]{1,0:T(8,128)(2,1)}, u32[]{:S(2)}) %copy-start.5) | copy-done | bytes 15384
  6.5 0.1 copy.17
  6.6 0.0 copy-start.6
  6.7 0.7 %copy-done.6 = bf16[96,80]{0,1:T(8,128)(2,1)S(1)} copy-done((bf16[96,80]{0,1:T(8,128)(2,1)S(1)}, bf16[96,80]{0,1:T(8,128)(2,1)}, u32[]{:S(2)}) %copy-start.6) | copy-done | bytes 15384
  7.4 0.1 copy.19
  7.5 0.1 dynamic_slice.7
  7.6 0.0 copy-start.10
  7.6 0.1 copy.22
  7.7 0.0 copy-start.1
  7.7 0.5 %copy-done.10 = f32[80]{0:T(128)S(1)} copy-done((f32[80]{0:T(128)S(1)}, f32[80]{0:T(128)}, u32[]{:S(2)}) %copy-start.10) | copy-done | bytes 344
  8.3 0.0 copy-start.3
  8.3 0.1 pad_add_fusion.place_ref.refs_7_
  8.4 0.2 copy-done.1
  8.5 0.4 copy-done.3
  8.9 2.7 %plan_pairs.1 = (s32[72,128]{1,0:T(8,128)S(1)}, s32[576]{0:T(1024)S(1)}, s32[1]{0:T(128)}) custom-call(s32[128,128]{1,0:T(8,128)S(1)} %copy-done.1, s32[128]{0:T(128)S(1)} %copy-done.3, s32[4]{0:T(128)S(1)} %pad_add_fusion.place_ref.refs_7_), custom_call_target="tpu_custom_call" | custom-call | tf_op jit(solution)/shard_map/plan_pairs/pallas_call | solution.py:56
  11.6 0.0 copy-start
  11.6 0.1 fusion.4
  11.7 0.0 copy-start.2
  11.8 0.0 collective-permute-done.1.refs_2_
  11.8 0.0 collective-permute-done.refs_1_
  11.8 0.0 collective-permute-done.2.refs_3_
  11.8 0.7 %copy-done = bf16[24,2048]{1,0:T(8,128)(2,1)S(1)} copy-done((bf16[24,2048]{1,0:T(8,128)(2,1)S(1)}, bf16[24,2048]{1,0:T(8,128)(2,1)}, u32[]{:S(2)}) %copy-start) | copy-done | bytes 98328
  12.5 0.0 copy-done.2
  12.5 2.6 %select_points.1 = (bf16[2048,128]{1,0:T(8,128)(2,1)S(1)}, bf16[1024,128]{1,0:T(8,128)(2,1)S(1)}) custom-call(bf16[24,2048]{1,0:T(8,128)(2,1)S(1)} %copy-done, bf16[24,2048]{1,0:T(8,128)(2,1)S(1)} %collective-permute-done.refs_1_, bf16[24,2048]{1,0:T(8,128)(2,1)S(1)} %collective-permute-done.1.refs_2_, bf16[24,2048]{1,0:T(8,128)(2,1)S(1)} %collective-permute-done.2.refs_3_, ...), custom_call_target="tpu_custom_call" | custom-call | tf_op jit(solution)/shard_map/select_points/pallas_call | solution.py:105
  15.1 1.9 %collective-permute-start.3 = (bf16[1024,128]{1,0:T(8,128)(2,1)S(1)}, bf16[1024,128]{1,0:T(8,128)(2,1)S(1)}, u32[]{:S(2)}, u32[]{:S(2)}) collective-permute-start(bf16[1024,128]{1,0:T(8,128)(2,1)S(1)} %get-tuple-element.16), channel_id=1, source_target_pairs={{0,4},{2,6},{4,8},{5,1},{6,10},{7,3},{8,12},{9,5},{10,14},{11,7},{... | collective-permute-start | bytes 786440 | tf_op jit(solution)/shard_map/ppermute | solution.py:303
  17.0 6.7 %collective-permute-done.3.other_ref = bf16[1024,128]{1,0:T(8,128)(2,1)S(1)} collective-permute-done((bf16[1024,128]{1,0:T(8,128)(2,1)S(1)}, bf16[1024,128]{1,0:T(8,128)(2,1)S(1)}, u32[]{:S(2)}, u32[]{:S(2)}) %collective-permute-start.3) | collective-permute-done | bytes 262176 | tf_op jit(solution)/shard_map/ppermute | solution.py:303
  23.7 11.5 %encode.1 = (f32[24,128]{1,0:T(8,128)S(1)}, f32[24,128]{1,0:T(8,128)S(1)}) custom-call(bf16[2048,128]{1,0:T(8,128)(2,1)S(1)} %get-tuple-element.15.own_ref, bf16[1024,128]{1,0:T(8,128)(2,1)S(1)} %collective-permute-done.3.other_ref, s32[9216]{0:T(1024)S(1)} %bitcast.26, s32[576]{0:T(1024)S(1)} %get-tuple-element.13.refs_9_.list_ref, ...), custom_call_target="tpu_custom_call" | custom-call | tf_op jit(solution)/shard_map/encode/pallas_call | solution.py:205
  35.2 0.1 collective-permute-start.4
  35.3 3.7 %collective-permute-done.4 = f32[24,128]{1,0:T(8,128)S(1)} collective-permute-done((f32[24,128]{1,0:T(8,128)S(1)}, f32[24,128]{1,0:T(8,128)S(1)}, u32[]{:S(2)}, u32[]{:S(2)}) %collective-permute-start.4) | collective-permute-done | bytes 12320 | tf_op jit(solution)/shard_map/ppermute | solution.py:305
  39.0 0.6 %add.67 = f32[24,128]{1,0:T(8,128)} add(f32[24,128]{1,0:T(8,128)S(1)} %get-tuple-element.17, f32[24,128]{1,0:T(8,128)S(1)} %collective-permute-done.4) | non-fusion elementwise | flops 3072 | bytes 36864 | tf_op jit(solution)/shard_map/add | solution.py:305
  (18 shorter events, 0.1 us)
Async XLA Ops:
  0.0 11.8 %collective-permute-start.1 = (bf16[24,2048]{1,0:T(8,128)(2,1)}, bf16[24,2048]{1,0:T(8,128)(2,1)S(1)}, u32[]{:S(2)}, u32[]{:S(2)}) collective-permute-start(bf16[24,2048]{1,0:T(8,128)(2,1)} %refs_0_.1), channel_id=1, source_target_pairs={{0,2},{1,3},{2,0},{3,1},{4,6},{5,7},{6,4},{7,5},{8,10},{9,11},{10,... | collective-permute-start | bytes 294920 | tf_op jit(solution)/shard_map/ppermute | solution.py:254
  2.6 9.2 %collective-permute-start = (bf16[24,2048]{1,0:T(8,128)(2,1)}, bf16[24,2048]{1,0:T(8,128)(2,1)S(1)}, u32[]{:S(2)}, u32[]{:S(2)}) collective-permute-start(bf16[24,2048]{1,0:T(8,128)(2,1)} %refs_0_.1), channel_id=1, source_target_pairs={{0,1},{1,0},{2,3},{3,2},{4,5},{5,4},{6,7},{7,6},{8,9},{9,8},{10,11... | collective-permute-start | bytes 294920 | tf_op jit(solution)/shard_map/ppermute | solution.py:254
  4.2 7.6 %collective-permute-start.2 = (bf16[24,2048]{1,0:T(8,128)(2,1)}, bf16[24,2048]{1,0:T(8,128)(2,1)S(1)}, u32[]{:S(2)}, u32[]{:S(2)}) collective-permute-start(bf16[24,2048]{1,0:T(8,128)(2,1)} %refs_0_.1), channel_id=1, source_target_pairs={{0,3},{1,2},{2,1},{3,0},{4,7},{5,6},{6,5},{7,4},{8,11},{9,10},{10,... | collective-permute-start | bytes 294920 | tf_op jit(solution)/shard_map/ppermute | solution.py:254
  4.4 0.7 %copy-start.11 = (f32[80]{0:T(128)S(1)}, f32[80]{0:T(128)}, u32[]{:S(2)}) copy-start(f32[80]{0:T(128)} %param.21) | copy-start | bytes 964
  4.4 0.7 %copy-start.12 = (s32[2,1]{0,1:T(1,128)S(1)}, s32[2,1]{0,1:T(1,128)}, u32[]{:S(2)}) copy-start(s32[2,1]{0,1:T(1,128)} %param.16) | copy-start | bytes 28
  4.4 0.7 %copy-start.9 = (f32[96]{0:T(128)S(1)}, f32[96]{0:T(128)}, u32[]{:S(2)}) copy-start(f32[96]{0:T(128)} %param.25) | copy-start | bytes 1156
  4.4 0.9 %copy-start.8 = (bf16[80,6]{0,1:T(8,128)(2,1)S(1)}, bf16[80,6]{0,1:T(8,128)(2,1)}, u32[]{:S(2)}) copy-start(bf16[80,6]{0,1:T(8,128)(2,1)} %param.19) | copy-start | bytes 2884
  4.5 0.9 %copy-start.7 = (s32[2,1024]{1,0:T(2,128)S(1)}, s32[2,1024]{1,0:T(2,128)}, u32[]{:S(2)}) copy-start(s32[2,1024]{1,0:T(2,128)} %param.15) | copy-start | bytes 24580
  5.1 0.7 %copy-start.4 = (bf16[80,80]{1,0:T(8,128)(2,1)S(1)}, bf16[80,80]{1,0:T(8,128)(2,1)}, u32[]{:S(2)}) copy-start(bf16[80,80]{1,0:T(8,128)(2,1)} %param.22) | copy-start | bytes 38404
  5.8 0.7 %copy-start.5 = (bf16[80,96]{1,0:T(8,128)(2,1)S(1)}, bf16[80,96]{1,0:T(8,128)(2,1)}, u32[]{:S(2)}) copy-start(bf16[80,96]{1,0:T(8,128)(2,1)} %param.20) | copy-start | bytes 46084
  6.6 0.7 %copy-start.6 = (bf16[96,80]{0,1:T(8,128)(2,1)S(1)}, bf16[96,80]{0,1:T(8,128)(2,1)}, u32[]{:S(2)}) copy-start(bf16[96,80]{0,1:T(8,128)(2,1)} %param.24) | copy-start | bytes 46084
  7.6 0.7 %copy-start.10 = (f32[80]{0:T(128)S(1)}, f32[80]{0:T(128)}, u32[]{:S(2)}) copy-start(f32[80]{0:T(128)} %param.23) | copy-start | bytes 964
  7.7 0.9 %copy-start.1 = (s32[128,128]{1,0:T(8,128)S(1)}, s32[128,128]{1,0:T(8,128)}, u32[]{:S(2)}) copy-start(s32[128,128]{1,0:T(8,128)} %nbr_ref.1) | copy-start | bytes 196612
  8.3 0.7 %copy-start.3 = (s32[128]{0:T(128)S(1)}, s32[128]{0:T(128)}, u32[]{:S(2)}) copy-start(s32[128]{0:T(128)} %count_ref.1) | copy-start | bytes 1540
  11.6 0.9 %copy-start = (bf16[24,2048]{1,0:T(8,128)(2,1)S(1)}, bf16[24,2048]{1,0:T(8,128)(2,1)}, u32[]{:S(2)}) copy-start(bf16[24,2048]{1,0:T(8,128)(2,1)} %refs_0_.1) | copy-start | bytes 294916
  11.7 0.8 %copy-start.2 = (bf16[3,2048]{1,0:T(4,128)(2,1)S(1)}, bf16[3,2048]{1,0:T(4,128)(2,1)}, u32[]{:S(2)}) copy-start(bf16[3,2048]{1,0:T(4,128)(2,1)} %refs_4_.1) | copy-start | bytes 36868
  15.1 8.6 %collective-permute-start.3 = (bf16[1024,128]{1,0:T(8,128)(2,1)S(1)}, bf16[1024,128]{1,0:T(8,128)(2,1)S(1)}, u32[]{:S(2)}, u32[]{:S(2)}) collective-permute-start(bf16[1024,128]{1,0:T(8,128)(2,1)S(1)} %get-tuple-element.16), channel_id=1, source_target_pairs={{0,4},{2,6},{4,8},{5,1},{6,10},{7,3},{8,12},{9,5},{10,14},{11,7},{... | collective-permute-start | bytes 786440 | tf_op jit(solution)/shard_map/ppermute | solution.py:303
  35.2 3.8 %collective-permute-start.4 = (f32[24,128]{1,0:T(8,128)S(1)}, f32[24,128]{1,0:T(8,128)S(1)}, u32[]{:S(2)}, u32[]{:S(2)}) collective-permute-start(f32[24,128]{1,0:T(8,128)S(1)} %get-tuple-element.18), channel_id=1, source_target_pairs={{0,1},{1,0},{2,3},{3,2},{4,5},{5,4},{6,7},{7,6},{8,9},{9,8},{10,11... | collective-permute-start | bytes 36872 | tf_op jit(solution)/shard_map/ppermute | solution.py:305

commit v4 on v3

v4 whole, which is shorter than its diff:
```python
import jax
import jax.numpy as jnp
from jax import lax
from jax.experimental import pallas as pl
from jax.experimental.pallas import tpu as pltpu
from jax.sharding import PartitionSpec as P

ZD = 2
GX = 16
GY = 4
LANES = 128
CHUNK = 16
BLOCK = 64
CONSTANT = 16.0
GELU_ONE = 0.7978845608028654
GELU_CUBE = 0.044715 * GELU_ONE

SMEM = pl.BlockSpec(memory_space=pltpu.SMEM)
VMEM = pl.BlockSpec(memory_space=pltpu.VMEM)
ANY = pl.BlockSpec(memory_space=pl.ANY)
HBM = pl.BlockSpec(memory_space=pltpu.MemorySpace.HBM)


def gelu_doubled(x):
    inner = x * (GELU_ONE + GELU_CUBE * (x * x))
    return x * (1.0 + jnp.tanh(inner))


def prepare(
    neighbours, neighbour_count, geom_weight, feat_weight, bias_one, hidden_weight, bias_two,
    out_weight, bias_three, place, groups, points, send, depth,
):
    per_slab, slots = neighbours.shape
    hidden, channels = feat_weight.shape
    chans = channels // groups
    width = LANES // groups
    nodes = per_slab // ZD
    per_node = slots // CHUNK
    most = nodes * per_node
    nothing = 2 * (points + send)
    extra = slice(hidden, hidden + 3)

    def parts(value):
        high = value.astype(jnp.bfloat16).astype(jnp.float32)
        mid = (value - high).astype(jnp.bfloat16).astype(jnp.float32)
        low = (value - high - mid).astype(jnp.bfloat16).astype(jnp.float32)
        return jnp.concatenate([high, mid, low], axis=0) * (1.0 / CONSTANT)

    given = (
        neighbour_count, neighbours, geom_weight.T, feat_weight, bias_one[None], hidden_weight,
        bias_two[None], out_weight.T, bias_three[None],
    )

    def kernel(*refs):
        place_ref = refs[len(given)]
        rows_ref, list_ref, total_ref, table_w, hidden_w, out_w, node_pre = refs[len(given) + 1 :][:7]
        held = refs[len(given) + 8 :][: len(given)]
        wide, square, spread, arrived = refs[2 * len(given) + 8 :]
        copies = [
            pltpu.make_async_copy(source, target, arrived.at[at])
            for at, (source, target) in enumerate(zip(refs, held))
        ]
        for copy in copies:
            copy.start()
        for copy in copies:
            copy.wait()
        count_ref, nbr_ref, geom_ref, feat_ref, one_ref, hidden_ref, two_ref, out_ref, three_ref = held
        member = place_ref[0]
        first_id = place_ref[2]
        start = place_ref[3]
        lane = lax.broadcasted_iota(jnp.int32, (1, LANES), 1)

        def one_node(node, at):
            count = count_ref[start + node]
            row = nbr_ref[pl.ds(start + node, 1), :]
            row = jnp.where(row >= points + send, row - send, row)
            slot = lax.broadcasted_iota(jnp.int32, (1, slots), 1)
            rows_ref[pl.ds(node, 1), :] = jnp.where(slot < count, 2 * row, nothing)
            for piece in range(per_node):
                list_ref[at + piece] = node * per_node + piece
            return at + (count + CHUNK - 1) // CHUNK

        used = lax.fori_loop(0, nodes, one_node, 0)
        rows_ref[pl.ds(nodes, 8), :] = jnp.full((8, slots), nothing, jnp.int32)
        total_ref[0] = (used + BLOCK - 1) // BLOCK

        def fill(step, carry):
            list_ref[used + step] = most
            return carry

        lax.fori_loop(0, BLOCK, fill, 0)

        square[...] = jnp.zeros((LANES, LANES), jnp.float32)
        square[0:hidden, 0:channels] = feat_ref[...].astype(jnp.float32)
        square[...] = square[...].T
        wide[...] = jnp.zeros((LANES, 2 * LANES), jnp.float32)
        for block in range(groups):
            wide[block * width : block * width + chans, 0:LANES] = square[
                block * chans : (block + 1) * chans, :
            ]
        geom = geom_ref[...].astype(jnp.float32)
        wide[chans : chans + 3, 0:hidden] = geom[3:6]
        row = lax.broadcasted_iota(jnp.int32, (LANES, LANES), 0)
        col = lax.broadcasted_iota(jnp.int32, (LANES, LANES), 1)
        pair = member // 2
        take = ((row == pair * 2 * width + col) & (col < 2 * width)) | (
            (row == chans + 3) & (col == LANES - 1)
        )
        wide[:, LANES:] = take.astype(jnp.float32)
        table_w[...] = wide[...].astype(jnp.bfloat16)

        square[...] = jnp.zeros((LANES, LANES), jnp.float32)
        square[0:hidden, 0:hidden] = 0.5 * hidden_ref[...].astype(jnp.float32)
        square[...] = square[...].T
        square[extra, 0:hidden] = parts(two_ref[...])
        ones = (lane >= hidden) & (lane < hidden + 3)
        square[hidden : hidden + 1, hidden:] = jnp.where(ones, 0.5, 0.0)[:, hidden:]
        hidden_w[...] = square[...].astype(jnp.bfloat16)

        square[...] = jnp.zeros((LANES, LANES), jnp.float32)
        square[0:hidden, 0:channels] = 0.5 * out_ref[...].astype(jnp.float32)
        square[extra, 0:channels] = parts(three_ref[...])
        square[...] = square[...].T
        spread[...] = jnp.zeros((LANES, LANES), jnp.float32)
        for half in range(2):
            spread[half * width : half * width + chans, :] = square[
                pl.ds((2 * pair + half) * chans, chans), :
            ]
        spread[LANES - 1 :, :] = jnp.where(lane == hidden, 1.0 / CONSTANT, 0.0)
        out_w[...] = spread[...].T.astype(jnp.bfloat16)

        ids = first_id + lax.broadcasted_iota(jnp.int32, (nodes + 8, 1), 0)
        along_x = ((ids % GX).astype(jnp.float32) + 0.5) / GX
        along_y = ((ids // GX % GY).astype(jnp.float32) + 0.5) / GY
        along_z = ((ids // (GX * GY)).astype(jnp.float32) + 0.5) / depth
        term = geom[0:1] * along_x + geom[1:2] * along_y + geom[2:3] * along_z + one_ref[...]
        node_pre[...] = jnp.broadcast_to(jnp.where(ones, 0.5 * CONSTANT, 0.0), (nodes + 8, LANES))
        node_pre[:, 0:hidden] = term

    out = pl.pallas_call(
        kernel,
        out_shape=(
            jax.ShapeDtypeStruct((nodes + 8, slots), jnp.int32),
            jax.ShapeDtypeStruct((most + BLOCK,), jnp.int32),
            jax.ShapeDtypeStruct((1,), jnp.int32),
            jax.ShapeDtypeStruct((LANES, 2 * LANES), jnp.bfloat16),
            jax.ShapeDtypeStruct((LANES, LANES), jnp.bfloat16),
            jax.ShapeDtypeStruct((LANES, LANES), jnp.bfloat16),
            jax.ShapeDtypeStruct((nodes + 8, LANES), jnp.float32),
        ),
        in_specs=[HBM] * len(given) + [SMEM],
        out_specs=(VMEM, SMEM, SMEM) + (VMEM,) * 4,
        scratch_shapes=[pltpu.SMEM(neighbour_count.shape, jnp.int32)]
        + [pltpu.VMEM(array.shape, array.dtype) for array in given[1:]]
        + [
            pltpu.VMEM((LANES, 2 * LANES), jnp.float32),
            pltpu.VMEM((LANES, LANES), jnp.float32),
            pltpu.VMEM((LANES, LANES), jnp.float32),
            pltpu.SemaphoreType.DMA((len(given),)),
        ],
        name="prepare",
    )(*given, place)
    return out[:3], out[3:]


def select_points(blocks, coords, send_rows, send_count, place, after):
    groups = len(blocks)
    chans, points = blocks[0].shape
    width = LANES // groups
    send = send_rows.shape[0] // 2
    unroll = 32

    def kernel(*refs):
        block_refs = refs[:groups]
        coords_ref, rows_ref, count_ref, place_ref = refs[groups : groups + 4]
        own_ref, sent_ref, stack, table, picked = refs[groups + 4 + len(after) :]
        member = place_ref[0]
        side = place_ref[1]
        for step in range(groups):
            base = pl.multiple_of((member ^ step) * width, width)
            empty = jnp.zeros((width - chans, points), jnp.bfloat16)
            stack[pl.ds(base, width), :] = jnp.concatenate([block_refs[step][...], empty], axis=0)
        stack[chans : chans + 3, :] = coords_ref[...]
        stack[chans + 3 : chans + 4, :] = jnp.ones((1, points), jnp.bfloat16)
        own = stack[...].T
        own_ref[...] = own
        table[...] = own.astype(jnp.float32)

        def gather(step, carry):
            base = step * unroll
            names = rows_ref.at[pl.ds(side * send + base, unroll)]
            rows = [table[pl.ds(names[j], 1), :] for j in range(unroll)]
            for j in range(unroll):
                picked[pl.ds(base + j, 1), :] = rows[j]
            return carry

        lax.fori_loop(0, send // unroll, gather, 0)
        slot = lax.broadcasted_iota(jnp.int32, (send, LANES), 0)
        sent_ref[...] = jnp.where(slot < count_ref[side, 0], picked[...], 0.0).astype(jnp.bfloat16)

    return pl.pallas_call(
        kernel,
        out_shape=(
            jax.ShapeDtypeStruct((points, LANES), jnp.bfloat16),
            jax.ShapeDtypeStruct((send, LANES), jnp.bfloat16),
        ),
        in_specs=[VMEM] * (groups + 1) + [SMEM] * 3 + [ANY] * len(after),
        out_specs=(VMEM, VMEM),
        scratch_shapes=[
            pltpu.VMEM((LANES, points), jnp.bfloat16),
            pltpu.VMEM((points, LANES), jnp.float32),
            pltpu.VMEM((send, LANES), jnp.float32),
        ],
        compiler_params=pltpu.CompilerParams(vmem_limit_bytes=12 << 20),
        name="select_points",
    )(*blocks, coords, send_rows, send_count, place, *after)


def encode(own, other, plan, place, weights, chans, width):
    rows, chunks, total = plan
    table_weight, hidden_weight, out_weight, node_part = weights
    points = own.shape[0]
    send = other.shape[0]
    nodes = rows.shape[0] - 8
    slots = rows.shape[1]
    shift = (slots // CHUNK).bit_length() - 1
    total_rows = points + send
    pairs = BLOCK * CHUNK

    def kernel(
        own_ref, other_ref, rows_ref, list_ref, total_ref, place_ref, table_w, hidden_w, out_w,
        node_pre, keep_ref, give_ref, table, picked, acc, turned,
    ):
        parity = place_ref[1]

        def fill(source, start, count):
            step = 256
            for at in range(0, count, step):
                both = jnp.dot(source[pl.ds(at, step), :], table_w[...], preferred_element_type=jnp.float32)
                pre = both[:, :LANES].astype(jnp.bfloat16).astype(jnp.float32)
                table[pl.ds(2 * (start + at), step, stride=2), :] = pre
                table[pl.ds(2 * (start + at) + 1, step, stride=2), :] = both[:, LANES:]

        fill(own_ref, 0, points)
        fill(other_ref, points, send)
        table[pl.ds(2 * total_rows, 8), :] = jnp.zeros((8, LANES), jnp.float32)
        acc[...] = jnp.zeros((nodes + 8, 8, LANES), jnp.float32)

        def one_block(index, carry):
            ids = list_ref.at[pl.ds(index * BLOCK, BLOCK)]
            names = [ids[piece] for piece in range(BLOCK)]
            for piece in range(BLOCK):
                where = rows_ref.at[pl.ds(names[piece] * CHUNK, CHUNK)]
                got = [table[pl.ds(where[j], 2), :] for j in range(CHUNK)]
                for j in range(CHUNK):
                    picked[pl.ds(2 * (piece * CHUNK + j), 2), :] = got[j]
            step = 8
            for group in range(BLOCK // step):
                base = group * step * CHUNK
                spots = [names[group * step + i] >> shift for i in range(step)]
                offset = jnp.concatenate(
                    [jnp.broadcast_to(node_pre[pl.ds(spot, 1), :], (CHUNK, LANES)) for spot in spots],
                    axis=0,
                )
                pre = picked[pl.ds(2 * base, step * CHUNK, stride=2), :]
                val = picked[pl.ds(2 * base + 1, step * CHUNK, stride=2), :]
                first = gelu_doubled(pre + offset).astype(jnp.bfloat16)
                second = jnp.dot(first, hidden_w[...], preferred_element_type=jnp.float32)
                second = gelu_doubled(second).astype(jnp.bfloat16)
                kappa = jnp.dot(second, out_w[...], preferred_element_type=jnp.float32)
                product = kappa * val
                for i, spot in enumerate(spots):
                    low = product[i * CHUNK : i * CHUNK + 8]
                    for j in range(8, CHUNK, 8):
                        low = low + product[i * CHUNK + j : i * CHUNK + j + 8]
                    acc[spot] = acc[spot] + low
            return carry

        lax.fori_loop(0, total_ref[0], one_block, 0)
        sums = jnp.sum(acc[0:nodes], axis=1)
        means = (sums / sums[:, LANES - 1 :]).T
        low = jnp.where(parity == 1, means, 0.0)
        turned[...] = jnp.concatenate([low, means - low], axis=1)
        mine = pl.multiple_of((1 - parity) * width, width)
        theirs = pl.multiple_of(parity * width, width)
        keep_ref[...] = turned[pl.ds(mine, chans), :]
        give_ref[...] = turned[pl.ds(theirs, chans), :]

    piece = jax.ShapeDtypeStruct((chans, ZD * nodes), jnp.float32)
    return pl.pallas_call(
        kernel,
        out_shape=(piece, piece),
        in_specs=[VMEM, VMEM] + [SMEM] * 4 + [VMEM] * 4,
        out_specs=(VMEM, VMEM),
        scratch_shapes=[
            pltpu.VMEM((2 * total_rows + 8, LANES), jnp.float32),
            pltpu.VMEM((2 * pairs, LANES), jnp.float32),
            pltpu.VMEM((nodes + 8, 8, LANES), jnp.float32),
            pltpu.VMEM((LANES, ZD * nodes), jnp.float32),
        ],
        compiler_params=pltpu.CompilerParams(vmem_limit_bytes=16 << 20),
        name="encode",
    )(
        own, other, rows.reshape(-1), chunks, total, place, table_weight, hidden_weight, out_weight,
        node_part,
    )


def shards(
    features,
    coords,
    send_rows,
    send_count,
    neighbours,
    neighbour_count,
    geom_weight,
    feat_weight,
    bias_one,
    hidden_weight,
    bias_two,
    out_weight,
    bias_three,
):
    groups = lax.axis_size("chan")
    slabs = lax.axis_size("slab")
    member = lax.axis_index("chan")
    slab_id = lax.axis_index("slab")
    chans, points = features.shape
    send = send_rows.shape[1]
    per_slab = neighbours.shape[0]
    nodes = per_slab // ZD
    width = LANES // groups

    blocks = [features]
    for step in range(1, groups):
        blocks.append(lax.ppermute(features, "chan", [(i, i ^ step) for i in range(groups)]))

    plane = member % 2
    start = plane * nodes
    upper = 1 - plane
    place = jnp.stack([member, upper, slab_id * per_slab + start, start]).astype(jnp.int32)
    plan, weights = prepare(
        neighbours, neighbour_count, geom_weight, feat_weight, bias_one, hidden_weight, bias_two,
        out_weight, bias_three, place, groups, points, send, ZD * slabs,
    )
    own, sent = select_points(
        blocks, coords, send_rows.reshape(-1), send_count, place, plan + weights
    )
    moves = []
    for slab in range(slabs):
        for who in range(groups):
            target = slab + 1 if who % 2 == 0 else slab - 1
            if 0 <= target < slabs:
                moves.append((slab * groups + who, target * groups + who))
    other = lax.ppermute(sent, ("slab", "chan"), moves)
    keep, give = encode(own, other, plan, place, weights, chans, width)
    return keep + lax.ppermute(give, "chan", [(i, i ^ 1) for i in range(groups)])


def solution(mesh):
    placed = (
        P("chan", "slab"),
        P(None, "slab"),
        P(None, "slab"),
        P(None, "slab"),
        P("slab", None),
        P("slab"),
        P(),
        P(),
        P(),
        P(),
        P(),
        P(),
        P(),
    )
    return jax.shard_map(
        shards, mesh=mesh, in_specs=placed, out_specs=P("chan", "slab"), check_vma=False
    )
```

time: 40 us -> 43.8 us (1.095)
  the two profiles are of different devices: /device:TPU:4 before, /device:TPU:20 now
where the time goes in v4:
time: 43.8 us; the launch traced here: 43.2 us
  Pallas kernels  17.7 us (40%)
  waiting for transfers between devices  13.2 us (30%)
  starting transfers between devices  5.48 us (13%)
  local copies, waits for them, and re-layouts  5.36 us (12%)
  other arithmetic  1.26 us (3%)
    pallas_call x1, Pallas kernels, encode(): pl.pallas_call(kernel, out_shape=(piece, piece), in_specs=[VMEM, VMEM] +...  11 us
    ppermute x1, waiting for transfers between devices, shards(): other = lax.ppermute(sent, ('slab', 'chan'), moves)  6.66 us
    unnamed x34, local copies, waits for them, and re-layouts  5.36 us
    pallas_call x1, Pallas kernels, prepare(): pl.pallas_call(kernel, out_shape=(jax.ShapeDtypeStruct((nodes + 8, slots)...  4.15 us
    ppermute x1, waiting for transfers between devices, shards(): lax.ppermute(give, 'chan', [(i, i ^ 1) for i in range(groups)])  3.68 us
    ppermute x3, starting transfers between devices, shards(): lax.ppermute(features, 'chan', [(i, i ^ step) for i in range(groups)])  3.49 us
    ppermute x3, waiting for transfers between devices, shards(): lax.ppermute(features, 'chan', [(i, i ^ step) for i in range(groups)])  2.88 us
    pallas_call x1, Pallas kernels, select_points(): pl.pallas_call(kernel, out_shape=(jax.ShapeDtypeStruct((points, LANES), j...  2.58 us
  transfers between devices with their start and end apart: 5, of which 3 were waited for; matrix products, arithmetic and copies ran while one was open for 2% of the time, Pallas kernels for 10%

profile of v4, /device:TPU:20, one launch (start us, length us, event | category | flops | bytes accessed | tf_op | source)
XLA Modules:
  0.0 43.2 jit_solution(1781180372327197988)
XLA Ops:
  0.0 0.3 collective-permute-start.1
  0.3 1.6 %collective-permute-start = (bf16[24,2048]{1,0:T(8,128)(2,1)}, bf16[24,2048]{1,0:T(8,128)(2,1)S(1)}, u32[]{:S(2)}, u32[]{:S(2)}) collective-permute-start(bf16[24,2048]{1,0:T(8,128)(2,1)} %refs_0_.3), channel_id=1, source_target_pairs={{0,1},{1,0},{2,3},{3,2},{4,5},{5,4},{6,7},{7,6},{8,9},{9,8},{10,11... | collective-permute-start | bytes 294920 | tf_op jit(solution)/shard_map/ppermute | solution.py:336
  1.9 1.6 %collective-permute-start.2 = (bf16[24,2048]{1,0:T(8,128)(2,1)}, bf16[24,2048]{1,0:T(8,128)(2,1)S(1)}, u32[]{:S(2)}, u32[]{:S(2)}) collective-permute-start(bf16[24,2048]{1,0:T(8,128)(2,1)} %refs_0_.3), channel_id=1, source_target_pairs={{0,3},{1,2},{2,1},{3,0},{4,7},{5,6},{6,5},{7,4},{8,11},{9,10},{10,... | collective-permute-start | bytes 294920 | tf_op jit(solution)/shard_map/ppermute | solution.py:336
  3.5 0.0 copy-start.14
  3.5 0.0 copy-start.15
  3.5 0.0 copy-start.10
  3.5 0.7 %copy-done.15 = s32[2,1]{0,1:T(1,128)S(1)} copy-done((s32[2,1]{0,1:T(1,128)S(1)}, s32[2,1]{0,1:T(1,128)}, u32[]{:S(2)}) %copy-start.15) | copy-done | bytes 32
  4.2 0.1 copy.14.refs_6_
  4.3 0.0 copy-done.14
  4.3 0.7 %pad_add_fusion.refs_9_.refs_7_.place_ref = s32[4]{0:T(128)} fusion(s32[1]{0:T(128)} %bitcast.3, s32[1]{0:T(128)} %bitcast.2, s32[1]{0:T(128)} %bitcast.1, s32[1]{0:T(128)} %bitcast), kind=kLoop, calls=%fused_computation.1 | loop fusion | flops 12 | bytes 32 | tf_op jit(solution)/shard_map/stack | solution.py:341
  4.9 0.0 copy-start.12
  4.9 4.1 %prepare.1 = (s32[72,128]{1,0:T(8,128)}, s32[576]{0:T(1024)}, s32[1]{0:T(128)}, bf16[128,256]{1,0:T(8,128)(2,1)}, bf16[128,128]{1,0:T(8,128)(2,1)}, /*index=5*/bf16[128,128]{1,0:T(8,128)(2,1)}, f32[72,128]{1,0:T(8,128)}) custom-call(s32[128]{0:T(128)} %refs_0_.2, s32[128,128]{1,0:T(8,128)} %refs_1_.1, bf16[6,80]{1,0:T(8,128)(2,1)} %bitcast.18, ...), custom_call_target="tpu_custom_call" | custom-call | tf_op jit(solution)/shard_map/prepare/pallas_call | solution.py:140
  9.1 0.0 collective-permute-done.1.refs_2_
  9.1 0.0 collective-permute-done.refs_1_
  9.1 2.9 %collective-permute-done.2.refs_3_ = bf16[24,2048]{1,0:T(8,128)(2,1)S(1)} collective-permute-done((bf16[24,2048]{1,0:T(8,128)(2,1)}, bf16[24,2048]{1,0:T(8,128)(2,1)S(1)}, u32[]{:S(2)}, u32[]{:S(2)}) %collective-permute-start.2) | collective-permute-done | bytes 98336 | tf_op jit(solution)/shard_map/ppermute | solution.py:336
  12.0 0.0 copy-start.11
  12.0 0.0 copy-start.13
  12.0 0.0 copy-done.10
  12.0 0.0 copy-done.12
  12.0 0.7 %copy-done.11 = s32[576]{0:T(1024)S(1)} copy-done((s32[576]{0:T(1024)S(1)}, s32[576]{0:T(1024)}, u32[]{:S(2)}) %copy-start.11) | copy-done | bytes 2328
  12.7 0.0 copy-done.13
  12.7 0.0 copy-start
  12.7 0.8 %copy-done = bf16[128,256]{1,0:T(8,128)(2,1)S(1)} copy-done((bf16[128,256]{1,0:T(8,128)(2,1)S(1)}, bf16[128,256]{1,0:T(8,128)(2,1)}, u32[]{:S(2)}) %copy-start) | copy-done | bytes 65560
  13.5 0.0 copy-start.2
  13.5 0.8 %copy-done.2 = s32[72,128]{1,0:T(8,128)S(1)} copy-done((s32[72,128]{1,0:T(8,128)S(1)}, s32[72,128]{1,0:T(8,128)}, u32[]{:S(2)}) %copy-start.2) | copy-done | bytes 36888
  14.3 0.0 copy-start.4
  14.3 0.8 %copy-done.4 = f32[72,128]{1,0:T(8,128)S(1)} copy-done((f32[72,128]{1,0:T(8,128)S(1)}, f32[72,128]{1,0:T(8,128)}, u32[]{:S(2)}) %copy-start.4) | copy-done | bytes 36888
  15.0 0.0 copy-start.6
  15.0 0.8 %copy-done.6 = bf16[128,128]{1,0:T(8,128)(2,1)S(1)} copy-done((bf16[128,128]{1,0:T(8,128)(2,1)S(1)}, bf16[128,128]{1,0:T(8,128)(2,1)}, u32[]{:S(2)}) %copy-start.6) | copy-done | bytes 32792
  15.8 0.0 copy-start.8
  15.8 0.8 %copy-done.8 = bf16[128,128]{1,0:T(8,128)(2,1)S(1)} copy-done((bf16[128,128]{1,0:T(8,128)(2,1)S(1)}, bf16[128,128]{1,0:T(8,128)(2,1)}, u32[]{:S(2)}) %copy-start.8) | copy-done | bytes 32792
  16.6 0.0 copy-start.1
  16.6 0.0 copy-start.3
  16.6 0.0 copy-start.5
  16.6 0.0 copy-start.7
  16.6 0.0 copy-start.9
  16.6 2.6 %select_points.1 = (bf16[2048,128]{1,0:T(8,128)(2,1)S(1)}, bf16[1024,128]{1,0:T(8,128)(2,1)S(1)}) custom-call(bf16[24,2048]{1,0:T(8,128)(2,1)S(1)} %copy-done.10, bf16[24,2048]{1,0:T(8,128)(2,1)S(1)} %collective-permute-done.refs_1_, bf16[24,2048]{1,0:T(8,128)(2,1)S(1)} %collective-permute-done.1.refs_2_, ...), custom_call_target="tpu_custom_call" | custom-call | tf_op jit(solution)/shard_map/select_points/pallas_call | solution.py:201
  19.2 1.9 %collective-permute-start.3 = (bf16[1024,128]{1,0:T(8,128)(2,1)S(1)}, bf16[1024,128]{1,0:T(8,128)(2,1)S(1)}, u32[]{:S(2)}, u32[]{:S(2)}) collective-permute-start(bf16[1024,128]{1,0:T(8,128)(2,1)S(1)} %get-tuple-element.24), channel_id=1, source_target_pairs={{0,4},{2,6},{4,8},{5,1},{6,10},{7,3},{8,12},{9,5},{10,14},{11,7},{... | collective-permute-start | bytes 786440 | tf_op jit(solution)/shard_map/ppermute | solution.py:355
  21.1 6.7 %collective-permute-done.3.other_ref = bf16[1024,128]{1,0:T(8,128)(2,1)S(1)} collective-permute-done((bf16[1024,128]{1,0:T(8,128)(2,1)S(1)}, bf16[1024,128]{1,0:T(8,128)(2,1)S(1)}, u32[]{:S(2)}, u32[]{:S(2)}) %collective-permute-start.3) | collective-permute-done | bytes 262176 | tf_op jit(solution)/shard_map/ppermute | solution.py:355
  27.7 0.0 copy-done.1
  27.8 0.0 copy-done.3
  27.8 0.0 copy-done.5
  27.8 0.0 copy-done.7
  27.8 0.0 copy-done.9
  27.8 11.0 %encode.1 = (f32[24,128]{1,0:T(8,128)S(1)}, f32[24,128]{1,0:T(8,128)S(1)}) custom-call(bf16[2048,128]{1,0:T(8,128)(2,1)S(1)} %get-tuple-element.23.own_ref, bf16[1024,128]{1,0:T(8,128)(2,1)S(1)} %collective-permute-done.3.other_ref, s32[9216]{0:T(1024)S(1)} %bitcast.14, s32[576]{0:T(1024)S(1)} %copy-done.11, s32[1]{0:T(128)} %get-tuple-element.18.refs_10_.total_ref, ...), custom_call_target="tpu_custom_call" | custom-call | tf_op jit(solution)/shard_map/encode/pallas_call | solution.py:290
  38.8 0.1 collective-permute-start.4
  38.9 3.7 %collective-permute-done.4 = f32[24,128]{1,0:T(8,128)S(1)} collective-permute-done((f32[24,128]{1,0:T(8,128)S(1)}, f32[24,128]{1,0:T(8,128)S(1)}, u32[]{:S(2)}, u32[]{:S(2)}) %collective-permute-start.4) | collective-permute-done | bytes 12320 | tf_op jit(solution)/shard_map/ppermute | solution.py:357
  42.5 0.6 %add.12 = f32[24,128]{1,0:T(8,128)} add(f32[24,128]{1,0:T(8,128)S(1)} %get-tuple-element.25, f32[24,128]{1,0:T(8,128)S(1)} %collective-permute-done.4) | non-fusion elementwise | flops 3072 | bytes 36864 | tf_op jit(solution)/shard_map/add | solution.py:357
  (1 shorter events, 0.0 us)
Async XLA Ops:
  0.0 9.1 %collective-permute-start.1 = (bf16[24,2048]{1,0:T(8,128)(2,1)}, bf16[24,2048]{1,0:T(8,128)(2,1)S(1)}, u32[]{:S(2)}, u32[]{:S(2)}) collective-permute-start(bf16[24,2048]{1,0:T(8,128)(2,1)} %refs_0_.3), channel_id=1, source_target_pairs={{0,2},{1,3},{2,0},{3,1},{4,6},{5,7},{6,4},{7,5},{8,10},{9,11},{10,... | collective-permute-start | bytes 294920 | tf_op jit(solution)/shard_map/ppermute | solution.py:336
  0.3 8.7 %collective-permute-start = (bf16[24,2048]{1,0:T(8,128)(2,1)}, bf16[24,2048]{1,0:T(8,128)(2,1)S(1)}, u32[]{:S(2)}, u32[]{:S(2)}) collective-permute-start(bf16[24,2048]{1,0:T(8,128)(2,1)} %refs_0_.3), channel_id=1, source_target_pairs={{0,1},{1,0},{2,3},{3,2},{4,5},{5,4},{6,7},{7,6},{8,9},{9,8},{10,11... | collective-permute-start | bytes 294920 | tf_op jit(solution)/shard_map/ppermute | solution.py:336
  1.9 10.1 %collective-permute-start.2 = (bf16[24,2048]{1,0:T(8,128)(2,1)}, bf16[24,2048]{1,0:T(8,128)(2,1)S(1)}, u32[]{:S(2)}, u32[]{:S(2)}) collective-permute-start(bf16[24,2048]{1,0:T(8,128)(2,1)} %refs_0_.3), channel_id=1, source_target_pairs={{0,3},{1,2},{2,1},{3,0},{4,7},{5,6},{6,5},{7,4},{8,11},{9,10},{10,... | collective-permute-start | bytes 294920 | tf_op jit(solution)/shard_map/ppermute | solution.py:336
  3.5 0.8 %copy-start.14 = (s32[2,1024]{1,0:T(2,128)S(1)}, s32[2,1024]{1,0:T(2,128)}, u32[]{:S(2)}) copy-start(s32[2,1024]{1,0:T(2,128)} %param.15) | copy-start | bytes 24580
  3.5 0.7 %copy-start.15 = (s32[2,1]{0,1:T(1,128)S(1)}, s32[2,1]{0,1:T(1,128)}, u32[]{:S(2)}) copy-start(s32[2,1]{0,1:T(1,128)} %param.16) | copy-start | bytes 28
  3.5 8.5 %copy-start.10 = (bf16[24,2048]{1,0:T(8,128)(2,1)S(1)}, bf16[24,2048]{1,0:T(8,128)(2,1)}, u32[]{:S(2)}) copy-start(bf16[24,2048]{1,0:T(8,128)(2,1)} %refs_0_.3) | copy-start | bytes 294916
  4.9 7.1 %copy-start.12 = (bf16[3,2048]{1,0:T(4,128)(2,1)S(1)}, bf16[3,2048]{1,0:T(4,128)(2,1)}, u32[]{:S(2)}) copy-start(bf16[3,2048]{1,0:T(4,128)(2,1)} %refs_4_.1) | copy-start | bytes 36868
  12.0 0.7 %copy-start.11 = (s32[576]{0:T(1024)S(1)}, s32[576]{0:T(1024)}, u32[]{:S(2)}) copy-start(s32[576]{0:T(1024)} %get-tuple-element.17.refs_9_.list_ref) | copy-start | bytes 6916
  12.0 0.7 %copy-start.13 = (s32[4]{0:T(128)S(1)}, s32[4]{0:T(128)}, u32[]{:S(2)}) copy-start(s32[4]{0:T(128)} %pad_add_fusion.refs_9_.refs_7_.place_ref) | copy-start | bytes 52
  12.7 0.8 %copy-start = (bf16[128,256]{1,0:T(8,128)(2,1)S(1)}, bf16[128,256]{1,0:T(8,128)(2,1)}, u32[]{:S(2)}) copy-start(bf16[128,256]{1,0:T(8,128)(2,1)} %get-tuple-element.19.refs_11_.table_w) | copy-start | bytes 196612
  13.5 0.8 %copy-start.2 = (s32[72,128]{1,0:T(8,128)S(1)}, s32[72,128]{1,0:T(8,128)}, u32[]{:S(2)}) copy-start(s32[72,128]{1,0:T(8,128)} %get-tuple-element.16.refs_8_) | copy-start | bytes 110596
  14.3 0.8 %copy-start.4 = (f32[72,128]{1,0:T(8,128)S(1)}, f32[72,128]{1,0:T(8,128)}, u32[]{:S(2)}) copy-start(f32[72,128]{1,0:T(8,128)} %get-tuple-element.22.refs_14_.node_pre) | copy-start | bytes 110596
  15.0 0.8 %copy-start.6 = (bf16[128,128]{1,0:T(8,128)(2,1)S(1)}, bf16[128,128]{1,0:T(8,128)(2,1)}, u32[]{:S(2)}) copy-start(bf16[128,128]{1,0:T(8,128)(2,1)} %get-tuple-element.20.refs_12_.hidden_w) | copy-start | bytes 98308
  15.8 0.8 %copy-start.8 = (bf16[128,128]{1,0:T(8,128)(2,1)S(1)}, bf16[128,128]{1,0:T(8,128)(2,1)}, u32[]{:S(2)}) copy-start(bf16[128,128]{1,0:T(8,128)(2,1)} %get-tuple-element.21.refs_13_.out_w) | copy-start | bytes 98308
  16.6 11.2 %copy-start.1 = (bf16[128,256]{1,0:T(8,128)(2,1)S(1)}, bf16[128,256]{1,0:T(8,128)(2,1)}, u32[]{:S(2)}) copy-start(bf16[128,256]{1,0:T(8,128)(2,1)} %get-tuple-element.19.refs_11_.table_w) | copy-start | bytes 196612
  16.6 11.2 %copy-start.3 = (s32[72,128]{1,0:T(8,128)S(1)}, s32[72,128]{1,0:T(8,128)}, u32[]{:S(2)}) copy-start(s32[72,128]{1,0:T(8,128)} %get-tuple-element.16.refs_8_) | copy-start | bytes 110596
  16.6 11.2 %copy-start.5 = (f32[72,128]{1,0:T(8,128)S(1)}, f32[72,128]{1,0:T(8,128)}, u32[]{:S(2)}) copy-start(f32[72,128]{1,0:T(8,128)} %get-tuple-element.22.refs_14_.node_pre) | copy-start | bytes 110596
  16.6 11.2 %copy-start.7 = (bf16[128,128]{1,0:T(8,128)(2,1)S(1)}, bf16[128,128]{1,0:T(8,128)(2,1)}, u32[]{:S(2)}) copy-start(bf16[128,128]{1,0:T(8,128)(2,1)} %get-tuple-element.20.refs_12_.hidden_w) | copy-start | bytes 98308
  16.6 11.2 %copy-start.9 = (bf16[128,128]{1,0:T(8,128)(2,1)S(1)}, bf16[128,128]{1,0:T(8,128)(2,1)}, u32[]{:S(2)}) copy-start(bf16[128,128]{1,0:T(8,128)(2,1)} %get-tuple-element.21.refs_13_.out_w) | copy-start | bytes 98308
  19.2 8.6 %collective-permute-start.3 = (bf16[1024,128]{1,0:T(8,128)(2,1)S(1)}, bf16[1024,128]{1,0:T(8,128)(2,1)S(1)}, u32[]{:S(2)}, u32[]{:S(2)}) collective-permute-start(bf16[1024,128]{1,0:T(8,128)(2,1)S(1)} %get-tuple-element.24), channel_id=1, source_target_pairs={{0,4},{2,6},{4,8},{5,1},{6,10},{7,3},{8,12},{9,5},{10,14},{11,7},{... | collective-permute-start | bytes 786440 | tf_op jit(solution)/shard_map/ppermute | solution.py:355
  38.8 3.8 %collective-permute-start.4 = (f32[24,128]{1,0:T(8,128)S(1)}, f32[24,128]{1,0:T(8,128)S(1)}, u32[]{:S(2)}, u32[]{:S(2)}) collective-permute-start(f32[24,128]{1,0:T(8,128)S(1)} %get-tuple-element.26), channel_id=1, source_target_pairs={{0,1},{1,0},{2,3},{3,2},{4,5},{5,4},{6,7},{7,6},{8,9},{9,8},{10,11... | collective-permute-start | bytes 36872 | tf_op jit(solution)/shard_map/ppermute | solution.py:357

commit v5 on v4

--- a/solution.py
+++ b/solution.py
@@ -344,7 +344,7 @@
         out_weight, bias_three, place, groups, points, send, ZD * slabs,
     )
     own, sent = select_points(
-        blocks, coords, send_rows.reshape(-1), send_count, place, plan + weights
+        blocks, coords, send_rows.reshape(-1), send_count, place, plan[2:]
     )
     moves = []
     for slab in range(slabs):

time: 43.8 us -> 40.3 us (0.920)
  local copies, waits for them, and re-layouts: 5.36 us -> 2.02 us
    unnamed x34 -> x24, local copies, waits for them, and re-layouts: 5.36 us -> 2.02 us
where the time goes in v5:
time: 40.3 us; the launch traced here: 39.9 us
  Pallas kernels  17.9 us (44%)
  waiting for transfers between devices  13.3 us (33%)
  starting transfers between devices  5.48 us (14%)
  local copies, waits for them, and re-layouts  2.02 us (5%)
  other arithmetic  1.18 us (3%)
    pallas_call x1, Pallas kernels, encode(): pl.pallas_call(kernel, out_shape=(piece, piece), in_specs=[VMEM, VMEM] +...  11.1 us
    ppermute x1, waiting for transfers between devices, shards(): other = lax.ppermute(sent, ('slab', 'chan'), moves)  6.66 us
    pallas_call x1, Pallas kernels, prepare(): pl.pallas_call(kernel, out_shape=(jax.ShapeDtypeStruct((nodes + 8, slots)...  4.14 us
    ppermute x1, waiting for transfers between devices, shards(): lax.ppermute(give, 'chan', [(i, i ^ 1) for i in range(groups)])  3.68 us
    ppermute x3, starting transfers between devices, shards(): lax.ppermute(features, 'chan', [(i, i ^ step) for i in range(groups)])  3.49 us
    ppermute x3, waiting for transfers between devices, shards(): lax.ppermute(features, 'chan', [(i, i ^ step) for i in range(groups)])  2.97 us
    pallas_call x1, Pallas kernels, select_points(): pl.pallas_call(kernel, out_shape=(jax.ShapeDtypeStruct((points, LANES), j...  2.65 us
    unnamed x24, local copies, waits for them, and re-layouts  2.02 us
  transfers between devices with their start and end apart: 5, of which 3 were waited for; matrix products, arithmetic and copies ran while one was open for 2% of the time, Pallas kernels for 10%

profile of v5, /device:TPU:20, one launch (start us, length us, event | category | flops | bytes accessed | tf_op | source)
XLA Modules:
  0.0 39.9 jit_solution(4216153443152690039)
XLA Ops:
  0.0 0.3 collective-permute-start.1
  0.3 1.6 %collective-permute-start = (bf16[24,2048]{1,0:T(8,128)(2,1)}, bf16[24,2048]{1,0:T(8,128)(2,1)S(1)}, u32[]{:S(2)}, u32[]{:S(2)}) collective-permute-start(bf16[24,2048]{1,0:T(8,128)(2,1)} %refs_0_.3), channel_id=1, source_target_pairs={{0,1},{1,0},{2,3},{3,2},{4,5},{5,4},{6,7},{7,6},{8,9},{9,8},{10,11... | collective-permute-start | bytes 294920 | tf_op jit(solution)/shard_map/ppermute | solution.py:336
  1.9 1.6 %collective-permute-start.2 = (bf16[24,2048]{1,0:T(8,128)(2,1)}, bf16[24,2048]{1,0:T(8,128)(2,1)S(1)}, u32[]{:S(2)}, u32[]{:S(2)}) collective-permute-start(bf16[24,2048]{1,0:T(8,128)(2,1)} %refs_0_.3), channel_id=1, source_target_pairs={{0,3},{1,2},{2,1},{3,0},{4,7},{5,6},{6,5},{7,4},{8,11},{9,10},{10,... | collective-permute-start | bytes 294920 | tf_op jit(solution)/shard_map/ppermute | solution.py:336
  3.5 0.0 copy-start.10
  3.5 0.0 copy-start.9
  3.5 0.0 copy-start
  3.5 0.6 %copy-done.10 = s32[2,1]{0,1:T(1,128)S(1)} copy-done((s32[2,1]{0,1:T(1,128)S(1)}, s32[2,1]{0,1:T(1,128)}, u32[]{:S(2)}) %copy-start.10) | copy-done | bytes 32
  4.1 0.1 copy.14.refs_6_
  4.2 0.0 copy-done.9
  4.2 0.6 %pad_add_fusion.refs_9_.refs_7_.place_ref = s32[4]{0:T(128)} fusion(s32[1]{0:T(128)} %bitcast.3, s32[1]{0:T(128)} %bitcast.2, s32[1]{0:T(128)} %bitcast.1, s32[1]{0:T(128)} %bitcast), kind=kLoop, calls=%fused_computation.1 | loop fusion | flops 12 | bytes 32 | tf_op jit(solution)/shard_map/stack | solution.py:341
  4.8 0.0 copy-start.6
  4.8 4.1 %prepare.1 = (s32[72,128]{1,0:T(8,128)}, s32[576]{0:T(1024)}, s32[1]{0:T(128)}, bf16[128,256]{1,0:T(8,128)(2,1)}, bf16[128,128]{1,0:T(8,128)(2,1)}, /*index=5*/bf16[128,128]{1,0:T(8,128)(2,1)}, f32[72,128]{1,0:T(8,128)}) custom-call(s32[128]{0:T(128)} %refs_0_.2, s32[128,128]{1,0:T(8,128)} %refs_1_.1, bf16[6,80]{1,0:T(8,128)(2,1)} %bitcast.18, ...), custom_call_target="tpu_custom_call" | custom-call | tf_op jit(solution)/shard_map/prepare/pallas_call | solution.py:140
  9.0 0.0 collective-permute-done.1.refs_2_
  9.0 0.0 collective-permute-done.refs_1_
  9.0 3.0 %collective-permute-done.2.refs_3_ = bf16[24,2048]{1,0:T(8,128)(2,1)S(1)} collective-permute-done((bf16[24,2048]{1,0:T(8,128)(2,1)}, bf16[24,2048]{1,0:T(8,128)(2,1)S(1)}, u32[]{:S(2)}, u32[]{:S(2)}) %collective-permute-start.2) | collective-permute-done | bytes 98336 | tf_op jit(solution)/shard_map/ppermute | solution.py:336
  12.0 0.0 copy-start.7
  12.0 0.0 copy-done
  12.0 0.0 copy-done.6
  12.0 0.6 %copy-done.7 = s32[4]{0:T(128)S(1)} copy-done((s32[4]{0:T(128)S(1)}, s32[4]{0:T(128)}, u32[]{:S(2)}) %copy-start.7) | copy-done | bytes 40
  12.6 0.0 copy-start.1
  12.6 0.0 copy-start.2
  12.6 0.0 copy-start.3
  12.6 0.0 copy-start.4
  12.6 0.0 copy-start.5
  12.6 2.6 %select_points.1 = (bf16[2048,128]{1,0:T(8,128)(2,1)S(1)}, bf16[1024,128]{1,0:T(8,128)(2,1)S(1)}) custom-call(bf16[24,2048]{1,0:T(8,128)(2,1)S(1)} %copy-done, bf16[24,2048]{1,0:T(8,128)(2,1)S(1)} %collective-permute-done.refs_1_, bf16[24,2048]{1,0:T(8,128)(2,1)S(1)} %collective-permute-done.1.refs_2_, bf16[24,2048]{1,0:T(8,128)(2,1)S(1)} %collective-permute-done.2.refs_3_, ...), custom_call_target="tpu_custom_call" | custom-call | tf_op jit(solution)/shard_map/select_points/pallas_call | solution.py:201
  15.2 1.9 %collective-permute-start.3 = (bf16[1024,128]{1,0:T(8,128)(2,1)S(1)}, bf16[1024,128]{1,0:T(8,128)(2,1)S(1)}, u32[]{:S(2)}, u32[]{:S(2)}) collective-permute-start(bf16[1024,128]{1,0:T(8,128)(2,1)S(1)} %get-tuple-element.18), channel_id=1, source_target_pairs={{0,4},{2,6},{4,8},{5,1},{6,10},{7,3},{8,12},{9,5},{10,14},{11,7},{... | collective-permute-start | bytes 786440 | tf_op jit(solution)/shard_map/ppermute | solution.py:355
  17.2 6.7 %collective-permute-done.3.other_ref = bf16[1024,128]{1,0:T(8,128)(2,1)S(1)} collective-permute-done((bf16[1024,128]{1,0:T(8,128)(2,1)S(1)}, bf16[1024,128]{1,0:T(8,128)(2,1)S(1)}, u32[]{:S(2)}, u32[]{:S(2)}) %collective-permute-start.3) | collective-permute-done | bytes 262176 | tf_op jit(solution)/shard_map/ppermute | solution.py:355
  23.8 0.0 copy-start.8
  23.8 0.0 copy-done.1
  23.8 0.0 copy-done.2
  23.8 0.0 copy-done.3
  23.8 0.0 copy-done.4
  23.9 0.0 copy-done.5
  23.9 0.7 %copy-done.8 = s32[576]{0:T(1024)S(1)} copy-done((s32[576]{0:T(1024)S(1)}, s32[576]{0:T(1024)}, u32[]{:S(2)}) %copy-start.8) | copy-done | bytes 2328
  24.5 11.1 %encode.1 = (f32[24,128]{1,0:T(8,128)S(1)}, f32[24,128]{1,0:T(8,128)S(1)}) custom-call(bf16[2048,128]{1,0:T(8,128)(2,1)S(1)} %get-tuple-element.17.own_ref, bf16[1024,128]{1,0:T(8,128)(2,1)S(1)} %collective-permute-done.3.other_ref, s32[9216]{0:T(1024)S(1)} %bitcast.14, s32[576]{0:T(1024)S(1)} %copy-done.8, s32[1]{0:T(128)} %get-tuple-element.16.refs_8_.total_ref, ...), custom_call_target="tpu_custom_call" | custom-call | tf_op jit(solution)/shard_map/encode/pallas_call | solution.py:290
  35.6 0.1 collective-permute-start.4
  35.7 3.7 %collective-permute-done.4 = f32[24,128]{1,0:T(8,128)S(1)} collective-permute-done((f32[24,128]{1,0:T(8,128)S(1)}, f32[24,128]{1,0:T(8,128)S(1)}, u32[]{:S(2)}, u32[]{:S(2)}) %collective-permute-start.4) | collective-permute-done | bytes 12320 | tf_op jit(solution)/shard_map/ppermute | solution.py:357
  39.3 0.6 %add.12 = f32[24,128]{1,0:T(8,128)} add(f32[24,128]{1,0:T(8,128)S(1)} %get-tuple-element.25, f32[24,128]{1,0:T(8,128)S(1)} %collective-permute-done.4) | non-fusion elementwise | flops 3072 | bytes 36864 | tf_op jit(solution)/shard_map/add | solution.py:357
  (1 shorter events, 0.0 us)
Async XLA Ops:
  0.0 9.0 %collective-permute-start.1 = (bf16[24,2048]{1,0:T(8,128)(2,1)}, bf16[24,2048]{1,0:T(8,128)(2,1)S(1)}, u32[]{:S(2)}, u32[]{:S(2)}) collective-permute-start(bf16[24,2048]{1,0:T(8,128)(2,1)} %refs_0_.3), channel_id=1, source_target_pairs={{0,2},{1,3},{2,0},{3,1},{4,6},{5,7},{6,4},{7,5},{8,10},{9,11},{10,... | collective-permute-start | bytes 294920 | tf_op jit(solution)/shard_map/ppermute | solution.py:336
  0.3 8.7 %collective-permute-start = (bf16[24,2048]{1,0:T(8,128)(2,1)}, bf16[24,2048]{1,0:T(8,128)(2,1)S(1)}, u32[]{:S(2)}, u32[]{:S(2)}) collective-permute-start(bf16[24,2048]{1,0:T(8,128)(2,1)} %refs_0_.3), channel_id=1, source_target_pairs={{0,1},{1,0},{2,3},{3,2},{4,5},{5,4},{6,7},{7,6},{8,9},{9,8},{10,11... | collective-permute-start | bytes 294920 | tf_op jit(solution)/shard_map/ppermute | solution.py:336
  1.9 10.1 %collective-permute-start.2 = (bf16[24,2048]{1,0:T(8,128)(2,1)}, bf16[24,2048]{1,0:T(8,128)(2,1)S(1)}, u32[]{:S(2)}, u32[]{:S(2)}) collective-permute-start(bf16[24,2048]{1,0:T(8,128)(2,1)} %refs_0_.3), channel_id=1, source_target_pairs={{0,3},{1,2},{2,1},{3,0},{4,7},{5,6},{6,5},{7,4},{8,11},{9,10},{10,... | collective-permute-start | bytes 294920 | tf_op jit(solution)/shard_map/ppermute | solution.py:336
  3.5 0.7 %copy-start.10 = (s32[2,1]{0,1:T(1,128)S(1)}, s32[2,1]{0,1:T(1,128)}, u32[]{:S(2)}) copy-start(s32[2,1]{0,1:T(1,128)} %param.16) | copy-start | bytes 28
  3.5 0.7 %copy-start.9 = (s32[2,1024]{1,0:T(2,128)S(1)}, s32[2,1024]{1,0:T(2,128)}, u32[]{:S(2)}) copy-start(s32[2,1024]{1,0:T(2,128)} %param.15) | copy-start | bytes 24580
  3.5 8.5 %copy-start = (bf16[24,2048]{1,0:T(8,128)(2,1)S(1)}, bf16[24,2048]{1,0:T(8,128)(2,1)}, u32[]{:S(2)}) copy-start(bf16[24,2048]{1,0:T(8,128)(2,1)} %refs_0_.3) | copy-start | bytes 294916
  4.8 7.1 %copy-start.6 = (bf16[3,2048]{1,0:T(4,128)(2,1)S(1)}, bf16[3,2048]{1,0:T(4,128)(2,1)}, u32[]{:S(2)}) copy-start(bf16[3,2048]{1,0:T(4,128)(2,1)} %refs_4_.1) | copy-start | bytes 36868
  12.0 0.6 %copy-start.7 = (s32[4]{0:T(128)S(1)}, s32[4]{0:T(128)}, u32[]{:S(2)}) copy-start(s32[4]{0:T(128)} %pad_add_fusion.refs_9_.refs_7_.place_ref) | copy-start | bytes 52
  12.6 11.3 %copy-start.1 = (bf16[128,256]{1,0:T(8,128)(2,1)S(1)}, bf16[128,256]{1,0:T(8,128)(2,1)}, u32[]{:S(2)}) copy-start(bf16[128,256]{1,0:T(8,128)(2,1)} %get-tuple-element.21.table_w) | copy-start | bytes 196612
  12.6 11.3 %copy-start.2 = (s32[72,128]{1,0:T(8,128)S(1)}, s32[72,128]{1,0:T(8,128)}, u32[]{:S(2)}) copy-start(s32[72,128]{1,0:T(8,128)} %get-tuple-element.19) | copy-start | bytes 110596
  12.6 11.3 %copy-start.3 = (f32[72,128]{1,0:T(8,128)S(1)}, f32[72,128]{1,0:T(8,128)}, u32[]{:S(2)}) copy-start(f32[72,128]{1,0:T(8,128)} %get-tuple-element.24.node_pre) | copy-start | bytes 110596
  12.6 11.3 %copy-start.4 = (bf16[128,128]{1,0:T(8,128)(2,1)S(1)}, bf16[128,128]{1,0:T(8,128)(2,1)}, u32[]{:S(2)}) copy-start(bf16[128,128]{1,0:T(8,128)(2,1)} %get-tuple-element.22.hidden_w) | copy-start | bytes 98308
  12.6 11.3 %copy-start.5 = (bf16[128,128]{1,0:T(8,128)(2,1)S(1)}, bf16[128,128]{1,0:T(8,128)(2,1)}, u32[]{:S(2)}) copy-start(bf16[128,128]{1,0:T(8,128)(2,1)} %get-tuple-element.23.out_w) | copy-start | bytes 98308
  15.2 8.6 %collective-permute-start.3 = (bf16[1024,128]{1,0:T(8,128)(2,1)S(1)}, bf16[1024,128]{1,0:T(8,128)(2,1)S(1)}, u32[]{:S(2)}, u32[]{:S(2)}) collective-permute-start(bf16[1024,128]{1,0:T(8,128)(2,1)S(1)} %get-tuple-element.18), channel_id=1, source_target_pairs={{0,4},{2,6},{4,8},{5,1},{6,10},{7,3},{8,12},{9,5},{10,14},{11,7},{... | collective-permute-start | bytes 786440 | tf_op jit(solution)/shard_map/ppermute | solution.py:355
  23.8 0.7 %copy-start.8 = (s32[576]{0:T(1024)S(1)}, s32[576]{0:T(1024)}, u32[]{:S(2)}) copy-start(s32[576]{0:T(1024)} %get-tuple-element.20.list_ref) | copy-start | bytes 6916
  35.6 3.8 %collective-permute-start.4 = (f32[24,128]{1,0:T(8,128)S(1)}, f32[24,128]{1,0:T(8,128)S(1)}, u32[]{:S(2)}, u32[]{:S(2)}) collective-permute-start(f32[24,128]{1,0:T(8,128)S(1)} %get-tuple-element.26), channel_id=1, source_target_pairs={{0,1},{1,0},{2,3},{3,2},{4,5},{5,4},{6,7},{7,6},{8,9},{9,8},{10,11... | collective-permute-start | bytes 36872 | tf_op jit(solution)/shard_map/ppermute | solution.py:357

commit v6 on v5

--- a/solution.py
+++ b/solution.py
@@ -17,7 +17,6 @@
 
 SMEM = pl.BlockSpec(memory_space=pltpu.SMEM)
 VMEM = pl.BlockSpec(memory_space=pltpu.VMEM)
-ANY = pl.BlockSpec(memory_space=pl.ANY)
 HBM = pl.BlockSpec(memory_space=pltpu.MemorySpace.HBM)
 
 
@@ -28,9 +27,10 @@
 
 def prepare(
     neighbours, neighbour_count, geom_weight, feat_weight, bias_one, hidden_weight, bias_two,
-    out_weight, bias_three, place, groups, points, send, depth,
+    out_weight, bias_three, place, groups, points, send_rows, depth,
 ):
     per_slab, slots = neighbours.shape
+    send = send_rows.shape[1]
     hidden, channels = feat_weight.shape
     chans = channels // groups
     width = LANES // groups
@@ -48,12 +48,14 @@
 
     given = (
         neighbour_count, neighbours, geom_weight.T, feat_weight, bias_one[None], hidden_weight,
-        bias_two[None], out_weight.T, bias_three[None],
+        bias_two[None], out_weight.T, bias_three[None], send_rows,
     )
+    tall = most * CHUNK // slots + 3 * BLOCK * CHUNK // slots
+    listed = send // LANES
 
     def kernel(*refs):
         place_ref = refs[len(given)]
-        rows_ref, list_ref, total_ref, table_w, hidden_w, out_w, node_pre = refs[len(given) + 1 :][:7]
+        rows_ref, list_ref, sent_ref, table_w, hidden_w, out_w, node_pre = refs[len(given) + 1 :][:7]
         held = refs[len(given) + 8 :][: len(given)]
         wide, square, spread, arrived = refs[2 * len(given) + 8 :]
         copies = [
@@ -64,31 +66,51 @@
             copy.start()
         for copy in copies:
             copy.wait()
-        count_ref, nbr_ref, geom_ref, feat_ref, one_ref, hidden_ref, two_ref, out_ref, three_ref = held
+        count_ref, nbr_ref, geom_ref, feat_ref, one_ref, hidden_ref, two_ref, out_ref, three_ref, send_ref = held
         member = place_ref[0]
         first_id = place_ref[2]
         start = place_ref[3]
         lane = lax.broadcasted_iota(jnp.int32, (1, LANES), 1)
 
-        def one_node(node, at):
-            count = count_ref[start + node]
-            row = nbr_ref[pl.ds(start + node, 1), :]
-            row = jnp.where(row >= points + send, row - send, row)
-            slot = lax.broadcasted_iota(jnp.int32, (1, slots), 1)
-            rows_ref[pl.ds(node, 1), :] = jnp.where(slot < count, 2 * row, nothing)
-            for piece in range(per_node):
-                list_ref[at + piece] = node * per_node + piece
-            return at + (count + CHUNK - 1) // CHUNK
-
-        used = lax.fori_loop(0, nodes, one_node, 0)
-        rows_ref[pl.ds(nodes, 8), :] = jnp.full((8, slots), nothing, jnp.int32)
-        total_ref[0] = (used + BLOCK - 1) // BLOCK
+        slot = lax.broadcasted_iota(jnp.int32, (1, slots), 1)
+        rows_ref[...] = jnp.full((tall, slots), nothing, jnp.int32)
+        together = 8
+
+        def some_nodes(step, at):
+            first = step * together
+            counts = [count_ref[start + first + i] for i in range(together)]
+            spots = []
+            for i in range(together):
+                spots.append(at)
+                at = at + (counts[i] + CHUNK - 1) // CHUNK
+            turned = []
+            for i in range(together):
+                row = nbr_ref[pl.ds(start + first + i, 1), :]
+                row = jnp.where(row >= points + send, row - send, row)
+                row = jnp.where(slot < counts[i], 2 * row, nothing)
+                turned.append(pltpu.roll(row, (spots[i] % per_node) * CHUNK, 1))
+            for i in range(together):
+                line = spots[i] // per_node
+                kept = slot < (spots[i] % per_node) * CHUNK
+                rows_ref[pl.ds(line, 1), :] = jnp.where(kept, rows_ref[pl.ds(line, 1), :], turned[i])
+                rows_ref[pl.ds(line + 1, 1), :] = turned[i]
+                for piece in range(per_node):
+                    list_ref[spots[i] + piece] = first + i
+            return at
+
+        used = lax.fori_loop(0, nodes // together, some_nodes, 0)
 
         def fill(step, carry):
-            list_ref[used + step] = most
+            for i in range(8):
+                list_ref[used + 8 * step + i] = nodes
             return carry
 
-        lax.fori_loop(0, BLOCK, fill, 0)
+        lax.fori_loop(0, 3 * BLOCK // 8, fill, 0)
+        list_ref[most + 3 * BLOCK] = (used + 2 * BLOCK - 1) // (2 * BLOCK)
+        side = place_ref[1]
+        chosen = send_ref[pl.ds(side, 1), :]
+        for line in range(listed):
+            sent_ref[line : line + 1, :] = chosen[:, line * LANES : (line + 1) * LANES]
 
         square[...] = jnp.zeros((LANES, LANES), jnp.float32)
         square[0:hidden, 0:channels] = feat_ref[...].astype(jnp.float32)
@@ -140,16 +162,16 @@
     out = pl.pallas_call(
         kernel,
         out_shape=(
-            jax.ShapeDtypeStruct((nodes + 8, slots), jnp.int32),
-            jax.ShapeDtypeStruct((most + BLOCK,), jnp.int32),
-            jax.ShapeDtypeStruct((1,), jnp.int32),
+            jax.ShapeDtypeStruct((tall, slots), jnp.int32),
+            jax.ShapeDtypeStruct((most + 3 * BLOCK + 1,), jnp.int32),
+            jax.ShapeDtypeStruct((listed, LANES), jnp.int32),
             jax.ShapeDtypeStruct((LANES, 2 * LANES), jnp.bfloat16),
             jax.ShapeDtypeStruct((LANES, LANES), jnp.bfloat16),
             jax.ShapeDtypeStruct((LANES, LANES), jnp.bfloat16),
             jax.ShapeDtypeStruct((nodes + 8, LANES), jnp.float32),
         ),
         in_specs=[HBM] * len(given) + [SMEM],
-        out_specs=(VMEM, SMEM, SMEM) + (VMEM,) * 4,
+        out_specs=(VMEM, SMEM, VMEM) + (VMEM,) * 4,
         scratch_shapes=[pltpu.SMEM(neighbour_count.shape, jnp.int32)]
         + [pltpu.VMEM(array.shape, array.dtype) for array in given[1:]]
         + [
@@ -160,20 +182,20 @@
         ],
         name="prepare",
     )(*given, place)
-    return out[:3], out[3:]
-
-
-def select_points(blocks, coords, send_rows, send_count, place, after):
+    return out[:2], out[2], out[3:]
+
+
+def select_points(blocks, coords, send_rows, send_count, place):
     groups = len(blocks)
     chans, points = blocks[0].shape
     width = LANES // groups
-    send = send_rows.shape[0] // 2
-    unroll = 32
+    send = send_rows.shape[0] * LANES
+    unroll = 16
 
     def kernel(*refs):
         block_refs = refs[:groups]
         coords_ref, rows_ref, count_ref, place_ref = refs[groups : groups + 4]
-        own_ref, sent_ref, stack, table, picked = refs[groups + 4 + len(after) :]
+        own_ref, sent_ref, stack, table, picked = refs[groups + 4 :]
         member = place_ref[0]
         side = place_ref[1]
         for step in range(groups):
@@ -186,15 +208,12 @@
         own_ref[...] = own
         table[...] = own.astype(jnp.float32)
 
-        def gather(step, carry):
-            base = step * unroll
-            names = rows_ref.at[pl.ds(side * send + base, unroll)]
-            rows = [table[pl.ds(names[j], 1), :] for j in range(unroll)]
+        for base in range(0, send, unroll):
+            rows = [
+                table[pl.ds(rows_ref[at // LANES, at % LANES], 1), :] for at in range(base, base + unroll)
+            ]
             for j in range(unroll):
-                picked[pl.ds(base + j, 1), :] = rows[j]
-            return carry
-
-        lax.fori_loop(0, send // unroll, gather, 0)
+                picked[base + j : base + j + 1, :] = rows[j]
         slot = lax.broadcasted_iota(jnp.int32, (send, LANES), 0)
         sent_ref[...] = jnp.where(slot < count_ref[side, 0], picked[...], 0.0).astype(jnp.bfloat16)
 
@@ -204,7 +223,7 @@
             jax.ShapeDtypeStruct((points, LANES), jnp.bfloat16),
             jax.ShapeDtypeStruct((send, LANES), jnp.bfloat16),
         ),
-        in_specs=[VMEM] * (groups + 1) + [SMEM] * 3 + [ANY] * len(after),
+        in_specs=[VMEM] * (groups + 1) + [SMEM] * 3,
         out_specs=(VMEM, VMEM),
         scratch_shapes=[
             pltpu.VMEM((LANES, points), jnp.bfloat16),
@@ -213,25 +232,33 @@
         ],
         compiler_params=pltpu.CompilerParams(vmem_limit_bytes=12 << 20),
         name="select_points",
-    )(*blocks, coords, send_rows, send_count, place, *after)
+    )(*blocks, coords, send_rows, send_count, place)
 
 
 def encode(own, other, plan, place, weights, chans, width):
-    rows, chunks, total = plan
+    rows, spots = plan
     table_weight, hidden_weight, out_weight, node_part = weights
     points = own.shape[0]
     send = other.shape[0]
-    nodes = rows.shape[0] - 8
+    nodes = node_part.shape[0] - 8
     slots = rows.shape[1]
-    shift = (slots // CHUNK).bit_length() - 1
     total_rows = points + send
     pairs = BLOCK * CHUNK
+    lines = pairs // slots
 
     def kernel(
-        own_ref, other_ref, rows_ref, list_ref, total_ref, place_ref, table_w, hidden_w, out_w,
-        node_pre, keep_ref, give_ref, table, picked, acc, turned,
+        own_ref, other_ref, rows_ref, spot_ref, place_ref, table_w, hidden_w, out_w, node_pre,
+        keep_ref, give_ref, table, picked_a, picked_b, names_a, names_b, acc, turned, arrived,
     ):
         parity = place_ref[1]
+        steps = spot_ref[spots.shape[0] - 1]
+
+        def fetch(block, names, which):
+            source = rows_ref.at[pl.ds(pl.multiple_of(block * lines, lines), lines), :]
+            return pltpu.make_async_copy(source, names, arrived.at[which])
+
+        fetch(0, names_a, 0).start()
+        fetch(1, names_b, 1).start()
 
         def fill(source, start, count):
             step = 256
@@ -246,20 +273,22 @@
         table[pl.ds(2 * total_rows, 8), :] = jnp.zeros((8, LANES), jnp.float32)
         acc[...] = jnp.zeros((nodes + 8, 8, LANES), jnp.float32)
 
-        def one_block(index, carry):
-            ids = list_ref.at[pl.ds(index * BLOCK, BLOCK)]
-            names = [ids[piece] for piece in range(BLOCK)]
-            for piece in range(BLOCK):
-                where = rows_ref.at[pl.ds(names[piece] * CHUNK, CHUNK)]
-                got = [table[pl.ds(where[j], 2), :] for j in range(CHUNK)]
+        def gather(names, picked):
+            for base in range(0, pairs, CHUNK):
+                got = [
+                    table[pl.ds(names[at // slots, at % slots], 2), :] for at in range(base, base + CHUNK)
+                ]
                 for j in range(CHUNK):
-                    picked[pl.ds(2 * (piece * CHUNK + j), 2), :] = got[j]
+                    picked[2 * (base + j) : 2 * (base + j) + 2, :] = got[j]
+
+        def compute(block, picked):
+            of_block = spot_ref.at[pl.ds(block * BLOCK, BLOCK)]
             step = 8
             for group in range(BLOCK // step):
                 base = group * step * CHUNK
-                spots = [names[group * step + i] >> shift for i in range(step)]
+                here = [of_block[group * step + i] for i in range(step)]
                 offset = jnp.concatenate(
-                    [jnp.broadcast_to(node_pre[pl.ds(spot, 1), :], (CHUNK, LANES)) for spot in spots],
+                    [jnp.broadcast_to(node_pre[pl.ds(spot, 1), :], (CHUNK, LANES)) for spot in here],
                     axis=0,
                 )
                 pre = picked[pl.ds(2 * base, step * CHUNK, stride=2), :]
@@ -269,14 +298,31 @@
                 second = gelu_doubled(second).astype(jnp.bfloat16)
                 kappa = jnp.dot(second, out_w[...], preferred_element_type=jnp.float32)
                 product = kappa * val
-                for i, spot in enumerate(spots):
-                    low = product[i * CHUNK : i * CHUNK + 8]
+                for i, spot in enumerate(here):
+                    part = product[i * CHUNK : i * CHUNK + 8]
                     for j in range(8, CHUNK, 8):
-                        low = low + product[i * CHUNK + j : i * CHUNK + j + 8]
-                    acc[spot] = acc[spot] + low
+                        part = part + product[i * CHUNK + j : i * CHUNK + j + 8]
+                    acc[spot] = acc[spot] + part
+
+        fetch(0, names_a, 0).wait()
+        gather(names_a, picked_a)
+        fetch(2, names_a, 0).start()
+
+        def one_step(index, carry):
+            block = 2 * index
+            fetch(block + 1, names_b, 1).wait()
+            gather(names_b, picked_b)
+            compute(block, picked_a)
+            fetch(block + 3, names_b, 1).start()
+            fetch(block + 2, names_a, 0).wait()
+            gather(names_a, picked_a)
+            compute(block + 1, picked_b)
+            fetch(block + 4, names_a, 0).start()
             return carry
 
-        lax.fori_loop(0, total_ref[0], one_block, 0)
+        lax.fori_loop(0, steps, one_step, 0)
+        fetch(0, names_a, 0).wait()
+        fetch(1, names_b, 1).wait()
         sums = jnp.sum(acc[0:nodes], axis=1)
         means = (sums / sums[:, LANES - 1 :]).T
         low = jnp.where(parity == 1, means, 0.0)
@@ -290,20 +336,21 @@
     return pl.pallas_call(
         kernel,
         out_shape=(piece, piece),
-        in_specs=[VMEM, VMEM] + [SMEM] * 4 + [VMEM] * 4,
+        in_specs=[VMEM, VMEM, VMEM, SMEM, SMEM] + [VMEM] * 4,
         out_specs=(VMEM, VMEM),
         scratch_shapes=[
             pltpu.VMEM((2 * total_rows + 8, LANES), jnp.float32),
             pltpu.VMEM((2 * pairs, LANES), jnp.float32),
+            pltpu.VMEM((2 * pairs, LANES), jnp.float32),
+            pltpu.SMEM((lines, slots), jnp.int32),
+            pltpu.SMEM((lines, slots), jnp.int32),
             pltpu.VMEM((nodes + 8, 8, LANES), jnp.float32),
             pltpu.VMEM((LANES, ZD * nodes), jnp.float32),
+            pltpu.SemaphoreType.DMA((2,)),
         ],
         compiler_params=pltpu.CompilerParams(vmem_limit_bytes=16 << 20),
         name="encode",
-    )(
-        own, other, rows.reshape(-1), chunks, total, place, table_weight, hidden_weight, out_weight,
-        node_part,
-    )
+    )(own, other, rows, spots, place, table_weight, hidden_weight, out_weight, node_part)
 
 
 def shards(
@@ -326,7 +373,6 @@
     member = lax.axis_index("chan")
     slab_id = lax.axis_index("slab")
     chans, points = features.shape
-    send = send_rows.shape[1]
     per_slab = neighbours.shape[0]
     nodes = per_slab // ZD
     width = LANES // groups
@@ -339,13 +385,11 @@
     start = plane * nodes
     upper = 1 - plane
     place = jnp.stack([member, upper, slab_id * per_slab + start, start]).astype(jnp.int32)
-    plan, weights = prepare(
+    plan, sent_rows, weights = prepare(
         neighbours, neighbour_count, geom_weight, feat_weight, bias_one, hidden_weight, bias_two,
-        out_weight, bias_three, place, groups, points, send, ZD * slabs,
+        out_weight, bias_three, place, groups, points, send_rows, ZD * slabs,
     )
-    own, sent = select_points(
-        blocks, coords, send_rows.reshape(-1), send_count, place, plan[2:]
-    )
+    own, sent = select_points(blocks, coords, sent_rows, send_count, place)
     moves = []
     for slab in range(slabs):
         for who in range(groups):

time: 40.3 us -> 38.1 us (0.945)
  Pallas kernels: 17.9 us -> 15.7 us
    pallas_call x2, Pallas kernels: 15.2 us -> 13.9 us  [the longest x1 9.66 us: encode(): pl.pallas_call(kernel, out_shape=(piece, piece), in_specs=[VMEM, VMEM, VM...]
    pallas_call x1, Pallas kernels: 2.65 us -> 1.82 us  [select_points(): pl.pallas_call(kernel, out_shape=(jax.ShapeDtypeStruct((points, LANES), j...]
    unnamed x24 -> x23, local copies, waits for them, and re-layouts: 2.02 us -> 2.1 us
  transfers between devices with their start and end apart: 5 -> 5, of which waited for: 3 -> 3; matrix products, arithmetic and copies ran while one was open for 2% -> 2% of each run, Pallas kernels for 10% -> 11%
where the time goes in v6:
time: 38.1 us; the launch traced here: 37.8 us
  Pallas kernels  15.7 us (41%)
  waiting for transfers between devices  13.2 us (35%)
  starting transfers between devices  5.48 us (14%)
  local copies, waits for them, and re-layouts  2.1 us (6%)
  other arithmetic  1.26 us (3%)
    pallas_call x1, Pallas kernels, encode(): pl.pallas_call(kernel, out_shape=(piece, piece), in_specs=[VMEM, VMEM, VM...  9.66 us
    ppermute x1, waiting for transfers between devices, shards(): other = lax.ppermute(sent, ('slab', 'chan'), moves)  6.66 us
    pallas_call x1, Pallas kernels, prepare(): pl.pallas_call(kernel, out_shape=(jax.ShapeDtypeStruct((tall, slots), jnp...  4.2 us
    ppermute x1, waiting for transfers between devices, shards(): lax.ppermute(give, 'chan', [(i, i ^ 1) for i in range(groups)])  3.68 us
    ppermute x3, starting transfers between devices, shards(): lax.ppermute(features, 'chan', [(i, i ^ step) for i in range(groups)])  3.49 us
    ppermute x3, waiting for transfers between devices, shards(): lax.ppermute(features, 'chan', [(i, i ^ step) for i in range(groups)])  2.83 us
    unnamed x23, local copies, waits for them, and re-layouts  2.1 us
    ppermute x1, starting transfers between devices, shards(): other = lax.ppermute(sent, ('slab', 'chan'), moves)  1.92 us
  transfers between devices with their start and end apart: 5, of which 3 were waited for; matrix products, arithmetic and copies ran while one was open for 2% of the time, Pallas kernels for 11%

profile of v6, /device:TPU:20, one launch (start us, length us, event | category | flops | bytes accessed | tf_op | source)
XLA Modules:
  0.0 37.8 jit_solution(5968510173741075186)
XLA Ops:
  0.0 0.3 collective-permute-start.1
  0.3 1.6 %collective-permute-start = (bf16[24,2048]{1,0:T(8,128)(2,1)}, bf16[24,2048]{1,0:T(8,128)(2,1)S(1)}, u32[]{:S(2)}, u32[]{:S(2)}) collective-permute-start(bf16[24,2048]{1,0:T(8,128)(2,1)} %refs_0_.3), channel_id=1, source_target_pairs={{0,1},{1,0},{2,3},{3,2},{4,5},{5,4},{6,7},{7,6},{8,9},{9,8},{10,11... | collective-permute-start | bytes 294920 | tf_op jit(solution)/shard_map/ppermute | solution.py:382
  1.9 1.6 %collective-permute-start.2 = (bf16[24,2048]{1,0:T(8,128)(2,1)}, bf16[24,2048]{1,0:T(8,128)(2,1)S(1)}, u32[]{:S(2)}, u32[]{:S(2)}) collective-permute-start(bf16[24,2048]{1,0:T(8,128)(2,1)} %refs_0_.3), channel_id=1, source_target_pairs={{0,3},{1,2},{2,1},{3,0},{4,7},{5,6},{6,5},{7,4},{8,11},{9,10},{10,... | collective-permute-start | bytes 294920 | tf_op jit(solution)/shard_map/ppermute | solution.py:382
  3.5 0.0 copy-start.10
  3.5 0.0 copy-start
  3.5 0.7 %copy-done.10 = s32[2,1]{0,1:T(1,128)S(1)} copy-done((s32[2,1]{0,1:T(1,128)S(1)}, s32[2,1]{0,1:T(1,128)}, u32[]{:S(2)}) %copy-start.10) | copy-done | bytes 32
  4.1 0.1 copy.14.refs_6_
  4.2 0.7 %pad_add_fusion.refs_10_.refs_7_.place_ref = s32[4]{0:T(128)} fusion(s32[1]{0:T(128)} %bitcast.8, s32[1]{0:T(128)} %bitcast.7, s32[1]{0:T(128)} %bitcast.6, s32[1]{0:T(128)} %bitcast.5), kind=kLoop, calls=%fused_computation | loop fusion | flops 12 | bytes 32 | tf_op jit(solution)/shard_map/stack | solution.py:387
  4.9 0.0 copy-start.6
  4.9 4.2 %prepare.1 = (s32[88,128]{1,0:T(8,128)}, s32[705]{0:T(1024)}, s32[8,128]{1,0:T(8,128)}, bf16[128,256]{1,0:T(8,128)(2,1)}, bf16[128,128]{1,0:T(8,128)(2,1)}, /*index=5*/bf16[128,128]{1,0:T(8,128)(2,1)}, f32[72,128]{1,0:T(8,128)}) custom-call(s32[128]{0:T(128)} %refs_0_.2, s32[128,128]{1,0:T(8,128)} %refs_1_.1, bf16[6,80]{1,0:T(8,128)(2,1)} %bitcast.10, ...), custom_call_target="tpu_custom_call" | custom-call | tf_op jit(solution)/shard_map/prepare/pallas_call | solution.py:162
  9.1 0.0 copy-start.7
  9.1 0.0 collective-permute-done.1.refs_2_
  9.1 0.0 collective-permute-done.refs_1_
  9.1 2.8 %collective-permute-done.2.refs_3_ = bf16[24,2048]{1,0:T(8,128)(2,1)S(1)} collective-permute-done((bf16[24,2048]{1,0:T(8,128)(2,1)}, bf16[24,2048]{1,0:T(8,128)(2,1)S(1)}, u32[]{:S(2)}, u32[]{:S(2)}) %collective-permute-start.2) | collective-permute-done | bytes 98336 | tf_op jit(solution)/shard_map/ppermute | solution.py:382
  12.0 0.0 copy-done
  12.0 0.0 copy-done.6
  12.0 0.0 copy-done.7
  12.0 0.0 copy-start.9
  12.0 0.7 %copy-done.9 = s32[8,128]{1,0:T(8,128)S(1)} copy-done((s32[8,128]{1,0:T(8,128)S(1)}, s32[8,128]{1,0:T(8,128)}, u32[]{:S(2)}) %copy-start.9) | copy-done | bytes 4120
  12.7 0.0 copy-start.1
  12.7 0.0 copy-start.2
  12.7 0.0 copy-start.3
  12.7 0.0 copy-start.4
  12.7 0.0 copy-start.5
  12.7 1.8 %select_points.1 = (bf16[2048,128]{1,0:T(8,128)(2,1)S(1)}, bf16[1024,128]{1,0:T(8,128)(2,1)S(1)}) custom-call(bf16[24,2048]{1,0:T(8,128)(2,1)S(1)} %copy-done, bf16[24,2048]{1,0:T(8,128)(2,1)S(1)} %collective-permute-done.refs_1_, bf16[24,2048]{1,0:T(8,128)(2,1)S(1)} %collective-permute-done.1.refs_2_, bf16[24,2048]{1,0:T(8,128)(2,1)S(1)} %collective-permute-done.2.refs_3_, ...), custom_call_target="tpu_custom_call" | custom-call | tf_op jit(solution)/shard_map/select_points/pallas_call | solution.py:220
  14.5 1.9 %collective-permute-start.3 = (bf16[1024,128]{1,0:T(8,128)(2,1)S(1)}, bf16[1024,128]{1,0:T(8,128)(2,1)S(1)}, u32[]{:S(2)}, u32[]{:S(2)}) collective-permute-start(bf16[1024,128]{1,0:T(8,128)(2,1)S(1)} %get-tuple-element.18), channel_id=1, source_target_pairs={{0,4},{2,6},{4,8},{5,1},{6,10},{7,3},{8,12},{9,5},{10,14},{11,7},{... | collective-permute-start | bytes 786440 | tf_op jit(solution)/shard_map/ppermute | solution.py:399
  16.4 6.7 %collective-permute-done.3.other_ref = bf16[1024,128]{1,0:T(8,128)(2,1)S(1)} collective-permute-done((bf16[1024,128]{1,0:T(8,128)(2,1)S(1)}, bf16[1024,128]{1,0:T(8,128)(2,1)S(1)}, u32[]{:S(2)}, u32[]{:S(2)}) %collective-permute-start.3) | collective-permute-done | bytes 262176 | tf_op jit(solution)/shard_map/ppermute | solution.py:399
  23.1 0.0 copy-start.8
  23.1 0.0 copy-done.1
  23.1 0.0 copy-done.2
  23.1 0.0 copy-done.3
  23.1 0.0 copy-done.4
  23.1 0.0 copy-done.5
  23.1 0.7 %copy-done.8 = s32[705]{0:T(1024)S(1)} copy-done((s32[705]{0:T(1024)S(1)}, s32[705]{0:T(1024)}, u32[]{:S(2)}) %copy-start.8) | copy-done | bytes 2844
  23.8 9.7 %encode.1 = (f32[24,128]{1,0:T(8,128)S(1)}, f32[24,128]{1,0:T(8,128)S(1)}) custom-call(bf16[2048,128]{1,0:T(8,128)(2,1)S(1)} %get-tuple-element.17.own_ref, bf16[1024,128]{1,0:T(8,128)(2,1)S(1)} %collective-permute-done.3.other_ref, s32[88,128]{1,0:T(8,128)S(1)} %copy-done.2, s32[705]{0:T(1024)S(1)} %copy-done.8, s32[4]{0:T(128)S(1)} %copy-done.7, ...), custom_call_target="tpu_custom_call" | custom-call | tf_op jit(solution)/shard_map/encode/pallas_call | solution.py:336
  33.4 0.1 collective-permute-start.4
  33.5 3.7 %collective-permute-done.4 = f32[24,128]{1,0:T(8,128)S(1)} collective-permute-done((f32[24,128]{1,0:T(8,128)S(1)}, f32[24,128]{1,0:T(8,128)S(1)}, u32[]{:S(2)}, u32[]{:S(2)}) %collective-permute-start.4) | collective-permute-done | bytes 12320 | tf_op jit(solution)/shard_map/ppermute | solution.py:401
  37.2 0.6 %add.12 = f32[24,128]{1,0:T(8,128)} add(f32[24,128]{1,0:T(8,128)S(1)} %get-tuple-element.25, f32[24,128]{1,0:T(8,128)S(1)} %collective-permute-done.4) | non-fusion elementwise | flops 3072 | bytes 36864 | tf_op jit(solution)/shard_map/add | solution.py:401
Async XLA Ops:
  0.0 9.1 %collective-permute-start.1 = (bf16[24,2048]{1,0:T(8,128)(2,1)}, bf16[24,2048]{1,0:T(8,128)(2,1)S(1)}, u32[]{:S(2)}, u32[]{:S(2)}) collective-permute-start(bf16[24,2048]{1,0:T(8,128)(2,1)} %refs_0_.3), channel_id=1, source_target_pairs={{0,2},{1,3},{2,0},{3,1},{4,6},{5,7},{6,4},{7,5},{8,10},{9,11},{10,... | collective-permute-start | bytes 294920 | tf_op jit(solution)/shard_map/ppermute | solution.py:382
  0.3 8.8 %collective-permute-start = (bf16[24,2048]{1,0:T(8,128)(2,1)}, bf16[24,2048]{1,0:T(8,128)(2,1)S(1)}, u32[]{:S(2)}, u32[]{:S(2)}) collective-permute-start(bf16[24,2048]{1,0:T(8,128)(2,1)} %refs_0_.3), channel_id=1, source_target_pairs={{0,1},{1,0},{2,3},{3,2},{4,5},{5,4},{6,7},{7,6},{8,9},{9,8},{10,11... | collective-permute-start | bytes 294920 | tf_op jit(solution)/shard_map/ppermute | solution.py:382
  1.9 10.1 %collective-permute-start.2 = (bf16[24,2048]{1,0:T(8,128)(2,1)}, bf16[24,2048]{1,0:T(8,128)(2,1)S(1)}, u32[]{:S(2)}, u32[]{:S(2)}) collective-permute-start(bf16[24,2048]{1,0:T(8,128)(2,1)} %refs_0_.3), channel_id=1, source_target_pairs={{0,3},{1,2},{2,1},{3,0},{4,7},{5,6},{6,5},{7,4},{8,11},{9,10},{10,... | collective-permute-start | bytes 294920 | tf_op jit(solution)/shard_map/ppermute | solution.py:382
  3.5 0.7 %copy-start.10 = (s32[2,1]{0,1:T(1,128)S(1)}, s32[2,1]{0,1:T(1,128)}, u32[]{:S(2)}) copy-start(s32[2,1]{0,1:T(1,128)} %param.16) | copy-start | bytes 28
  3.5 8.5 %copy-start = (bf16[24,2048]{1,0:T(8,128)(2,1)S(1)}, bf16[24,2048]{1,0:T(8,128)(2,1)}, u32[]{:S(2)}) copy-start(bf16[24,2048]{1,0:T(8,128)(2,1)} %refs_0_.3) | copy-start | bytes 294916
  4.9 7.1 %copy-start.6 = (bf16[3,2048]{1,0:T(4,128)(2,1)S(1)}, bf16[3,2048]{1,0:T(4,128)(2,1)}, u32[]{:S(2)}) copy-start(bf16[3,2048]{1,0:T(4,128)(2,1)} %refs_4_.1) | copy-start | bytes 36868
  9.1 2.9 %copy-start.7 = (s32[4]{0:T(128)S(1)}, s32[4]{0:T(128)}, u32[]{:S(2)}) copy-start(s32[4]{0:T(128)} %pad_add_fusion.refs_10_.refs_7_.place_ref) | copy-start | bytes 52
  12.0 0.7 %copy-start.9 = (s32[8,128]{1,0:T(8,128)S(1)}, s32[8,128]{1,0:T(8,128)}, u32[]{:S(2)}) copy-start(s32[8,128]{1,0:T(8,128)} %get-tuple-element.16.refs_5_) | copy-start | bytes 12292
  12.7 10.4 %copy-start.1 = (bf16[128,256]{1,0:T(8,128)(2,1)S(1)}, bf16[128,256]{1,0:T(8,128)(2,1)}, u32[]{:S(2)}) copy-start(bf16[128,256]{1,0:T(8,128)(2,1)} %get-tuple-element.21.table_w) | copy-start | bytes 196612
  12.7 10.4 %copy-start.2 = (s32[88,128]{1,0:T(8,128)S(1)}, s32[88,128]{1,0:T(8,128)}, u32[]{:S(2)}) copy-start(s32[88,128]{1,0:T(8,128)} %get-tuple-element.19.rows_ref) | copy-start | bytes 135172
  12.7 10.4 %copy-start.3 = (f32[72,128]{1,0:T(8,128)S(1)}, f32[72,128]{1,0:T(8,128)}, u32[]{:S(2)}) copy-start(f32[72,128]{1,0:T(8,128)} %get-tuple-element.24.node_pre) | copy-start | bytes 110596
  12.7 10.4 %copy-start.4 = (bf16[128,128]{1,0:T(8,128)(2,1)S(1)}, bf16[128,128]{1,0:T(8,128)(2,1)}, u32[]{:S(2)}) copy-start(bf16[128,128]{1,0:T(8,128)(2,1)} %get-tuple-element.22.hidden_w) | copy-start | bytes 98308
  12.7 10.4 %copy-start.5 = (bf16[128,128]{1,0:T(8,128)(2,1)S(1)}, bf16[128,128]{1,0:T(8,128)(2,1)}, u32[]{:S(2)}) copy-start(bf16[128,128]{1,0:T(8,128)(2,1)} %get-tuple-element.23.out_w) | copy-start | bytes 98308
  14.5 8.6 %collective-permute-start.3 = (bf16[1024,128]{1,0:T(8,128)(2,1)S(1)}, bf16[1024,128]{1,0:T(8,128)(2,1)S(1)}, u32[]{:S(2)}, u32[]{:S(2)}) collective-permute-start(bf16[1024,128]{1,0:T(8,128)(2,1)S(1)} %get-tuple-element.18), channel_id=1, source_target_pairs={{0,4},{2,6},{4,8},{5,1},{6,10},{7,3},{8,12},{9,5},{10,14},{11,7},{... | collective-permute-start | bytes 786440 | tf_op jit(solution)/shard_map/ppermute | solution.py:399
  23.1 0.7 %copy-start.8 = (s32[705]{0:T(1024)S(1)}, s32[705]{0:T(1024)}, u32[]{:S(2)}) copy-start(s32[705]{0:T(1024)} %get-tuple-element.20.spot_ref) | copy-start | bytes 8464
  33.4 3.8 %collective-permute-start.4 = (f32[24,128]{1,0:T(8,128)S(1)}, f32[24,128]{1,0:T(8,128)S(1)}, u32[]{:S(2)}, u32[]{:S(2)}) collective-permute-start(f32[24,128]{1,0:T(8,128)S(1)} %get-tuple-element.26), channel_id=1, source_target_pairs={{0,1},{1,0},{2,3},{3,2},{4,5},{5,4},{6,7},{7,6},{8,9},{9,8},{10,11... | collective-permute-start | bytes 36872 | tf_op jit(solution)/shard_map/ppermute | solution.py:401

commit v7 on v6

--- a/solution.py
+++ b/solution.py
@@ -27,7 +27,7 @@
 
 def prepare(
     neighbours, neighbour_count, geom_weight, feat_weight, bias_one, hidden_weight, bias_two,
-    out_weight, bias_three, place, groups, points, send_rows, depth,
+    out_weight, bias_three, groups, points, send_rows, depth,
 ):
     per_slab, slots = neighbours.shape
     send = send_rows.shape[1]
@@ -54,10 +54,9 @@
     listed = send // LANES
 
     def kernel(*refs):
-        place_ref = refs[len(given)]
-        rows_ref, list_ref, sent_ref, table_w, hidden_w, out_w, node_pre = refs[len(given) + 1 :][:7]
-        held = refs[len(given) + 8 :][: len(given)]
-        wide, square, spread, arrived = refs[2 * len(given) + 8 :]
+        rows_ref, spot_ref, sent_ref, table_w, hidden_w, out_w, node_pre = refs[len(given) :][:7]
+        held = refs[len(given) + 7 :][: len(given)]
+        wide, square, spread, arrived = refs[2 * len(given) + 7 :]
         copies = [
             pltpu.make_async_copy(source, target, arrived.at[at])
             for at, (source, target) in enumerate(zip(refs, held))
@@ -67,16 +66,20 @@
         for copy in copies:
             copy.wait()
         count_ref, nbr_ref, geom_ref, feat_ref, one_ref, hidden_ref, two_ref, out_ref, three_ref, send_ref = held
-        member = place_ref[0]
-        first_id = place_ref[2]
-        start = place_ref[3]
+        member = lax.axis_index("chan")
+        start = (member % ZD) * nodes
+        first_id = lax.axis_index("slab") * per_slab + start
         lane = lax.broadcasted_iota(jnp.int32, (1, LANES), 1)
 
         slot = lax.broadcasted_iota(jnp.int32, (1, slots), 1)
         rows_ref[...] = jnp.full((tall, slots), nothing, jnp.int32)
         together = 8
 
-        def some_nodes(step, at):
+        chunk = BLOCK * lax.broadcasted_iota(jnp.int32, (8, LANES), 0)
+        chunk = chunk + lax.broadcasted_iota(jnp.int32, (8, LANES), 1)
+
+        def some_nodes(step, carry):
+            at, node_of = carry
             first = step * together
             counts = [count_ref[start + first + i] for i in range(together)]
             spots = []
@@ -94,20 +97,15 @@
                 kept = slot < (spots[i] % per_node) * CHUNK
                 rows_ref[pl.ds(line, 1), :] = jnp.where(kept, rows_ref[pl.ds(line, 1), :], turned[i])
                 rows_ref[pl.ds(line + 1, 1), :] = turned[i]
-                for piece in range(per_node):
-                    list_ref[spots[i] + piece] = first + i
-            return at
-
-        used = lax.fori_loop(0, nodes // together, some_nodes, 0)
-
-        def fill(step, carry):
-            for i in range(8):
-                list_ref[used + 8 * step + i] = nodes
-            return carry
-
-        lax.fori_loop(0, 3 * BLOCK // 8, fill, 0)
-        list_ref[most + 3 * BLOCK] = (used + 2 * BLOCK - 1) // (2 * BLOCK)
-        side = place_ref[1]
+            for end in spots[1:] + [at]:
+                node_of = node_of + (chunk >= end).astype(jnp.int32)
+            return at, node_of
+
+        none = jnp.zeros((8, LANES), jnp.int32)
+        used, node_of = lax.fori_loop(0, nodes // together, some_nodes, (jnp.int32(0), none))
+        spot_ref[0:8, :] = node_of
+        spot_ref[8:16, :] = none + (used + BLOCK - 1) // BLOCK
+        side = 1 - member % ZD
         chosen = send_ref[pl.ds(side, 1), :]
         for line in range(listed):
             sent_ref[line : line + 1, :] = chosen[:, line * LANES : (line + 1) * LANES]
@@ -163,15 +161,15 @@
         kernel,
         out_shape=(
             jax.ShapeDtypeStruct((tall, slots), jnp.int32),
-            jax.ShapeDtypeStruct((most + 3 * BLOCK + 1,), jnp.int32),
+            jax.ShapeDtypeStruct((16, LANES), jnp.int32),
             jax.ShapeDtypeStruct((listed, LANES), jnp.int32),
             jax.ShapeDtypeStruct((LANES, 2 * LANES), jnp.bfloat16),
             jax.ShapeDtypeStruct((LANES, LANES), jnp.bfloat16),
             jax.ShapeDtypeStruct((LANES, LANES), jnp.bfloat16),
             jax.ShapeDtypeStruct((nodes + 8, LANES), jnp.float32),
         ),
-        in_specs=[HBM] * len(given) + [SMEM],
-        out_specs=(VMEM, SMEM, VMEM) + (VMEM,) * 4,
+        in_specs=[HBM] * len(given),
+        out_specs=(VMEM,) * 7,
         scratch_shapes=[pltpu.SMEM(neighbour_count.shape, jnp.int32)]
         + [pltpu.VMEM(array.shape, array.dtype) for array in given[1:]]
         + [
@@ -181,11 +179,11 @@
             pltpu.SemaphoreType.DMA((len(given),)),
         ],
         name="prepare",
-    )(*given, place)
+    )(*given)
     return out[:2], out[2], out[3:]
 
 
-def select_points(blocks, coords, send_rows, send_count, place):
+def select_points(blocks, coords, send_rows, send_count):
     groups = len(blocks)
     chans, points = blocks[0].shape
     width = LANES // groups
@@ -194,10 +192,10 @@
 
     def kernel(*refs):
         block_refs = refs[:groups]
-        coords_ref, rows_ref, count_ref, place_ref = refs[groups : groups + 4]
-        own_ref, sent_ref, stack, table, picked = refs[groups + 4 :]
-        member = place_ref[0]
-        side = place_ref[1]
+        coords_ref, rows_ref, count_ref = refs[groups : groups + 3]
+        own_ref, sent_ref, stack, table, picked = refs[groups + 3 :]
+        member = lax.axis_index("chan")
+        side = 1 - member % ZD
         for step in range(groups):
             base = pl.multiple_of((member ^ step) * width, width)
             empty = jnp.zeros((width - chans, points), jnp.bfloat16)
@@ -223,7 +221,7 @@
             jax.ShapeDtypeStruct((points, LANES), jnp.bfloat16),
             jax.ShapeDtypeStruct((send, LANES), jnp.bfloat16),
         ),
-        in_specs=[VMEM] * (groups + 1) + [SMEM] * 3,
+        in_specs=[VMEM] * (groups + 1) + [SMEM] * 2,
         out_specs=(VMEM, VMEM),
         scratch_shapes=[
             pltpu.VMEM((LANES, points), jnp.bfloat16),
@@ -232,10 +230,10 @@
         ],
         compiler_params=pltpu.CompilerParams(vmem_limit_bytes=12 << 20),
         name="select_points",
-    )(*blocks, coords, send_rows, send_count, place)
-
-
-def encode(own, other, plan, place, weights, chans, width):
+    )(*blocks, coords, send_rows, send_count)
+
+
+def encode(own, other, plan, weights, chans, width):
     rows, spots = plan
     table_weight, hidden_weight, out_weight, node_part = weights
     points = own.shape[0]
@@ -247,11 +245,11 @@
     lines = pairs // slots
 
     def kernel(
-        own_ref, other_ref, rows_ref, spot_ref, place_ref, table_w, hidden_w, out_w, node_pre,
-        keep_ref, give_ref, table, picked_a, picked_b, names_a, names_b, acc, turned, arrived,
+        own_ref, other_ref, rows_ref, spots_ref, table_w, hidden_w, out_w, node_pre,
+        keep_ref, give_ref, table, picked, names_a, names_b, spot_ref, acc, turned,
+        arrived,
     ):
-        parity = place_ref[1]
-        steps = spot_ref[spots.shape[0] - 1]
+        parity = 1 - lax.axis_index("chan") % ZD
 
         def fetch(block, names, which):
             source = rows_ref.at[pl.ds(pl.multiple_of(block * lines, lines), lines), :]
@@ -259,6 +257,8 @@
 
         fetch(0, names_a, 0).start()
         fetch(1, names_b, 1).start()
+        of_blocks = pltpu.make_async_copy(spots_ref, spot_ref, arrived.at[2])
+        of_blocks.start()
 
         def fill(source, start, count):
             step = 256
@@ -273,20 +273,17 @@
         table[pl.ds(2 * total_rows, 8), :] = jnp.zeros((8, LANES), jnp.float32)
         acc[...] = jnp.zeros((nodes + 8, 8, LANES), jnp.float32)
 
-        def gather(names, picked):
+        def one_block(block, names):
             for base in range(0, pairs, CHUNK):
                 got = [
                     table[pl.ds(names[at // slots, at % slots], 2), :] for at in range(base, base + CHUNK)
                 ]
                 for j in range(CHUNK):
                     picked[2 * (base + j) : 2 * (base + j) + 2, :] = got[j]
-
-        def compute(block, picked):
-            of_block = spot_ref.at[pl.ds(block * BLOCK, BLOCK)]
             step = 8
             for group in range(BLOCK // step):
                 base = group * step * CHUNK
-                here = [of_block[group * step + i] for i in range(step)]
+                here = [spot_ref[block, group * step + i] for i in range(step)]
                 offset = jnp.concatenate(
                     [jnp.broadcast_to(node_pre[pl.ds(spot, 1), :], (CHUNK, LANES)) for spot in here],
                     axis=0,
@@ -304,23 +301,23 @@
                         part = part + product[i * CHUNK + j : i * CHUNK + j + 8]
                     acc[spot] = acc[spot] + part
 
-        fetch(0, names_a, 0).wait()
-        gather(names_a, picked_a)
-        fetch(2, names_a, 0).start()
-
         def one_step(index, carry):
             block = 2 * index
+            fetch(block, names_a, 0).wait()
+            one_block(block, names_a)
+            fetch(block + 2, names_a, 0).start()
             fetch(block + 1, names_b, 1).wait()
-            gather(names_b, picked_b)
-            compute(block, picked_a)
+
+            @pl.when(block + 1 < spot_ref[spots.shape[0] - 1, 0])
+            def _():
+                one_block(block + 1, names_b)
+
             fetch(block + 3, names_b, 1).start()
-            fetch(block + 2, names_a, 0).wait()
-            gather(names_a, picked_a)
-            compute(block + 1, picked_b)
-            fetch(block + 4, names_a, 0).start()
             return carry
 
-        lax.fori_loop(0, steps, one_step, 0)
+        of_blocks.wait()
+        blocks = spot_ref[spots.shape[0] - 1, 0]
+        lax.fori_loop(0, (blocks + 1) // 2, one_step, 0)
         fetch(0, names_a, 0).wait()
         fetch(1, names_b, 1).wait()
         sums = jnp.sum(acc[0:nodes], axis=1)
@@ -336,21 +333,21 @@
     return pl.pallas_call(
         kernel,
         out_shape=(piece, piece),
-        in_specs=[VMEM, VMEM, VMEM, SMEM, SMEM] + [VMEM] * 4,
+        in_specs=[VMEM] * 8,
         out_specs=(VMEM, VMEM),
         scratch_shapes=[
             pltpu.VMEM((2 * total_rows + 8, LANES), jnp.float32),
             pltpu.VMEM((2 * pairs, LANES), jnp.float32),
-            pltpu.VMEM((2 * pairs, LANES), jnp.float32),
             pltpu.SMEM((lines, slots), jnp.int32),
             pltpu.SMEM((lines, slots), jnp.int32),
+            pltpu.SMEM(spots.shape, jnp.int32),
             pltpu.VMEM((nodes + 8, 8, LANES), jnp.float32),
             pltpu.VMEM((LANES, ZD * nodes), jnp.float32),
-            pltpu.SemaphoreType.DMA((2,)),
+            pltpu.SemaphoreType.DMA((3,)),
         ],
         compiler_params=pltpu.CompilerParams(vmem_limit_bytes=16 << 20),
         name="encode",
-    )(own, other, rows, spots, place, table_weight, hidden_weight, out_weight, node_part)
+    )(own, other, rows, spots, table_weight, hidden_weight, out_weight, node_part)
 
 
 def shards(
@@ -370,26 +367,18 @@
 ):
     groups = lax.axis_size("chan")
     slabs = lax.axis_size("slab")
-    member = lax.axis_index("chan")
-    slab_id = lax.axis_index("slab")
     chans, points = features.shape
-    per_slab = neighbours.shape[0]
-    nodes = per_slab // ZD
     width = LANES // groups
 
     blocks = [features]
     for step in range(1, groups):
         blocks.append(lax.ppermute(features, "chan", [(i, i ^ step) for i in range(groups)]))
 
-    plane = member % 2
-    start = plane * nodes
-    upper = 1 - plane
-    place = jnp.stack([member, upper, slab_id * per_slab + start, start]).astype(jnp.int32)
     plan, sent_rows, weights = prepare(
         neighbours, neighbour_count, geom_weight, feat_weight, bias_one, hidden_weight, bias_two,
-        out_weight, bias_three, place, groups, points, send_rows, ZD * slabs,
+        out_weight, bias_three, groups, points, send_rows, ZD * slabs,
     )
-    own, sent = select_points(blocks, coords, sent_rows, send_count, place)
+    own, sent = select_points(blocks, coords, sent_rows, send_count)
     moves = []
     for slab in range(slabs):
         for who in range(groups):
@@ -397,7 +386,7 @@
             if 0 <= target < slabs:
                 moves.append((slab * groups + who, target * groups + who))
     other = lax.ppermute(sent, ("slab", "chan"), moves)
-    keep, give = encode(own, other, plan, place, weights, chans, width)
+    keep, give = encode(own, other, plan, weights, chans, width)
     return keep + lax.ppermute(give, "chan", [(i, i ^ 1) for i in range(groups)])
 
 

time: 38.1 us -> 37.6 us (0.987)
  waiting for transfers between devices: 13.2 us -> 14.9 us
  Pallas kernels: 15.7 us -> 14.7 us
  other arithmetic: 1.26 us -> 0.6 us
  local copies, waits for them, and re-layouts: 2.1 us -> 1.45 us
    ppermute x3, waiting for transfers between devices: 2.83 us -> 4.61 us  [shards(): lax.ppermute(features, 'chan', [(i, i ^ step) for i in range(groups)])]
    pallas_call x1, Pallas kernels: 4.2 us -> 3.1 us  [prepare(): pl.pallas_call(kernel, out_shape=(jax.ShapeDtypeStruct((tall, slots), jnp...]
    another operation x1 -> x0, other arithmetic: 0.66 us -> none  [shards(): jnp.stack([member, upper, slab_id * per_slab + start, start])]
    unnamed x23 -> x19, local copies, waits for them, and re-layouts: 2.1 us -> 1.45 us
  transfers between devices with their start and end apart: 5 -> 5, of which waited for: 3 -> 4; matrix products, arithmetic and copies ran while one was open for 2% -> 2% of each run, Pallas kernels for 11% -> 8%
where the time goes in v7:
time: 37.6 us; the launch traced here: 37.3 us
  waiting for transfers between devices  14.9 us (40%)
  Pallas kernels  14.7 us (39%)
  starting transfers between devices  5.48 us (15%)
  local copies, waits for them, and re-layouts  1.45 us (4%)
  other arithmetic  0.6 us (2%)
    pallas_call x1, Pallas kernels, encode(): pl.pallas_call(kernel, out_shape=(piece, piece), in_specs=[VMEM] * 8, out...  9.83 us
    ppermute x1, waiting for transfers between devices, shards(): other = lax.ppermute(sent, ('slab', 'chan'), moves)  6.66 us
    ppermute x3, waiting for transfers between devices, shards(): lax.ppermute(features, 'chan', [(i, i ^ step) for i in range(groups)])  4.61 us
    ppermute x1, waiting for transfers between devices, shards(): lax.ppermute(give, 'chan', [(i, i ^ 1) for i in range(groups)])  3.68 us
    ppermute x3, starting transfers between devices, shards(): lax.ppermute(features, 'chan', [(i, i ^ step) for i in range(groups)])  3.49 us
    pallas_call x1, Pallas kernels, prepare(): pl.pallas_call(kernel, out_shape=(jax.ShapeDtypeStruct((tall, slots), jnp...  3.1 us
    ppermute x1, starting transfers between devices, shards(): other = lax.ppermute(sent, ('slab', 'chan'), moves)  1.92 us
    pallas_call x1, Pallas kernels, select_points(): pl.pallas_call(kernel, out_shape=(jax.ShapeDtypeStruct((points, LANES), j...  1.81 us
  transfers between devices with their start and end apart: 5, of which 4 were waited for; matrix products, arithmetic and copies ran while one was open for 2% of the time, Pallas kernels for 8%

profile of v7, /device:TPU:20, one launch (start us, length us, event | category | flops | bytes accessed | tf_op | source)
XLA Modules:
  0.0 37.3 jit_solution(4104180319796462718)
XLA Ops:
  0.0 0.0 copy-start
  0.0 0.3 collective-permute-start.1
  0.3 1.6 %collective-permute-start = (bf16[24,2048]{1,0:T(8,128)(2,1)}, bf16[24,2048]{1,0:T(8,128)(2,1)S(1)}, u32[]{:S(2)}, u32[]{:S(2)}) collective-permute-start(bf16[24,2048]{1,0:T(8,128)(2,1)} %refs_0_.3), channel_id=1, source_target_pairs={{0,1},{1,0},{2,3},{3,2},{4,5},{5,4},{6,7},{7,6},{8,9},{9,8},{10,11... | collective-permute-start | bytes 294920 | tf_op jit(solution)/shard_map/ppermute | solution.py:375
  1.9 1.6 %collective-permute-start.2 = (bf16[24,2048]{1,0:T(8,128)(2,1)}, bf16[24,2048]{1,0:T(8,128)(2,1)S(1)}, u32[]{:S(2)}, u32[]{:S(2)}) collective-permute-start(bf16[24,2048]{1,0:T(8,128)(2,1)} %refs_0_.3), channel_id=1, source_target_pairs={{0,3},{1,2},{2,1},{3,0},{4,7},{5,6},{6,5},{7,4},{8,11},{9,10},{10,... | collective-permute-start | bytes 294920 | tf_op jit(solution)/shard_map/ppermute | solution.py:375
  3.5 0.7 %copy.14.refs_6_ = s32[2,1]{1,0:T(2,128)S(1)} copy(s32[2,1]{0,1:T(1,128)} %param.16) | data formatting | bytes 16 | tf_op args[3]
  4.2 0.0 copy-start.6
  4.2 3.1 %prepare.1 = (s32[88,128]{1,0:T(8,128)}, s32[16,128]{1,0:T(8,128)}, s32[8,128]{1,0:T(8,128)}, bf16[128,256]{1,0:T(8,128)(2,1)}, bf16[128,128]{1,0:T(8,128)(2,1)}...) custom-call(s32[128]{0:T(128)} %refs_0_.2, s32[128,128]{1,0:T(8,128)} %refs_1_.1, bf16[6,80]{1,0:T(8,128)(2,1)} %bitcast.6, ...), custom_call_target="tpu_custom_call" | custom-call | tf_op jit(solution)/shard_map/prepare/pallas_call | solution.py:160
  7.3 0.0 collective-permute-done.1.refs_2_
  7.4 0.1 collective-permute-done.refs_1_
  7.5 4.5 %collective-permute-done.2.refs_3_ = bf16[24,2048]{1,0:T(8,128)(2,1)S(1)} collective-permute-done((bf16[24,2048]{1,0:T(8,128)(2,1)}, bf16[24,2048]{1,0:T(8,128)(2,1)S(1)}, u32[]{:S(2)}, u32[]{:S(2)}) %collective-permute-start.2) | collective-permute-done | bytes 98336 | tf_op jit(solution)/shard_map/ppermute | solution.py:375
  12.0 0.0 copy-done
  12.0 0.0 copy-done.6
  12.0 0.0 copy-start.8
  12.0 0.7 %copy-done.8 = s32[8,128]{1,0:T(8,128)S(1)} copy-done((s32[8,128]{1,0:T(8,128)S(1)}, s32[8,128]{1,0:T(8,128)}, u32[]{:S(2)}) %copy-start.8) | copy-done | bytes 4120
  12.6 0.0 copy-start.1
  12.7 0.0 copy-start.2
  12.7 0.0 copy-start.3
  12.7 0.0 copy-start.4
  12.7 0.0 copy-start.5
  12.7 1.8 %select_points.1 = (bf16[2048,128]{1,0:T(8,128)(2,1)S(1)}, bf16[1024,128]{1,0:T(8,128)(2,1)S(1)}) custom-call(bf16[24,2048]{1,0:T(8,128)(2,1)S(1)} %copy-done, bf16[24,2048]{1,0:T(8,128)(2,1)S(1)} %collective-permute-done.refs_1_, bf16[24,2048]{1,0:T(8,128)(2,1)S(1)} %collective-permute-done.1.refs_2_, bf16[24,2048]{1,0:T(8,128)(2,1)S(1)} %collective-permute-done.2.refs_3_, ...), custom_call_target="tpu_custom_call" | custom-call | tf_op jit(solution)/shard_map/select_points/pallas_call | solution.py:218
  14.5 0.0 copy-start.7
  14.5 1.9 %collective-permute-start.3 = (bf16[1024,128]{1,0:T(8,128)(2,1)S(1)}, bf16[1024,128]{1,0:T(8,128)(2,1)S(1)}, u32[]{:S(2)}, u32[]{:S(2)}) collective-permute-start(bf16[1024,128]{1,0:T(8,128)(2,1)S(1)} %get-tuple-element.18), channel_id=1, source_target_pairs={{0,4},{2,6},{4,8},{5,1},{6,10},{7,3},{8,12},{9,5},{10,14},{11,7},{... | collective-permute-start | bytes 786440 | tf_op jit(solution)/shard_map/ppermute | solution.py:388
  16.4 6.7 %collective-permute-done.3.other_ref = bf16[1024,128]{1,0:T(8,128)(2,1)S(1)} collective-permute-done((bf16[1024,128]{1,0:T(8,128)(2,1)S(1)}, bf16[1024,128]{1,0:T(8,128)(2,1)S(1)}, u32[]{:S(2)}, u32[]{:S(2)}) %collective-permute-start.3) | collective-permute-done | bytes 262176 | tf_op jit(solution)/shard_map/ppermute | solution.py:388
  23.1 0.0 copy-done.1
  23.1 0.0 copy-done.2
  23.1 0.0 copy-done.3
  23.1 0.0 copy-done.4
  23.1 0.0 copy-done.5
  23.1 0.0 copy-done.7
  23.1 9.8 %encode.1 = (f32[24,128]{1,0:T(8,128)S(1)}, f32[24,128]{1,0:T(8,128)S(1)}) custom-call(bf16[2048,128]{1,0:T(8,128)(2,1)S(1)} %get-tuple-element.17.own_ref, bf16[1024,128]{1,0:T(8,128)(2,1)S(1)} %collective-permute-done.3.other_ref, s32[88,128]{1,0:T(8,128)S(1)} %copy-done.2, s32[16,128]{1,0:T(8,128)S(1)} %copy-done.7, bf16[128,256]{1,0:T(8,128)(2,1)S(1)} %copy-done.1, ...), custom_call_target="tpu_custom_call" | custom-call | tf_op jit(solution)/shard_map/encode/pallas_call | solution.py:333
  33.0 0.1 collective-permute-start.4
  33.0 3.7 %collective-permute-done.4 = f32[24,128]{1,0:T(8,128)S(1)} collective-permute-done((f32[24,128]{1,0:T(8,128)S(1)}, f32[24,128]{1,0:T(8,128)S(1)}, u32[]{:S(2)}, u32[]{:S(2)}) %collective-permute-start.4) | collective-permute-done | bytes 12320 | tf_op jit(solution)/shard_map/ppermute | solution.py:390
  36.7 0.6 %add.3 = f32[24,128]{1,0:T(8,128)} add(f32[24,128]{1,0:T(8,128)S(1)} %get-tuple-element.25, f32[24,128]{1,0:T(8,128)S(1)} %collective-permute-done.4) | non-fusion elementwise | flops 3072 | bytes 36864 | tf_op jit(solution)/shard_map/add | solution.py:390
Async XLA Ops:
  0.0 12.0 %copy-start = (bf16[24,2048]{1,0:T(8,128)(2,1)S(1)}, bf16[24,2048]{1,0:T(8,128)(2,1)}, u32[]{:S(2)}) copy-start(bf16[24,2048]{1,0:T(8,128)(2,1)} %refs_0_.3) | copy-start | bytes 294916
  0.0 7.3 %collective-permute-start.1 = (bf16[24,2048]{1,0:T(8,128)(2,1)}, bf16[24,2048]{1,0:T(8,128)(2,1)S(1)}, u32[]{:S(2)}, u32[]{:S(2)}) collective-permute-start(bf16[24,2048]{1,0:T(8,128)(2,1)} %refs_0_.3), channel_id=1, source_target_pairs={{0,2},{1,3},{2,0},{3,1},{4,6},{5,7},{6,4},{7,5},{8,10},{9,11},{10,... | collective-permute-start | bytes 294920 | tf_op jit(solution)/shard_map/ppermute | solution.py:375
  0.3 7.2 %collective-permute-start = (bf16[24,2048]{1,0:T(8,128)(2,1)}, bf16[24,2048]{1,0:T(8,128)(2,1)S(1)}, u32[]{:S(2)}, u32[]{:S(2)}) collective-permute-start(bf16[24,2048]{1,0:T(8,128)(2,1)} %refs_0_.3), channel_id=1, source_target_pairs={{0,1},{1,0},{2,3},{3,2},{4,5},{5,4},{6,7},{7,6},{8,9},{9,8},{10,11... | collective-permute-start | bytes 294920 | tf_op jit(solution)/shard_map/ppermute | solution.py:375
  1.9 10.1 %collective-permute-start.2 = (bf16[24,2048]{1,0:T(8,128)(2,1)}, bf16[24,2048]{1,0:T(8,128)(2,1)S(1)}, u32[]{:S(2)}, u32[]{:S(2)}) collective-permute-start(bf16[24,2048]{1,0:T(8,128)(2,1)} %refs_0_.3), channel_id=1, source_target_pairs={{0,3},{1,2},{2,1},{3,0},{4,7},{5,6},{6,5},{7,4},{8,11},{9,10},{10,... | collective-permute-start | bytes 294920 | tf_op jit(solution)/shard_map/ppermute | solution.py:375
  4.2 7.7 %copy-start.6 = (bf16[3,2048]{1,0:T(4,128)(2,1)S(1)}, bf16[3,2048]{1,0:T(4,128)(2,1)}, u32[]{:S(2)}) copy-start(bf16[3,2048]{1,0:T(4,128)(2,1)} %refs_4_.1) | copy-start | bytes 36868
  12.0 0.7 %copy-start.8 = (s32[8,128]{1,0:T(8,128)S(1)}, s32[8,128]{1,0:T(8,128)}, u32[]{:S(2)}) copy-start(s32[8,128]{1,0:T(8,128)} %get-tuple-element.16.refs_5_) | copy-start | bytes 12292
  12.6 10.4 %copy-start.1 = (bf16[128,256]{1,0:T(8,128)(2,1)S(1)}, bf16[128,256]{1,0:T(8,128)(2,1)}, u32[]{:S(2)}) copy-start(bf16[128,256]{1,0:T(8,128)(2,1)} %get-tuple-element.21.table_w) | copy-start | bytes 196612
  12.7 10.4 %copy-start.2 = (s32[88,128]{1,0:T(8,128)S(1)}, s32[88,128]{1,0:T(8,128)}, u32[]{:S(2)}) copy-start(s32[88,128]{1,0:T(8,128)} %get-tuple-element.19.rows_ref) | copy-start | bytes 135172
  12.7 10.4 %copy-start.3 = (f32[72,128]{1,0:T(8,128)S(1)}, f32[72,128]{1,0:T(8,128)}, u32[]{:S(2)}) copy-start(f32[72,128]{1,0:T(8,128)} %get-tuple-element.24.node_pre) | copy-start | bytes 110596
  12.7 10.4 %copy-start.4 = (bf16[128,128]{1,0:T(8,128)(2,1)S(1)}, bf16[128,128]{1,0:T(8,128)(2,1)}, u32[]{:S(2)}) copy-start(bf16[128,128]{1,0:T(8,128)(2,1)} %get-tuple-element.22.hidden_w) | copy-start | bytes 98308
  12.7 10.5 %copy-start.5 = (bf16[128,128]{1,0:T(8,128)(2,1)S(1)}, bf16[128,128]{1,0:T(8,128)(2,1)}, u32[]{:S(2)}) copy-start(bf16[128,128]{1,0:T(8,128)(2,1)} %get-tuple-element.23.out_w) | copy-start | bytes 98308
  14.5 8.6 %copy-start.7 = (s32[16,128]{1,0:T(8,128)S(1)}, s32[16,128]{1,0:T(8,128)}, u32[]{:S(2)}) copy-start(s32[16,128]{1,0:T(8,128)} %get-tuple-element.20.spots_ref) | copy-start | bytes 24580
  14.5 8.6 %collective-permute-start.3 = (bf16[1024,128]{1,0:T(8,128)(2,1)S(1)}, bf16[1024,128]{1,0:T(8,128)(2,1)S(1)}, u32[]{:S(2)}, u32[]{:S(2)}) collective-permute-start(bf16[1024,128]{1,0:T(8,128)(2,1)S(1)} %get-tuple-element.18), channel_id=1, source_target_pairs={{0,4},{2,6},{4,8},{5,1},{6,10},{7,3},{8,12},{9,5},{10,14},{11,7},{... | collective-permute-start | bytes 786440 | tf_op jit(solution)/shard_map/ppermute | solution.py:388
  33.0 3.8 %collective-permute-start.4 = (f32[24,128]{1,0:T(8,128)S(1)}, f32[24,128]{1,0:T(8,128)S(1)}, u32[]{:S(2)}, u32[]{:S(2)}) collective-permute-start(f32[24,128]{1,0:T(8,128)S(1)} %get-tuple-element.26), channel_id=1, source_target_pairs={{0,1},{1,0},{2,3},{3,2},{4,5},{5,4},{6,7},{7,6},{8,9},{9,8},{10,11... | collective-permute-start | bytes 36872 | tf_op jit(solution)/shard_map/ppermute | solution.py:390

commit v8 on v7

--- a/solution.py
+++ b/solution.py
@@ -4,6 +4,7 @@
 from jax.experimental import pallas as pl
 from jax.experimental.pallas import tpu as pltpu
 from jax.sharding import PartitionSpec as P
+
 
 ZD = 2
 GX = 16
@@ -183,29 +184,38 @@
     return out[:2], out[2], out[3:]
 
 
-def select_points(blocks, coords, send_rows, send_count):
-    groups = len(blocks)
+def select_points(blocks, first_step, coords, sent_rows, send_count, groups, earlier=None):
     chans, points = blocks[0].shape
     width = LANES // groups
-    send = send_rows.shape[0] * LANES
+    send = sent_rows.shape[0] * LANES
     unroll = 16
+    late = earlier is not None
+    extra = (earlier,) if late else (coords,)
 
     def kernel(*refs):
-        block_refs = refs[:groups]
-        coords_ref, rows_ref, count_ref = refs[groups : groups + 3]
-        own_ref, sent_ref, stack, table, picked = refs[groups + 3 :]
+        block_refs = refs[: len(blocks)]
+        extra_ref, list_ref, count_ref, own_ref, sent_ref = refs[len(blocks) :][:5]
+        stack, table, picked, rows_ref, arrived = refs[len(blocks) + 5 :][:5]
+        listed = pltpu.make_async_copy(list_ref, rows_ref, arrived)
+        listed.start()
         member = lax.axis_index("chan")
         side = 1 - member % ZD
+        empty = jnp.zeros((width - chans, points), jnp.bfloat16)
+        known = range(first_step, first_step + len(blocks))
         for step in range(groups):
             base = pl.multiple_of((member ^ step) * width, width)
-            empty = jnp.zeros((width - chans, points), jnp.bfloat16)
-            stack[pl.ds(base, width), :] = jnp.concatenate([block_refs[step][...], empty], axis=0)
-        stack[chans : chans + 3, :] = coords_ref[...]
-        stack[chans + 3 : chans + 4, :] = jnp.ones((1, points), jnp.bfloat16)
+            if step in known:
+                block = jnp.concatenate([block_refs[step - first_step][...], empty], axis=0)
+            else:
+                block = jnp.zeros((width, points), jnp.bfloat16)
+            stack[pl.ds(base, width), :] = block
+        if not late:
+            stack[chans : chans + 3, :] = extra_ref[...]
+            stack[chans + 3 : chans + 4, :] = jnp.ones((1, points), jnp.bfloat16)
         own = stack[...].T
-        own_ref[...] = own
+        own_ref[...] = own + extra_ref[...] if late else own
         table[...] = own.astype(jnp.float32)
-
+        listed.wait()
         for base in range(0, send, unroll):
             rows = [
                 table[pl.ds(rows_ref[at // LANES, at % LANES], 1), :] for at in range(base, base + unroll)
@@ -213,27 +223,37 @@
             for j in range(unroll):
                 picked[base + j : base + j + 1, :] = rows[j]
         slot = lax.broadcasted_iota(jnp.int32, (send, LANES), 0)
-        sent_ref[...] = jnp.where(slot < count_ref[side, 0], picked[...], 0.0).astype(jnp.bfloat16)
+        live = jnp.where(slot < count_ref[0, side], picked[...], 0.0)
+        if late:
+            turned = refs[-1]
+            turned[...] = live.T
+            base = pl.multiple_of((member ^ first_step) * width, width)
+            sent_ref[...] = turned[pl.ds(base, width), :].astype(jnp.bfloat16)
+        else:
+            sent_ref[...] = live.astype(jnp.bfloat16)
 
     return pl.pallas_call(
         kernel,
         out_shape=(
             jax.ShapeDtypeStruct((points, LANES), jnp.bfloat16),
-            jax.ShapeDtypeStruct((send, LANES), jnp.bfloat16),
+            jax.ShapeDtypeStruct((width, send) if late else (send, LANES), jnp.bfloat16),
         ),
-        in_specs=[VMEM] * (groups + 1) + [SMEM] * 2,
+        in_specs=[VMEM] * (len(blocks) + 1) + [HBM, SMEM],
         out_specs=(VMEM, VMEM),
         scratch_shapes=[
             pltpu.VMEM((LANES, points), jnp.bfloat16),
             pltpu.VMEM((points, LANES), jnp.float32),
             pltpu.VMEM((send, LANES), jnp.float32),
-        ],
+            pltpu.SMEM(sent_rows.shape, jnp.int32),
+            pltpu.SemaphoreType.DMA,
+        ]
+        + [pltpu.VMEM((LANES, send), jnp.float32)] * late,
         compiler_params=pltpu.CompilerParams(vmem_limit_bytes=12 << 20),
-        name="select_points",
-    )(*blocks, coords, send_rows, send_count)
-
-
-def encode(own, other, plan, weights, chans, width):
+        name="select_late" if late else "select_points",
+    )(*blocks, *extra, sent_rows, send_count)
+
+
+def encode(own, other, other_late, plan, weights, chans, width, groups):
     rows, spots = plan
     table_weight, hidden_weight, out_weight, node_part = weights
     points = own.shape[0]
@@ -245,9 +265,9 @@
     lines = pairs // slots
 
     def kernel(
-        own_ref, other_ref, rows_ref, spots_ref, table_w, hidden_w, out_w, node_pre,
+        own_ref, other_ref, late_ref, rows_ref, spots_ref, table_w, hidden_w, out_w, node_pre,
         keep_ref, give_ref, table, picked, names_a, names_b, spot_ref, acc, turned,
-        arrived,
+        late, whole, arrived,
     ):
         parity = 1 - lax.axis_index("chan") % ZD
 
@@ -269,7 +289,11 @@
                 table[pl.ds(2 * (start + at) + 1, step, stride=2), :] = both[:, LANES:]
 
         fill(own_ref, 0, points)
-        fill(other_ref, points, send)
+        base = pl.multiple_of((lax.axis_index("chan") ^ (groups - 1)) * width, width)
+        late[...] = jnp.zeros((LANES, send), jnp.bfloat16)
+        late[pl.ds(base, width), :] = late_ref[...]
+        whole[...] = other_ref[...] + late[...].T
+        fill(whole, points, send)
         table[pl.ds(2 * total_rows, 8), :] = jnp.zeros((8, LANES), jnp.float32)
         acc[...] = jnp.zeros((nodes + 8, 8, LANES), jnp.float32)
 
@@ -333,7 +357,7 @@
     return pl.pallas_call(
         kernel,
         out_shape=(piece, piece),
-        in_specs=[VMEM] * 8,
+        in_specs=[VMEM] * 9,
         out_specs=(VMEM, VMEM),
         scratch_shapes=[
             pltpu.VMEM((2 * total_rows + 8, LANES), jnp.float32),
@@ -343,11 +367,13 @@
             pltpu.SMEM(spots.shape, jnp.int32),
             pltpu.VMEM((nodes + 8, 8, LANES), jnp.float32),
             pltpu.VMEM((LANES, ZD * nodes), jnp.float32),
+            pltpu.VMEM((LANES, send), jnp.bfloat16),
+            pltpu.VMEM((send, LANES), jnp.bfloat16),
             pltpu.SemaphoreType.DMA((3,)),
         ],
         compiler_params=pltpu.CompilerParams(vmem_limit_bytes=16 << 20),
         name="encode",
-    )(own, other, rows, spots, table_weight, hidden_weight, out_weight, node_part)
+    )(own, other, other_late, rows, spots, table_weight, hidden_weight, out_weight, node_part)
 
 
 def shards(
@@ -378,7 +404,8 @@
         neighbours, neighbour_count, geom_weight, feat_weight, bias_one, hidden_weight, bias_two,
         out_weight, bias_three, groups, points, send_rows, ZD * slabs,
     )
-    own, sent = select_points(blocks, coords, sent_rows, send_count)
+
+    early, sent = select_points(blocks[:-1], 0, coords, sent_rows, send_count.T, groups)
     moves = []
     for slab in range(slabs):
         for who in range(groups):
@@ -386,7 +413,11 @@
             if 0 <= target < slabs:
                 moves.append((slab * groups + who, target * groups + who))
     other = lax.ppermute(sent, ("slab", "chan"), moves)
-    keep, give = encode(own, other, plan, weights, chans, width)
+    own, sent_late = select_points(
+        blocks[-1:], groups - 1, None, sent_rows, send_count.T, groups, early
+    )
+    other_late = lax.ppermute(sent_late, ("slab", "chan"), moves)
+    keep, give = encode(own, other, other_late, plan, weights, chans, width, groups)
     return keep + lax.ppermute(give, "chan", [(i, i ^ 1) for i in range(groups)])
 
 

time: 37.6 us -> 44.1 us (1.17)
  the two profiles are of different devices: /device:TPU:20 before, /device:TPU:4 now
where the time goes in v8:
time: 44.1 us; the launch traced here: 43.8 us
  Pallas kernels  16.6 us (38%)
  waiting for transfers between devices  14 us (32%)
  starting transfers between devices  11 us (25%)
  local copies, waits for them, and re-layouts  1.36 us (3%)
  other arithmetic  0.6 us (1%)
    pallas_call x1, Pallas kernels, encode(): pl.pallas_call(kernel, out_shape=(piece, piece), in_specs=[VMEM] * 9, out...  9.69 us
    ppermute x3, starting transfers between devices, shards(): lax.ppermute(features, 'chan', [(i, i ^ step) for i in range(groups)])  6.65 us
    ppermute x3, waiting for transfers between devices, shards(): lax.ppermute(features, 'chan', [(i, i ^ step) for i in range(groups)])  6.23 us
    ppermute x1, waiting for transfers between devices, shards(): other_late = lax.ppermute(sent_late, ('slab', 'chan'), moves)  4.12 us
    pallas_call x2, Pallas kernels, select_points(): pl.pallas_call(kernel, out_shape=(jax.ShapeDtypeStruct((points, LANES), j...  3.85 us
    ppermute x1, waiting for transfers between devices, shards(): lax.ppermute(give, 'chan', [(i, i ^ 1) for i in range(groups)])  3.68 us
    pallas_call x1, Pallas kernels, prepare(): pl.pallas_call(kernel, out_shape=(jax.ShapeDtypeStruct((tall, slots), jnp...  3.11 us
    ppermute x1, starting transfers between devices, shards(): other_late = lax.ppermute(sent_late, ('slab', 'chan'), moves)  2.35 us
  transfers between devices with their start and end apart: 6, of which 4 were waited for; matrix products, arithmetic and copies ran while one was open for 0% of the time, Pallas kernels for 12%

profile of v8, /device:TPU:4, one launch (start us, length us, event | category | flops | bytes accessed | tf_op | source)
XLA Modules:
  0.0 43.8 jit_solution(11014316699650575483)
XLA Ops:
  0.0 0.0 copy-start
  0.0 1.6 %collective-permute-start.1 = (bf16[24,2048]{1,0:T(8,128)(2,1)}, bf16[24,2048]{1,0:T(8,128)(2,1)S(1)}, u32[]{:S(2)}, u32[]{:S(2)}) collective-permute-start(bf16[24,2048]{1,0:T(8,128)(2,1)} %refs_0_.3), channel_id=1, source_target_pairs={{0,1},{1,0},{2,3},{3,2},{4,5},{5,4},{6,7},{7,6},{8,9},{9,8},{10,11... | collective-permute-start | bytes 294920 | tf_op jit(solution)/shard_map/ppermute | solution.py:401
  1.6 2.6 %collective-permute-start.2 = (bf16[24,2048]{1,0:T(8,128)(2,1)}, bf16[24,2048]{1,0:T(8,128)(2,1)S(1)}, u32[]{:S(2)}, u32[]{:S(2)}) collective-permute-start(bf16[24,2048]{1,0:T(8,128)(2,1)} %refs_0_.3), channel_id=1, source_target_pairs={{0,2},{1,3},{2,0},{3,1},{4,6},{5,7},{6,4},{7,5},{8,10},{9,11},{10,... | collective-permute-start | bytes 294920 | tf_op jit(solution)/shard_map/ppermute | solution.py:401
  4.2 0.0 copy-start.7
  4.2 3.1 %prepare.1 = (s32[88,128]{1,0:T(8,128)}, s32[16,128]{1,0:T(8,128)}, s32[8,128]{1,0:T(8,128)}, bf16[128,256]{1,0:T(8,128)(2,1)}, bf16[128,128]{1,0:T(8,128)(2,1)}...) custom-call(s32[128]{0:T(128)} %refs_0_.2, s32[128,128]{1,0:T(8,128)} %refs_1_.1, bf16[6,80]{1,0:T(8,128)(2,1)} %bitcast.9, ...), custom_call_target="tpu_custom_call" | custom-call | tf_op jit(solution)/shard_map/prepare/pallas_call | solution.py:161
  7.3 0.0 collective-permute-done.1.refs_1_
  7.3 1.8 %collective-permute-done.2.refs_2_ = bf16[24,2048]{1,0:T(8,128)(2,1)S(1)} collective-permute-done((bf16[24,2048]{1,0:T(8,128)(2,1)}, bf16[24,2048]{1,0:T(8,128)(2,1)S(1)}, u32[]{:S(2)}, u32[]{:S(2)}) %collective-permute-start.2) | collective-permute-done | bytes 98336 | tf_op jit(solution)/shard_map/ppermute | solution.py:401
  9.1 0.0 copy-start.9
  9.1 0.0 copy-done
  9.1 0.0 copy-done.7
  9.1 0.6 %copy-done.9 = s32[2,1]{0,1:T(1,128)S(1)} copy-done((s32[2,1]{0,1:T(1,128)S(1)}, s32[2,1]{0,1:T(1,128)}, u32[]{:S(2)}) %copy-start.9) | copy-done | bytes 32
  9.8 0.0 copy-start.6
  9.8 0.7 %copy-done.6 = s32[8,128]{1,0:T(8,128)S(1)} copy-done((s32[8,128]{1,0:T(8,128)S(1)}, s32[8,128]{1,0:T(8,128)}, u32[]{:S(2)}) %copy-start.6) | copy-done | bytes 4120
  10.4 1.8 %select_points.1 = (bf16[2048,128]{1,0:T(8,128)(2,1)S(1)}, bf16[1024,128]{1,0:T(8,128)(2,1)S(1)}) custom-call(bf16[24,2048]{1,0:T(8,128)(2,1)S(1)} %copy-done, bf16[24,2048]{1,0:T(8,128)(2,1)S(1)} %collective-permute-done.1.refs_1_, bf16[24,2048]{1,0:T(8,128)(2,1)S(1)} %collective-permute-done.2.refs_2_, bf16[3,2048]{1,0:T(4,128)(2,1)S(1)} %copy-done.7, ...), custom_call_target="tpu_custom_call" | custom-call | tf_op jit(solution)/shard_map/select_points/pallas_call | solution.py:235
  12.3 1.9 %collective-permute-start.3 = (bf16[1024,128]{1,0:T(8,128)(2,1)S(1)}, bf16[1024,128]{1,0:T(8,128)(2,1)S(1)}, u32[]{:S(2)}, u32[]{:S(2)}) collective-permute-start(bf16[1024,128]{1,0:T(8,128)(2,1)S(1)} %get-tuple-element.21), channel_id=1, source_target_pairs={{0,4},{2,6},{4,8},{5,1},{6,10},{7,3},{8,12},{9,5},{10,14},{11,7},{... | collective-permute-start | bytes 786440 | tf_op jit(solution)/shard_map/ppermute | solution.py:415
  14.2 2.5 %collective-permute-start = (bf16[24,2048]{1,0:T(8,128)(2,1)S(1)}, bf16[24,2048]{1,0:T(8,128)(2,1)S(1)}, u32[]{:S(2)}, u32[]{:S(2)}) collective-permute-start(bf16[24,2048]{1,0:T(8,128)(2,1)S(1)} %copy-done), channel_id=1, source_target_pairs={{0,3},{1,2},{2,1},{3,0},{4,7},{5,6},{6,5},{7,4},{8,11},{9,10},{10,... | collective-permute-start | bytes 294920 | tf_op jit(solution)/shard_map/ppermute | solution.py:401
  16.7 4.4 %collective-permute-done.refs_0_ = bf16[24,2048]{1,0:T(8,128)(2,1)S(1)} collective-permute-done((bf16[24,2048]{1,0:T(8,128)(2,1)S(1)}, bf16[24,2048]{1,0:T(8,128)(2,1)S(1)}, u32[]{:S(2)}, u32[]{:S(2)}) %collective-permute-start) | collective-permute-done | bytes 98336 | tf_op jit(solution)/shard_map/ppermute | solution.py:401
  21.1 0.0 copy-start.1
  21.1 0.0 copy-start.2
  21.1 0.0 copy-start.3
  21.1 0.0 copy-start.4
  21.1 0.0 copy-start.5
  21.1 2.0 %select_late.1 = (bf16[2048,128]{1,0:T(8,128)(2,1)S(1)}, bf16[32,1024]{1,0:T(8,128)(2,1)S(1)}) custom-call(bf16[24,2048]{1,0:T(8,128)(2,1)S(1)} %collective-permute-done.refs_0_, bf16[2048,128]{1,0:T(8,128)(2,1)S(1)} %get-tuple-element.19.refs_1_, s32[8,128]{1,0:T(8,128)S(1)} %copy-done.6, s32[1,2]{1,0:T(1,128)S(1)} %bitcast.7), custom_call_target="tpu_custom_call" | custom-call | tf_op jit(solution)/shard_map/select_late/pallas_call | solution.py:235
  23.2 0.0 copy-start.8
  23.2 2.4 %collective-permute-start.4 = (bf16[32,1024]{1,0:T(8,128)(2,1)S(1)}, bf16[32,1024]{1,0:T(8,128)(2,1)S(1)}, u32[]{:S(2)}, u32[]{:S(2)}) collective-permute-start(bf16[32,1024]{1,0:T(8,128)(2,1)S(1)} %get-tuple-element.22), channel_id=1, source_target_pairs={{0,4},{2,6},{4,8},{5,1},{6,10},{7,3},{8,12},{9,5},{10,14},{11,7},{... | collective-permute-start | bytes 196616 | tf_op jit(solution)/shard_map/ppermute | solution.py:419
  25.5 4.1 %collective-permute-done.4.late_ref = bf16[32,1024]{1,0:T(8,128)(2,1)S(1)} collective-permute-done((bf16[32,1024]{1,0:T(8,128)(2,1)S(1)}, bf16[32,1024]{1,0:T(8,128)(2,1)S(1)}, u32[]{:S(2)}, u32[]{:S(2)}) %collective-permute-start.4) | collective-permute-done | bytes 65568 | tf_op jit(solution)/shard_map/ppermute | solution.py:419
  29.7 0.0 collective-permute-done.3.other_ref
  29.7 0.0 copy-done.1
  29.7 0.0 copy-done.2
  29.7 0.0 copy-done.3
  29.7 0.0 copy-done.4
  29.7 0.0 copy-done.5
  29.7 0.0 copy-done.8
  29.7 9.7 %encode.1 = (f32[24,128]{1,0:T(8,128)S(1)}, f32[24,128]{1,0:T(8,128)S(1)}) custom-call(bf16[2048,128]{1,0:T(8,128)(2,1)S(1)} %get-tuple-element.20.own_ref, bf16[1024,128]{1,0:T(8,128)(2,1)S(1)} %collective-permute-done.3.other_ref, bf16[32,1024]{1,0:T(8,128)(2,1)S(1)} %collective-permute-done.4.late_ref, s32[88,128]{1,0:T(8,128)S(1)} %copy-done.2, ...), custom_call_target="tpu_custom_call" | custom-call | tf_op jit(solution)/shard_map/encode/pallas_call | solution.py:357
  39.4 0.1 collective-permute-start.5
  39.5 3.7 %collective-permute-done.5 = f32[24,128]{1,0:T(8,128)S(1)} collective-permute-done((f32[24,128]{1,0:T(8,128)S(1)}, f32[24,128]{1,0:T(8,128)S(1)}, u32[]{:S(2)}, u32[]{:S(2)}) %collective-permute-start.5) | collective-permute-done | bytes 12320 | tf_op jit(solution)/shard_map/ppermute | solution.py:421
  43.2 0.6 %add.3 = f32[24,128]{1,0:T(8,128)} add(f32[24,128]{1,0:T(8,128)S(1)} %get-tuple-element.29, f32[24,128]{1,0:T(8,128)S(1)} %collective-permute-done.5) | non-fusion elementwise | flops 3072 | bytes 36864 | tf_op jit(solution)/shard_map/add | solution.py:421
Async XLA Ops:
  0.0 9.1 %copy-start = (bf16[24,2048]{1,0:T(8,128)(2,1)S(1)}, bf16[24,2048]{1,0:T(8,128)(2,1)}, u32[]{:S(2)}) copy-start(bf16[24,2048]{1,0:T(8,128)(2,1)} %refs_0_.3) | copy-start | bytes 294916
  0.0 7.3 %collective-permute-start.1 = (bf16[24,2048]{1,0:T(8,128)(2,1)}, bf16[24,2048]{1,0:T(8,128)(2,1)S(1)}, u32[]{:S(2)}, u32[]{:S(2)}) collective-permute-start(bf16[24,2048]{1,0:T(8,128)(2,1)} %refs_0_.3), channel_id=1, source_target_pairs={{0,1},{1,0},{2,3},{3,2},{4,5},{5,4},{6,7},{7,6},{8,9},{9,8},{10,11... | collective-permute-start | bytes 294920 | tf_op jit(solution)/shard_map/ppermute | solution.py:401
  1.6 7.5 %collective-permute-start.2 = (bf16[24,2048]{1,0:T(8,128)(2,1)}, bf16[24,2048]{1,0:T(8,128)(2,1)S(1)}, u32[]{:S(2)}, u32[]{:S(2)}) collective-permute-start(bf16[24,2048]{1,0:T(8,128)(2,1)} %refs_0_.3), channel_id=1, source_target_pairs={{0,2},{1,3},{2,0},{3,1},{4,6},{5,7},{6,4},{7,5},{8,10},{9,11},{10,... | collective-permute-start | bytes 294920 | tf_op jit(solution)/shard_map/ppermute | solution.py:401
  4.2 4.9 %copy-start.7 = (bf16[3,2048]{1,0:T(4,128)(2,1)S(1)}, bf16[3,2048]{1,0:T(4,128)(2,1)}, u32[]{:S(2)}) copy-start(bf16[3,2048]{1,0:T(4,128)(2,1)} %refs_3_.3) | copy-start | bytes 36868
  9.1 0.7 %copy-start.9 = (s32[2,1]{0,1:T(1,128)S(1)}, s32[2,1]{0,1:T(1,128)}, u32[]{:S(2)}) copy-start(s32[2,1]{0,1:T(1,128)} %param.16) | copy-start | bytes 28
  9.8 0.7 %copy-start.6 = (s32[8,128]{1,0:T(8,128)S(1)}, s32[8,128]{1,0:T(8,128)}, u32[]{:S(2)}) copy-start(s32[8,128]{1,0:T(8,128)} %get-tuple-element.18.refs_4_.refs_2_) | copy-start | bytes 12292
  12.3 17.4 %collective-permute-start.3 = (bf16[1024,128]{1,0:T(8,128)(2,1)S(1)}, bf16[1024,128]{1,0:T(8,128)(2,1)S(1)}, u32[]{:S(2)}, u32[]{:S(2)}) collective-permute-start(bf16[1024,128]{1,0:T(8,128)(2,1)S(1)} %get-tuple-element.21), channel_id=1, source_target_pairs={{0,4},{2,6},{4,8},{5,1},{6,10},{7,3},{8,12},{9,5},{10,14},{11,7},{... | collective-permute-start | bytes 786440 | tf_op jit(solution)/shard_map/ppermute | solution.py:415
  14.2 6.9 %collective-permute-start = (bf16[24,2048]{1,0:T(8,128)(2,1)S(1)}, bf16[24,2048]{1,0:T(8,128)(2,1)S(1)}, u32[]{:S(2)}, u32[]{:S(2)}) collective-permute-start(bf16[24,2048]{1,0:T(8,128)(2,1)S(1)} %copy-done), channel_id=1, source_target_pairs={{0,3},{1,2},{2,1},{3,0},{4,7},{5,6},{6,5},{7,4},{8,11},{9,10},{10,... | collective-permute-start | bytes 294920 | tf_op jit(solution)/shard_map/ppermute | solution.py:401
  21.1 8.6 %copy-start.1 = (bf16[128,256]{1,0:T(8,128)(2,1)S(1)}, bf16[128,256]{1,0:T(8,128)(2,1)}, u32[]{:S(2)}) copy-start(bf16[128,256]{1,0:T(8,128)(2,1)} %get-tuple-element.25.table_w) | copy-start | bytes 196612
  21.1 8.6 %copy-start.2 = (s32[88,128]{1,0:T(8,128)S(1)}, s32[88,128]{1,0:T(8,128)}, u32[]{:S(2)}) copy-start(s32[88,128]{1,0:T(8,128)} %get-tuple-element.23.rows_ref) | copy-start | bytes 135172
  21.1 8.6 %copy-start.3 = (f32[72,128]{1,0:T(8,128)S(1)}, f32[72,128]{1,0:T(8,128)}, u32[]{:S(2)}) copy-start(f32[72,128]{1,0:T(8,128)} %get-tuple-element.28.node_pre) | copy-start | bytes 110596
  21.1 8.6 %copy-start.4 = (bf16[128,128]{1,0:T(8,128)(2,1)S(1)}, bf16[128,128]{1,0:T(8,128)(2,1)}, u32[]{:S(2)}) copy-start(bf16[128,128]{1,0:T(8,128)(2,1)} %get-tuple-element.26.hidden_w) | copy-start | bytes 98308
  21.1 8.6 %copy-start.5 = (bf16[128,128]{1,0:T(8,128)(2,1)S(1)}, bf16[128,128]{1,0:T(8,128)(2,1)}, u32[]{:S(2)}) copy-start(bf16[128,128]{1,0:T(8,128)(2,1)} %get-tuple-element.27.out_w) | copy-start | bytes 98308
  23.2 6.5 %copy-start.8 = (s32[16,128]{1,0:T(8,128)S(1)}, s32[16,128]{1,0:T(8,128)}, u32[]{:S(2)}) copy-start(s32[16,128]{1,0:T(8,128)} %get-tuple-element.24.spots_ref) | copy-start | bytes 24580
  23.2 6.5 %collective-permute-start.4 = (bf16[32,1024]{1,0:T(8,128)(2,1)S(1)}, bf16[32,1024]{1,0:T(8,128)(2,1)S(1)}, u32[]{:S(2)}, u32[]{:S(2)}) collective-permute-start(bf16[32,1024]{1,0:T(8,128)(2,1)S(1)} %get-tuple-element.22), channel_id=1, source_target_pairs={{0,4},{2,6},{4,8},{5,1},{6,10},{7,3},{8,12},{9,5},{10,14},{11,7},{... | collective-permute-start | bytes 196616 | tf_op jit(solution)/shard_map/ppermute | solution.py:419
  39.4 3.8 %collective-permute-start.5 = (f32[24,128]{1,0:T(8,128)S(1)}, f32[24,128]{1,0:T(8,128)S(1)}, u32[]{:S(2)}, u32[]{:S(2)}) collective-permute-start(f32[24,128]{1,0:T(8,128)S(1)} %get-tuple-element.30), channel_id=1, source_target_pairs={{0,1},{1,0},{2,3},{3,2},{4,5},{5,4},{6,7},{7,6},{8,9},{9,8},{10,11... | collective-permute-start | bytes 36872 | tf_op jit(solution)/shard_map/ppermute | solution.py:421

commit v9 on v7

--- a/solution.py
+++ b/solution.py
@@ -11,7 +11,6 @@
 LANES = 128
 CHUNK = 16
 BLOCK = 64
-CONSTANT = 16.0
 GELU_ONE = 0.7978845608028654
 GELU_CUBE = 0.044715 * GELU_ONE
 
@@ -37,14 +36,7 @@
     nodes = per_slab // ZD
     per_node = slots // CHUNK
     most = nodes * per_node
-    nothing = 2 * (points + send)
-    extra = slice(hidden, hidden + 3)
-
-    def parts(value):
-        high = value.astype(jnp.bfloat16).astype(jnp.float32)
-        mid = (value - high).astype(jnp.bfloat16).astype(jnp.float32)
-        low = (value - high - mid).astype(jnp.bfloat16).astype(jnp.float32)
-        return jnp.concatenate([high, mid, low], axis=0) * (1.0 / CONSTANT)
+    nothing = points + send
 
     given = (
         neighbour_count, neighbours, geom_weight.T, feat_weight, bias_one[None], hidden_weight,
@@ -54,9 +46,11 @@
     listed = send // LANES
 
     def kernel(*refs):
-        rows_ref, spot_ref, sent_ref, table_w, hidden_w, out_w, node_pre = refs[len(given) :][:7]
-        held = refs[len(given) + 7 :][: len(given)]
-        wide, square, spread, arrived = refs[2 * len(given) + 7 :]
+        rows_ref, spot_ref, sent_ref, halo_ref, table_w, hidden_w, out_w, node_pre, vec_ref = refs[
+            len(given) :
+        ][:9]
+        held = refs[len(given) + 9 :][: len(given)]
+        wide, square, spread, arrived = refs[2 * len(given) + 9 :]
         copies = [
             pltpu.make_async_copy(source, target, arrived.at[at])
             for at, (source, target) in enumerate(zip(refs, held))
@@ -69,7 +63,6 @@
         member = lax.axis_index("chan")
         start = (member % ZD) * nodes
         first_id = lax.axis_index("slab") * per_slab + start
-        lane = lax.broadcasted_iota(jnp.int32, (1, LANES), 1)
 
         slot = lax.broadcasted_iota(jnp.int32, (1, slots), 1)
         rows_ref[...] = jnp.full((tall, slots), nothing, jnp.int32)
@@ -90,7 +83,9 @@
             for i in range(together):
                 row = nbr_ref[pl.ds(start + first + i, 1), :]
                 row = jnp.where(row >= points + send, row - send, row)
-                row = jnp.where(slot < counts[i], 2 * row, nothing)
+                row = jnp.where(slot < counts[i], row, nothing)
+                halo = jnp.where(row < points, -1, row - points).astype(jnp.float32)
+                halo_ref[pl.ds(first + i, 1), :] = halo
                 turned.append(pltpu.roll(row, (spots[i] % per_node) * CHUNK, 1))
             for i in range(together):
                 line = spots[i] // per_node
@@ -113,48 +108,43 @@
         square[...] = jnp.zeros((LANES, LANES), jnp.float32)
         square[0:hidden, 0:channels] = feat_ref[...].astype(jnp.float32)
         square[...] = square[...].T
-        wide[...] = jnp.zeros((LANES, 2 * LANES), jnp.float32)
+        wide[...] = jnp.zeros((LANES, LANES), jnp.float32)
         for block in range(groups):
-            wide[block * width : block * width + chans, 0:LANES] = square[
+            wide[block * width : block * width + chans, :] = square[
                 block * chans : (block + 1) * chans, :
             ]
         geom = geom_ref[...].astype(jnp.float32)
         wide[chans : chans + 3, 0:hidden] = geom[3:6]
         row = lax.broadcasted_iota(jnp.int32, (LANES, LANES), 0)
-        col = lax.broadcasted_iota(jnp.int32, (LANES, LANES), 1)
+        value = lax.broadcasted_iota(jnp.int32, (LANES, LANES), 1) - hidden
         pair = member // 2
-        take = ((row == pair * 2 * width + col) & (col < 2 * width)) | (
-            (row == chans + 3) & (col == LANES - 1)
-        )
-        wide[:, LANES:] = take.astype(jnp.float32)
-        table_w[...] = wide[...].astype(jnp.bfloat16)
+        half = (value >= chans).astype(jnp.int32)
+        take = (value >= 0) & (value < 2 * chans)
+        take = take & (row == (2 * pair + half) * width + value - half * chans)
+        table_w[...] = jnp.where(take, 1.0, wide[...]).astype(jnp.bfloat16)
 
         square[...] = jnp.zeros((LANES, LANES), jnp.float32)
         square[0:hidden, 0:hidden] = 0.5 * hidden_ref[...].astype(jnp.float32)
-        square[...] = square[...].T
-        square[extra, 0:hidden] = parts(two_ref[...])
-        ones = (lane >= hidden) & (lane < hidden + 3)
-        square[hidden : hidden + 1, hidden:] = jnp.where(ones, 0.5, 0.0)[:, hidden:]
-        hidden_w[...] = square[...].astype(jnp.bfloat16)
+        hidden_w[...] = square[...].T.astype(jnp.bfloat16)
 
         square[...] = jnp.zeros((LANES, LANES), jnp.float32)
         square[0:hidden, 0:channels] = 0.5 * out_ref[...].astype(jnp.float32)
-        square[extra, 0:channels] = parts(three_ref[...])
+        square[hidden : hidden + 1, 0:channels] = three_ref[...]
         square[...] = square[...].T
         spread[...] = jnp.zeros((LANES, LANES), jnp.float32)
-        for half in range(2):
-            spread[half * width : half * width + chans, :] = square[
-                pl.ds((2 * pair + half) * chans, chans), :
-            ]
-        spread[LANES - 1 :, :] = jnp.where(lane == hidden, 1.0 / CONSTANT, 0.0)
-        out_w[...] = spread[...].T.astype(jnp.bfloat16)
+        spread[hidden : hidden + 2 * chans, :] = square[pl.ds(2 * pair * chans, 2 * chans), :]
+        square[...] = spread[...].T
+        out_w[...] = jnp.where(row < hidden, square[...], 0.0).astype(jnp.bfloat16)
+        vec_ref[...] = jnp.zeros((8, LANES), jnp.float32)
+        vec_ref[0:1, 0:hidden] = two_ref[...]
+        vec_ref[1:2, :] = square[hidden : hidden + 1, :]
 
         ids = first_id + lax.broadcasted_iota(jnp.int32, (nodes + 8, 1), 0)
         along_x = ((ids % GX).astype(jnp.float32) + 0.5) / GX
         along_y = ((ids // GX % GY).astype(jnp.float32) + 0.5) / GY
         along_z = ((ids // (GX * GY)).astype(jnp.float32) + 0.5) / depth
         term = geom[0:1] * along_x + geom[1:2] * along_y + geom[2:3] * along_z + one_ref[...]
-        node_pre[...] = jnp.broadcast_to(jnp.where(ones, 0.5 * CONSTANT, 0.0), (nodes + 8, LANES))
+        node_pre[...] = jnp.zeros((nodes + 8, LANES), jnp.float32)
         node_pre[:, 0:hidden] = term
 
     out = pl.pallas_call(
@@ -163,17 +153,19 @@
             jax.ShapeDtypeStruct((tall, slots), jnp.int32),
             jax.ShapeDtypeStruct((16, LANES), jnp.int32),
             jax.ShapeDtypeStruct((listed, LANES), jnp.int32),
-            jax.ShapeDtypeStruct((LANES, 2 * LANES), jnp.bfloat16),
+            jax.ShapeDtypeStruct((nodes, slots), jnp.float32),
+            jax.ShapeDtypeStruct((LANES, LANES), jnp.bfloat16),
             jax.ShapeDtypeStruct((LANES, LANES), jnp.bfloat16),
             jax.ShapeDtypeStruct((LANES, LANES), jnp.bfloat16),
             jax.ShapeDtypeStruct((nodes + 8, LANES), jnp.float32),
+            jax.ShapeDtypeStruct((8, LANES), jnp.float32),
         ),
         in_specs=[HBM] * len(given),
-        out_specs=(VMEM,) * 7,
+        out_specs=(VMEM,) * 9,
         scratch_shapes=[pltpu.SMEM(neighbour_count.shape, jnp.int32)]
         + [pltpu.VMEM(array.shape, array.dtype) for array in given[1:]]
         + [
-            pltpu.VMEM((LANES, 2 * LANES), jnp.float32),
+            pltpu.VMEM((LANES, LANES), jnp.float32),
             pltpu.VMEM((LANES, LANES), jnp.float32),
             pltpu.VMEM((LANES, LANES), jnp.float32),
             pltpu.SemaphoreType.DMA((len(given),)),
@@ -233,9 +225,9 @@
     )(*blocks, coords, send_rows, send_count)
 
 
-def encode(own, other, plan, weights, chans, width):
+def encode(own, other, plan, weights, chans, hidden):
     rows, spots = plan
-    table_weight, hidden_weight, out_weight, node_part = weights
+    halo, table_weight, hidden_weight, out_weight, node_part, vectors = weights
     points = own.shape[0]
     send = other.shape[0]
     nodes = node_part.shape[0] - 8
@@ -245,8 +237,8 @@
     lines = pairs // slots
 
     def kernel(
-        own_ref, other_ref, rows_ref, spots_ref, table_w, hidden_w, out_w, node_pre,
-        keep_ref, give_ref, table, picked, names_a, names_b, spot_ref, acc, turned,
+        own_ref, other_ref, rows_ref, spots_ref, halo_ref, table_w, hidden_w, out_w, node_pre,
+        vec_ref, keep_ref, give_ref, table, picked, names_a, names_b, spot_ref, acc, turned,
         arrived,
     ):
         parity = 1 - lax.axis_index("chan") % ZD
@@ -264,22 +256,20 @@
             step = 256
             for at in range(0, count, step):
                 both = jnp.dot(source[pl.ds(at, step), :], table_w[...], preferred_element_type=jnp.float32)
-                pre = both[:, :LANES].astype(jnp.bfloat16).astype(jnp.float32)
-                table[pl.ds(2 * (start + at), step, stride=2), :] = pre
-                table[pl.ds(2 * (start + at) + 1, step, stride=2), :] = both[:, LANES:]
+                table[start + at : start + at + step, :] = both.astype(jnp.bfloat16).astype(jnp.float32)
 
         fill(own_ref, 0, points)
         fill(other_ref, points, send)
-        table[pl.ds(2 * total_rows, 8), :] = jnp.zeros((8, LANES), jnp.float32)
+        table[total_rows : total_rows + 8, :] = jnp.zeros((8, LANES), jnp.float32)
         acc[...] = jnp.zeros((nodes + 8, 8, LANES), jnp.float32)
 
         def one_block(block, names):
             for base in range(0, pairs, CHUNK):
                 got = [
-                    table[pl.ds(names[at // slots, at % slots], 2), :] for at in range(base, base + CHUNK)
+                    table[pl.ds(names[at // slots, at % slots], 1), :] for at in range(base, base + CHUNK)
                 ]
                 for j in range(CHUNK):
-                    picked[2 * (base + j) : 2 * (base + j) + 2, :] = got[j]
+                    picked[base + j : base + j + 1, :] = got[j]
             step = 8
             for group in range(BLOCK // step):
                 base = group * step * CHUNK
@@ -288,13 +278,12 @@
                     [jnp.broadcast_to(node_pre[pl.ds(spot, 1), :], (CHUNK, LANES)) for spot in here],
                     axis=0,
                 )
-                pre = picked[pl.ds(2 * base, step * CHUNK, stride=2), :]
-                val = picked[pl.ds(2 * base + 1, step * CHUNK, stride=2), :]
-                first = gelu_doubled(pre + offset).astype(jnp.bfloat16)
+                row = picked[base : base + step * CHUNK, :]
+                first = gelu_doubled(row + offset).astype(jnp.bfloat16)
                 second = jnp.dot(first, hidden_w[...], preferred_element_type=jnp.float32)
-                second = gelu_doubled(second).astype(jnp.bfloat16)
-                kappa = jnp.dot(second, out_w[...], preferred_element_type=jnp.float32)
-                product = kappa * val
+                second = gelu_doubled(second + vec_ref[0:1]).astype(jnp.bfloat16)
+                kappa = jnp.dot(second, out_w[...], preferred_element_type=jnp.float32) + vec_ref[1:2]
+                product = kappa * row
                 for i, spot in enumerate(here):
                     part = product[i * CHUNK : i * CHUNK + 8]
                     for j in range(8, CHUNK, 8):
@@ -320,24 +309,26 @@
         lax.fori_loop(0, (blocks + 1) // 2, one_step, 0)
         fetch(0, names_a, 0).wait()
         fetch(1, names_b, 1).wait()
-        sums = jnp.sum(acc[0:nodes], axis=1)
-        means = (sums / sums[:, LANES - 1 :]).T
+        live = jnp.sum(other_ref[:, chans + 3 : chans + 4].astype(jnp.float32), axis=0, keepdims=True)
+        used = jnp.where(halo_ref[...] < live, 1.0, 0.0)
+        used = jnp.sum(used, axis=1, keepdims=True)
+        means = (jnp.sum(acc[0:nodes], axis=1) / used).T
         low = jnp.where(parity == 1, means, 0.0)
         turned[...] = jnp.concatenate([low, means - low], axis=1)
-        mine = pl.multiple_of((1 - parity) * width, width)
-        theirs = pl.multiple_of(parity * width, width)
-        keep_ref[...] = turned[pl.ds(mine, chans), :]
-        give_ref[...] = turned[pl.ds(theirs, chans), :]
+        first = turned[hidden : hidden + chans, :]
+        second = turned[hidden + chans : hidden + 2 * chans, :]
+        keep_ref[...] = jnp.where(parity == 1, first, second)
+        give_ref[...] = jnp.where(parity == 1, second, first)
 
     piece = jax.ShapeDtypeStruct((chans, ZD * nodes), jnp.float32)
     return pl.pallas_call(
         kernel,
         out_shape=(piece, piece),
-        in_specs=[VMEM] * 8,
+        in_specs=[VMEM] * 10,
         out_specs=(VMEM, VMEM),
         scratch_shapes=[
-            pltpu.VMEM((2 * total_rows + 8, LANES), jnp.float32),
-            pltpu.VMEM((2 * pairs, LANES), jnp.float32),
+            pltpu.VMEM((total_rows + 8, LANES), jnp.float32),
+            pltpu.VMEM((pairs, LANES), jnp.float32),
             pltpu.SMEM((lines, slots), jnp.int32),
             pltpu.SMEM((lines, slots), jnp.int32),
             pltpu.SMEM(spots.shape, jnp.int32),
@@ -347,7 +338,9 @@
         ],
         compiler_params=pltpu.CompilerParams(vmem_limit_bytes=16 << 20),
         name="encode",
-    )(own, other, rows, spots, table_weight, hidden_weight, out_weight, node_part)
+    )(
+        own, other, rows, spots, halo, table_weight, hidden_weight, out_weight, node_part, vectors
+    )
 
 
 def shards(
@@ -368,7 +361,6 @@
     groups = lax.axis_size("chan")
     slabs = lax.axis_size("slab")
     chans, points = features.shape
-    width = LANES // groups
 
     blocks = [features]
     for step in range(1, groups):
@@ -386,7 +378,7 @@
             if 0 <= target < slabs:
                 moves.append((slab * groups + who, target * groups + who))
     other = lax.ppermute(sent, ("slab", "chan"), moves)
-    keep, give = encode(own, other, plan, weights, chans, width)
+    keep, give = encode(own, other, plan, weights, chans, hidden_weight.shape[0])
     return keep + lax.ppermute(give, "chan", [(i, i ^ 1) for i in range(groups)])
 
 

time: 37.6 us -> 38.2 us (1.016)
  local copies, waits for them, and re-layouts: 1.45 us -> 2.12 us
    unnamed x19 -> x23, local copies, waits for them, and re-layouts: 1.45 us -> 2.12 us
where the time goes in v9:
time: 38.2 us; the launch traced here: 37.9 us
  waiting for transfers between devices  15 us (39%)
  Pallas kernels  14.5 us (38%)
  starting transfers between devices  5.48 us (14%)
  local copies, waits for them, and re-layouts  2.12 us (6%)
  other arithmetic  0.6 us (2%)
    pallas_call x1, Pallas kernels, encode(): pl.pallas_call(kernel, out_shape=(piece, piece), in_specs=[VMEM] * 10, ou...  9.69 us
    ppermute x1, waiting for transfers between devices, shards(): other = lax.ppermute(sent, ('slab', 'chan'), moves)  6.66 us
    ppermute x3, waiting for transfers between devices, shards(): lax.ppermute(features, 'chan', [(i, i ^ step) for i in range(groups)])  4.68 us
    ppermute x1, waiting for transfers between devices, shards(): lax.ppermute(give, 'chan', [(i, i ^ 1) for i in range(groups)])  3.68 us
    ppermute x3, starting transfers between devices, shards(): lax.ppermute(features, 'chan', [(i, i ^ step) for i in range(groups)])  3.49 us
    pallas_call x1, Pallas kernels, prepare(): pl.pallas_call(kernel, out_shape=(jax.ShapeDtypeStruct((tall, slots), jnp...  3.04 us
    unnamed x23, local copies, waits for them, and re-layouts  2.12 us
    ppermute x1, starting transfers between devices, shards(): other = lax.ppermute(sent, ('slab', 'chan'), moves)  1.92 us
  transfers between devices with their start and end apart: 5, of which 4 were waited for; matrix products, arithmetic and copies ran while one was open for 2% of the time, Pallas kernels for 8%

profile of v9, /device:TPU:20, one launch (start us, length us, event | category | flops | bytes accessed | tf_op | source)
XLA Modules:
  0.0 37.9 jit_solution(13569334059098022753)
XLA Ops:
  0.0 0.0 copy-start
  0.0 0.3 collective-permute-start.1
  0.3 1.6 %collective-permute-start = (bf16[24,2048]{1,0:T(8,128)(2,1)}, bf16[24,2048]{1,0:T(8,128)(2,1)S(1)}, u32[]{:S(2)}, u32[]{:S(2)}) collective-permute-start(bf16[24,2048]{1,0:T(8,128)(2,1)} %refs_0_.3), channel_id=1, source_target_pairs={{0,1},{1,0},{2,3},{3,2},{4,5},{5,4},{6,7},{7,6},{8,9},{9,8},{10,11... | collective-permute-start | bytes 294920 | tf_op jit(solution)/shard_map/ppermute | solution.py:367
  1.9 1.6 %collective-permute-start.2 = (bf16[24,2048]{1,0:T(8,128)(2,1)}, bf16[24,2048]{1,0:T(8,128)(2,1)S(1)}, u32[]{:S(2)}, u32[]{:S(2)}) collective-permute-start(bf16[24,2048]{1,0:T(8,128)(2,1)} %refs_0_.3), channel_id=1, source_target_pairs={{0,3},{1,2},{2,1},{3,0},{4,7},{5,6},{6,5},{7,4},{8,11},{9,10},{10,... | collective-permute-start | bytes 294920 | tf_op jit(solution)/shard_map/ppermute | solution.py:367
  3.5 0.7 %copy.14.refs_6_ = s32[2,1]{1,0:T(2,128)S(1)} copy(s32[2,1]{0,1:T(1,128)} %param.16) | data formatting | bytes 16 | tf_op args[3]
  4.2 0.0 copy-start.7
  4.2 3.0 %prepare.1 = (s32[88,128]{1,0:T(8,128)}, s32[16,128]{1,0:T(8,128)}, s32[8,128]{1,0:T(8,128)}, f32[64,128]{1,0:T(8,128)}, bf16[128,128]{1,0:T(8,128)(2,1)}, /*ind...) custom-call(s32[128]{0:T(128)} %refs_0_.2, s32[128,128]{1,0:T(8,128)} %refs_1_.1, ...), custom_call_target="tpu_custom_call" | custom-call | tf_op jit(solution)/shard_map/prepare/pallas_call | solution.py:150
  7.3 0.0 collective-permute-done.1.refs_2_
  7.3 0.2 collective-permute-done.refs_1_
  7.5 4.5 %collective-permute-done.2.refs_3_ = bf16[24,2048]{1,0:T(8,128)(2,1)S(1)} collective-permute-done((bf16[24,2048]{1,0:T(8,128)(2,1)}, bf16[24,2048]{1,0:T(8,128)(2,1)S(1)}, u32[]{:S(2)}, u32[]{:S(2)}) %collective-permute-start.2) | collective-permute-done | bytes 98336 | tf_op jit(solution)/shard_map/ppermute | solution.py:367
  12.0 0.0 copy-done
  12.0 0.0 copy-done.7
  12.0 0.0 copy-start.10
  12.0 0.7 %copy-done.10 = s32[8,128]{1,0:T(8,128)S(1)} copy-done((s32[8,128]{1,0:T(8,128)S(1)}, s32[8,128]{1,0:T(8,128)}, u32[]{:S(2)}) %copy-start.10) | copy-done | bytes 4120
  12.6 0.0 copy-start.1
  12.7 0.0 copy-start.2
  12.7 0.0 copy-start.3
  12.7 0.0 copy-start.4
  12.7 0.0 copy-start.5
  12.7 0.0 copy-start.6
  12.7 1.8 %select_points.1 = (bf16[2048,128]{1,0:T(8,128)(2,1)S(1)}, bf16[1024,128]{1,0:T(8,128)(2,1)S(1)}) custom-call(bf16[24,2048]{1,0:T(8,128)(2,1)S(1)} %copy-done, bf16[24,2048]{1,0:T(8,128)(2,1)S(1)} %collective-permute-done.refs_1_, bf16[24,2048]{1,0:T(8,128)(2,1)S(1)} %collective-permute-done.1.refs_2_, bf16[24,2048]{1,0:T(8,128)(2,1)S(1)} %collective-permute-done.2.refs_3_, ...), custom_call_target="tpu_custom_call" | custom-call | tf_op jit(solution)/shard_map/select_points/pallas_call | solution.py:210
  14.5 1.9 %collective-permute-start.3 = (bf16[1024,128]{1,0:T(8,128)(2,1)S(1)}, bf16[1024,128]{1,0:T(8,128)(2,1)S(1)}, u32[]{:S(2)}, u32[]{:S(2)}) collective-permute-start(bf16[1024,128]{1,0:T(8,128)(2,1)S(1)} %get-tuple-element.20), channel_id=1, source_target_pairs={{0,4},{2,6},{4,8},{5,1},{6,10},{7,3},{8,12},{9,5},{10,14},{11,7},{... | collective-permute-start | bytes 786440 | tf_op jit(solution)/shard_map/ppermute | solution.py:380
  16.4 6.7 %collective-permute-done.3.other_ref = bf16[1024,128]{1,0:T(8,128)(2,1)S(1)} collective-permute-done((bf16[1024,128]{1,0:T(8,128)(2,1)S(1)}, bf16[1024,128]{1,0:T(8,128)(2,1)S(1)}, u32[]{:S(2)}, u32[]{:S(2)}) %collective-permute-start.3) | collective-permute-done | bytes 262176 | tf_op jit(solution)/shard_map/ppermute | solution.py:380
  23.1 0.0 copy-start.8
  23.1 0.0 copy-start.9
  23.1 0.0 copy-done.1
  23.1 0.0 copy-done.2
  23.1 0.0 copy-done.3
  23.1 0.0 copy-done.4
  23.1 0.0 copy-done.5
  23.1 0.0 copy-done.6
  23.1 0.6 %copy-done.8 = s32[16,128]{1,0:T(8,128)S(1)} copy-done((s32[16,128]{1,0:T(8,128)S(1)}, s32[16,128]{1,0:T(8,128)}, u32[]{:S(2)}) %copy-start.8) | copy-done | bytes 8216
  23.8 0.0 copy-done.9
  23.8 9.7 %encode.1 = (f32[24,128]{1,0:T(8,128)S(1)}, f32[24,128]{1,0:T(8,128)S(1)}) custom-call(bf16[2048,128]{1,0:T(8,128)(2,1)S(1)} %get-tuple-element.19.own_ref, bf16[1024,128]{1,0:T(8,128)(2,1)S(1)} %collective-permute-done.3.other_ref, s32[88,128]{1,0:T(8,128)S(1)} %copy-done.1, s32[16,128]{1,0:T(8,128)S(1)} %copy-done.8, f32[64,128]{1,0:T(8,128)S(1)} %copy-done.3, ...), custom_call_target="tpu_custom_call" | custom-call | tf_op jit(solution)/shard_map/encode/pallas_call | solution.py:324
  33.5 0.1 collective-permute-start.4
  33.6 3.7 %collective-permute-done.4 = f32[24,128]{1,0:T(8,128)S(1)} collective-permute-done((f32[24,128]{1,0:T(8,128)S(1)}, f32[24,128]{1,0:T(8,128)S(1)}, u32[]{:S(2)}, u32[]{:S(2)}) %collective-permute-start.4) | collective-permute-done | bytes 12320 | tf_op jit(solution)/shard_map/ppermute | solution.py:382
  37.3 0.6 %add.3 = f32[24,128]{1,0:T(8,128)} add(f32[24,128]{1,0:T(8,128)S(1)} %get-tuple-element.29, f32[24,128]{1,0:T(8,128)S(1)} %collective-permute-done.4) | non-fusion elementwise | flops 3072 | bytes 36864 | tf_op jit(solution)/shard_map/add | solution.py:382
Async XLA Ops:
  0.0 12.0 %copy-start = (bf16[24,2048]{1,0:T(8,128)(2,1)S(1)}, bf16[24,2048]{1,0:T(8,128)(2,1)}, u32[]{:S(2)}) copy-start(bf16[24,2048]{1,0:T(8,128)(2,1)} %refs_0_.3) | copy-start | bytes 294916
  0.0 7.3 %collective-permute-start.1 = (bf16[24,2048]{1,0:T(8,128)(2,1)}, bf16[24,2048]{1,0:T(8,128)(2,1)S(1)}, u32[]{:S(2)}, u32[]{:S(2)}) collective-permute-start(bf16[24,2048]{1,0:T(8,128)(2,1)} %refs_0_.3), channel_id=1, source_target_pairs={{0,2},{1,3},{2,0},{3,1},{4,6},{5,7},{6,4},{7,5},{8,10},{9,11},{10,... | collective-permute-start | bytes 294920 | tf_op jit(solution)/shard_map/ppermute | solution.py:367
  0.3 7.2 %collective-permute-start = (bf16[24,2048]{1,0:T(8,128)(2,1)}, bf16[24,2048]{1,0:T(8,128)(2,1)S(1)}, u32[]{:S(2)}, u32[]{:S(2)}) collective-permute-start(bf16[24,2048]{1,0:T(8,128)(2,1)} %refs_0_.3), channel_id=1, source_target_pairs={{0,1},{1,0},{2,3},{3,2},{4,5},{5,4},{6,7},{7,6},{8,9},{9,8},{10,11... | collective-permute-start | bytes 294920 | tf_op jit(solution)/shard_map/ppermute | solution.py:367
  1.9 10.1 %collective-permute-start.2 = (bf16[24,2048]{1,0:T(8,128)(2,1)}, bf16[24,2048]{1,0:T(8,128)(2,1)S(1)}, u32[]{:S(2)}, u32[]{:S(2)}) collective-permute-start(bf16[24,2048]{1,0:T(8,128)(2,1)} %refs_0_.3), channel_id=1, source_target_pairs={{0,3},{1,2},{2,1},{3,0},{4,7},{5,6},{6,5},{7,4},{8,11},{9,10},{10,... | collective-permute-start | bytes 294920 | tf_op jit(solution)/shard_map/ppermute | solution.py:367
  4.2 7.7 %copy-start.7 = (bf16[3,2048]{1,0:T(4,128)(2,1)S(1)}, bf16[3,2048]{1,0:T(4,128)(2,1)}, u32[]{:S(2)}) copy-start(bf16[3,2048]{1,0:T(4,128)(2,1)} %refs_4_.1) | copy-start | bytes 36868
  12.0 0.7 %copy-start.10 = (s32[8,128]{1,0:T(8,128)S(1)}, s32[8,128]{1,0:T(8,128)}, u32[]{:S(2)}) copy-start(s32[8,128]{1,0:T(8,128)} %get-tuple-element.18.refs_5_) | copy-start | bytes 12292
  12.6 10.4 %copy-start.1 = (s32[88,128]{1,0:T(8,128)S(1)}, s32[88,128]{1,0:T(8,128)}, u32[]{:S(2)}) copy-start(s32[88,128]{1,0:T(8,128)} %get-tuple-element.21.rows_ref) | copy-start | bytes 135172
  12.7 10.4 %copy-start.2 = (f32[72,128]{1,0:T(8,128)S(1)}, f32[72,128]{1,0:T(8,128)}, u32[]{:S(2)}) copy-start(f32[72,128]{1,0:T(8,128)} %get-tuple-element.27.node_pre) | copy-start | bytes 110596
  12.7 10.4 %copy-start.3 = (f32[64,128]{1,0:T(8,128)S(1)}, f32[64,128]{1,0:T(8,128)}, u32[]{:S(2)}) copy-start(f32[64,128]{1,0:T(8,128)} %get-tuple-element.23.halo_ref) | copy-start | bytes 98308
  12.7 10.5 %copy-start.4 = (bf16[128,128]{1,0:T(8,128)(2,1)S(1)}, bf16[128,128]{1,0:T(8,128)(2,1)}, u32[]{:S(2)}) copy-start(bf16[128,128]{1,0:T(8,128)(2,1)} %get-tuple-element.24.table_w) | copy-start | bytes 98308
  12.7 10.5 %copy-start.5 = (bf16[128,128]{1,0:T(8,128)(2,1)S(1)}, bf16[128,128]{1,0:T(8,128)(2,1)}, u32[]{:S(2)}) copy-start(bf16[128,128]{1,0:T(8,128)(2,1)} %get-tuple-element.25.hidden_w) | copy-start | bytes 98308
  12.7 10.5 %copy-start.6 = (bf16[128,128]{1,0:T(8,128)(2,1)S(1)}, bf16[128,128]{1,0:T(8,128)(2,1)}, u32[]{:S(2)}) copy-start(bf16[128,128]{1,0:T(8,128)(2,1)} %get-tuple-element.26.out_w) | copy-start | bytes 98308
  14.5 8.6 %collective-permute-start.3 = (bf16[1024,128]{1,0:T(8,128)(2,1)S(1)}, bf16[1024,128]{1,0:T(8,128)(2,1)S(1)}, u32[]{:S(2)}, u32[]{:S(2)}) collective-permute-start(bf16[1024,128]{1,0:T(8,128)(2,1)S(1)} %get-tuple-element.20), channel_id=1, source_target_pairs={{0,4},{2,6},{4,8},{5,1},{6,10},{7,3},{8,12},{9,5},{10,14},{11,7},{... | collective-permute-start | bytes 786440 | tf_op jit(solution)/shard_map/ppermute | solution.py:380
  23.1 0.7 %copy-start.8 = (s32[16,128]{1,0:T(8,128)S(1)}, s32[16,128]{1,0:T(8,128)}, u32[]{:S(2)}) copy-start(s32[16,128]{1,0:T(8,128)} %get-tuple-element.22.spots_ref) | copy-start | bytes 24580
  23.1 0.7 %copy-start.9 = (f32[8,128]{1,0:T(8,128)S(1)}, f32[8,128]{1,0:T(8,128)}, u32[]{:S(2)}) copy-start(f32[8,128]{1,0:T(8,128)} %get-tuple-element.28.vec_ref) | copy-start | bytes 12292
  33.5 3.8 %collective-permute-start.4 = (f32[24,128]{1,0:T(8,128)S(1)}, f32[24,128]{1,0:T(8,128)S(1)}, u32[]{:S(2)}, u32[]{:S(2)}) collective-permute-start(f32[24,128]{1,0:T(8,128)S(1)} %get-tuple-element.30), channel_id=1, source_target_pairs={{0,1},{1,0},{2,3},{3,2},{4,5},{5,4},{6,7},{7,6},{8,9},{9,8},{10,11... | collective-permute-start | bytes 36872 | tf_op jit(solution)/shard_map/ppermute | solution.py:382

commit v10 on v7

--- a/solution.py
+++ b/solution.py
@@ -4,6 +4,7 @@
 from jax.experimental import pallas as pl
 from jax.experimental.pallas import tpu as pltpu
 from jax.sharding import PartitionSpec as P
+
 
 ZD = 2
 GX = 16
@@ -48,15 +49,14 @@
 
     given = (
         neighbour_count, neighbours, geom_weight.T, feat_weight, bias_one[None], hidden_weight,
-        bias_two[None], out_weight.T, bias_three[None], send_rows,
+        bias_two[None], out_weight.T, bias_three[None],
     )
     tall = most * CHUNK // slots + 3 * BLOCK * CHUNK // slots
-    listed = send // LANES
 
     def kernel(*refs):
-        rows_ref, spot_ref, sent_ref, table_w, hidden_w, out_w, node_pre = refs[len(given) :][:7]
-        held = refs[len(given) + 7 :][: len(given)]
-        wide, square, spread, arrived = refs[2 * len(given) + 7 :]
+        rows_ref, spot_ref, table_w, hidden_w, out_w, node_pre = refs[len(given) :][:6]
+        held = refs[len(given) + 6 :][: len(given)]
+        wide, square, spread, arrived = refs[2 * len(given) + 6 :]
         copies = [
             pltpu.make_async_copy(source, target, arrived.at[at])
             for at, (source, target) in enumerate(zip(refs, held))
@@ -65,7 +65,7 @@
             copy.start()
         for copy in copies:
             copy.wait()
-        count_ref, nbr_ref, geom_ref, feat_ref, one_ref, hidden_ref, two_ref, out_ref, three_ref, send_ref = held
+        count_ref, nbr_ref, geom_ref, feat_ref, one_ref, hidden_ref, two_ref, out_ref, three_ref = held
         member = lax.axis_index("chan")
         start = (member % ZD) * nodes
         first_id = lax.axis_index("slab") * per_slab + start
@@ -105,10 +105,6 @@
         used, node_of = lax.fori_loop(0, nodes // together, some_nodes, (jnp.int32(0), none))
         spot_ref[0:8, :] = node_of
         spot_ref[8:16, :] = none + (used + BLOCK - 1) // BLOCK
-        side = 1 - member % ZD
-        chosen = send_ref[pl.ds(side, 1), :]
-        for line in range(listed):
-            sent_ref[line : line + 1, :] = chosen[:, line * LANES : (line + 1) * LANES]
 
         square[...] = jnp.zeros((LANES, LANES), jnp.float32)
         square[0:hidden, 0:channels] = feat_ref[...].astype(jnp.float32)
@@ -162,14 +158,13 @@
         out_shape=(
             jax.ShapeDtypeStruct((tall, slots), jnp.int32),
             jax.ShapeDtypeStruct((16, LANES), jnp.int32),
-            jax.ShapeDtypeStruct((listed, LANES), jnp.int32),
             jax.ShapeDtypeStruct((LANES, 2 * LANES), jnp.bfloat16),
             jax.ShapeDtypeStruct((LANES, LANES), jnp.bfloat16),
             jax.ShapeDtypeStruct((LANES, LANES), jnp.bfloat16),
             jax.ShapeDtypeStruct((nodes + 8, LANES), jnp.float32),
         ),
         in_specs=[HBM] * len(given),
-        out_specs=(VMEM,) * 7,
+        out_specs=(VMEM,) * 6,
         scratch_shapes=[pltpu.SMEM(neighbour_count.shape, jnp.int32)]
         + [pltpu.VMEM(array.shape, array.dtype) for array in given[1:]]
         + [
@@ -180,22 +175,27 @@
         ],
         name="prepare",
     )(*given)
-    return out[:2], out[2], out[3:]
+    return out[:2], out[2:]
 
 
 def select_points(blocks, coords, send_rows, send_count):
     groups = len(blocks)
     chans, points = blocks[0].shape
     width = LANES // groups
-    send = send_rows.shape[0] * LANES
+    send = send_rows.shape[1]
     unroll = 16
 
     def kernel(*refs):
         block_refs = refs[:groups]
-        coords_ref, rows_ref, count_ref = refs[groups : groups + 3]
-        own_ref, sent_ref, stack, table, picked = refs[groups + 3 :]
+        coords_ref, lists_ref, count_ref = refs[groups : groups + 3]
+        own_ref, sent_ref, stack, table, picked, lines, rows_ref, arrived = refs[groups + 3 :]
         member = lax.axis_index("chan")
         side = 1 - member % ZD
+        chosen = lists_ref[pl.ds(side, 1), :]
+        for line in range(send // LANES):
+            lines[line : line + 1, :] = chosen[:, line * LANES : (line + 1) * LANES]
+        listed = pltpu.make_async_copy(lines, rows_ref, arrived)
+        listed.start()
         for step in range(groups):
             base = pl.multiple_of((member ^ step) * width, width)
             empty = jnp.zeros((width - chans, points), jnp.bfloat16)
@@ -206,6 +206,7 @@
         own_ref[...] = own
         table[...] = own.astype(jnp.float32)
 
+        listed.wait()
         for base in range(0, send, unroll):
             rows = [
                 table[pl.ds(rows_ref[at // LANES, at % LANES], 1), :] for at in range(base, base + unroll)
@@ -213,7 +214,7 @@
             for j in range(unroll):
                 picked[base + j : base + j + 1, :] = rows[j]
         slot = lax.broadcasted_iota(jnp.int32, (send, LANES), 0)
-        sent_ref[...] = jnp.where(slot < count_ref[side, 0], picked[...], 0.0).astype(jnp.bfloat16)
+        sent_ref[...] = jnp.where(slot < count_ref[0, side], picked[...], 0.0).astype(jnp.bfloat16)
 
     return pl.pallas_call(
         kernel,
@@ -221,12 +222,15 @@
             jax.ShapeDtypeStruct((points, LANES), jnp.bfloat16),
             jax.ShapeDtypeStruct((send, LANES), jnp.bfloat16),
         ),
-        in_specs=[VMEM] * (groups + 1) + [SMEM] * 2,
+        in_specs=[VMEM] * (groups + 2) + [SMEM],
         out_specs=(VMEM, VMEM),
         scratch_shapes=[
             pltpu.VMEM((LANES, points), jnp.bfloat16),
             pltpu.VMEM((points, LANES), jnp.float32),
             pltpu.VMEM((send, LANES), jnp.float32),
+            pltpu.VMEM((send // LANES, LANES), jnp.int32),
+            pltpu.SMEM((send // LANES, LANES), jnp.int32),
+            pltpu.SemaphoreType.DMA,
         ],
         compiler_params=pltpu.CompilerParams(vmem_limit_bytes=12 << 20),
         name="select_points",
@@ -374,11 +378,12 @@
     for step in range(1, groups):
         blocks.append(lax.ppermute(features, "chan", [(i, i ^ step) for i in range(groups)]))
 
-    plan, sent_rows, weights = prepare(
+    plan, weights = prepare(
         neighbours, neighbour_count, geom_weight, feat_weight, bias_one, hidden_weight, bias_two,
         out_weight, bias_three, groups, points, send_rows, ZD * slabs,
     )
-    own, sent = select_points(blocks, coords, sent_rows, send_count)
+
+    own, sent = select_points(blocks, coords, send_rows, send_count.T)
     moves = []
     for slab in range(slabs):
         for who in range(groups):

time: 37.6 us -> 43.9 us (1.17)
  local copies, waits for them, and re-layouts: 1.45 us -> 6.23 us
  waiting for transfers between devices: 14.9 us -> 16 us
    unnamed x19 -> x20, local copies, waits for them, and re-layouts: 1.45 us -> 6.23 us
    ppermute x3, waiting for transfers between devices: 4.61 us -> 8.76 us  [shards(): lax.ppermute(features, 'chan', [(i, i ^ step) for i in range(groups)])]
    ppermute x1, waiting for transfers between devices: 6.66 us -> 3.56 us  [shards(): other = lax.ppermute(sent, ('slab', 'chan'), moves)]
  transfers between devices with their start and end apart: 5 -> 5, of which waited for: 4 -> 5; matrix products, arithmetic and copies ran while one was open for 2% -> 0% of each run, Pallas kernels for 8% -> 7%
where the time goes in v10:
time: 43.9 us; the launch traced here: 43.3 us
  waiting for transfers between devices  16 us (36%)
  Pallas kernels  14.9 us (34%)
  local copies, waits for them, and re-layouts  6.23 us (14%)
  starting transfers between devices  5.48 us (12%)
  other arithmetic  0.6 us (1%)
    pallas_call x1, Pallas kernels, encode(): pl.pallas_call(kernel, out_shape=(piece, piece), in_specs=[VMEM] * 8, out...  9.82 us
    ppermute x3, waiting for transfers between devices, shards(): lax.ppermute(features, 'chan', [(i, i ^ step) for i in range(groups)])  8.76 us
    unnamed x20, local copies, waits for them, and re-layouts  6.23 us
    ppermute x1, waiting for transfers between devices, shards(): lax.ppermute(give, 'chan', [(i, i ^ 1) for i in range(groups)])  3.68 us
    ppermute x1, waiting for transfers between devices, shards(): other = lax.ppermute(sent, ('slab', 'chan'), moves)  3.56 us
    ppermute x3, starting transfers between devices, shards(): lax.ppermute(features, 'chan', [(i, i ^ step) for i in range(groups)])  3.49 us
    pallas_call x1, Pallas kernels, prepare(): pl.pallas_call(kernel, out_shape=(jax.ShapeDtypeStruct((tall, slots), jnp...  3.08 us
    pallas_call x1, Pallas kernels, select_points(): pl.pallas_call(kernel, out_shape=(jax.ShapeDtypeStruct((points, LANES), j...  1.98 us
  transfers between devices with their start and end apart: 5, of which 5 were waited for; matrix products, arithmetic and copies ran while one was open for 0% of the time, Pallas kernels for 7%

profile of v10, /device:TPU:20, one launch (start us, length us, event | category | flops | bytes accessed | tf_op | source)
XLA Modules:
  0.0 43.3 jit_solution(12994288966919895418)
XLA Ops:
  0.0 0.0 copy-start.9
  0.0 1.6 %collective-permute-start = (bf16[24,2048]{1,0:T(8,128)(2,1)}, bf16[24,2048]{1,0:T(8,128)(2,1)S(1)}, u32[]{:S(2)}, u32[]{:S(2)}) collective-permute-start(bf16[24,2048]{1,0:T(8,128)(2,1)} %refs_0_.2), channel_id=1, source_target_pairs={{0,1},{1,0},{2,3},{3,2},{4,5},{5,4},{6,7},{7,6},{8,9},{9,8},{10,11... | collective-permute-start | bytes 294920 | tf_op jit(solution)/shard_map/ppermute | solution.py:379
  1.6 0.3 collective-permute-start.1
  1.9 1.6 %collective-permute-start.2 = (bf16[24,2048]{1,0:T(8,128)(2,1)}, bf16[24,2048]{1,0:T(8,128)(2,1)S(1)}, u32[]{:S(2)}, u32[]{:S(2)}) collective-permute-start(bf16[24,2048]{1,0:T(8,128)(2,1)} %refs_0_.2), channel_id=1, source_target_pairs={{0,3},{1,2},{2,1},{3,0},{4,7},{5,6},{6,5},{7,4},{8,11},{9,10},{10,... | collective-permute-start | bytes 294920 | tf_op jit(solution)/shard_map/ppermute | solution.py:379
  3.5 2.3 %collective-permute-done.refs_1_ = bf16[24,2048]{1,0:T(8,128)(2,1)S(1)} collective-permute-done((bf16[24,2048]{1,0:T(8,128)(2,1)}, bf16[24,2048]{1,0:T(8,128)(2,1)S(1)}, u32[]{:S(2)}, u32[]{:S(2)}) %collective-permute-start) | collective-permute-done | bytes 98336 | tf_op jit(solution)/shard_map/ppermute | solution.py:379
  5.8 3.5 %collective-permute-done.1.refs_2_ = bf16[24,2048]{1,0:T(8,128)(2,1)S(1)} collective-permute-done((bf16[24,2048]{1,0:T(8,128)(2,1)}, bf16[24,2048]{1,0:T(8,128)(2,1)S(1)}, u32[]{:S(2)}, u32[]{:S(2)}) %collective-permute-start.1) | collective-permute-done | bytes 98336 | tf_op jit(solution)/shard_map/ppermute | solution.py:379
  9.3 3.0 %collective-permute-done.2.refs_3_ = bf16[24,2048]{1,0:T(8,128)(2,1)S(1)} collective-permute-done((bf16[24,2048]{1,0:T(8,128)(2,1)}, bf16[24,2048]{1,0:T(8,128)(2,1)S(1)}, u32[]{:S(2)}, u32[]{:S(2)}) %collective-permute-start.2) | collective-permute-done | bytes 98336 | tf_op jit(solution)/shard_map/ppermute | solution.py:379
  12.3 0.0 copy-done.9
  12.3 0.0 copy-start
  12.3 0.9 %copy-done = bf16[24,2048]{1,0:T(8,128)(2,1)S(1)} copy-done((bf16[24,2048]{1,0:T(8,128)(2,1)S(1)}, bf16[24,2048]{1,0:T(8,128)(2,1)}, u32[]{:S(2)}) %copy-start) | copy-done | bytes 98328
  13.1 0.0 copy-start.6
  13.2 0.7 %copy-done.6 = bf16[3,2048]{1,0:T(4,128)(2,1)S(1)} copy-done((bf16[3,2048]{1,0:T(4,128)(2,1)S(1)}, bf16[3,2048]{1,0:T(4,128)(2,1)}, u32[]{:S(2)}) %copy-start.6) | copy-done | bytes 12312
  13.9 0.0 copy-start.8
  13.9 0.7 %copy-done.8 = s32[2,1024]{1,0:T(2,128)S(1)} copy-done((s32[2,1024]{1,0:T(2,128)S(1)}, s32[2,1024]{1,0:T(2,128)}, u32[]{:S(2)}) %copy-start.8) | copy-done | bytes 8216
  14.6 2.0 %select_points.1 = (bf16[2048,128]{1,0:T(8,128)(2,1)S(1)}, bf16[1024,128]{1,0:T(8,128)(2,1)S(1)}) custom-call(bf16[24,2048]{1,0:T(8,128)(2,1)S(1)} %copy-done, bf16[24,2048]{1,0:T(8,128)(2,1)S(1)} %collective-permute-done.refs_1_, bf16[24,2048]{1,0:T(8,128)(2,1)S(1)} %collective-permute-done.1.refs_2_, bf16[24,2048]{1,0:T(8,128)(2,1)S(1)} %collective-permute-done.2.refs_3_, ...), custom_call_target="tpu_custom_call" | custom-call | tf_op jit(solution)/shard_map/select_points/pallas_call | solution.py:219
  16.6 1.9 %collective-permute-start.3 = (bf16[1024,128]{1,0:T(8,128)(2,1)S(1)}, bf16[1024,128]{1,0:T(8,128)(2,1)S(1)}, u32[]{:S(2)}, u32[]{:S(2)}) collective-permute-start(bf16[1024,128]{1,0:T(8,128)(2,1)S(1)} %get-tuple-element.16), channel_id=1, source_target_pairs={{0,4},{2,6},{4,8},{5,1},{6,10},{7,3},{8,12},{9,5},{10,14},{11,7},{... | collective-permute-start | bytes 786440 | tf_op jit(solution)/shard_map/ppermute | solution.py:393
  18.5 3.1 %prepare.1 = (s32[88,128]{1,0:T(8,128)}, s32[16,128]{1,0:T(8,128)}, bf16[128,256]{1,0:T(8,128)(2,1)}, bf16[128,128]{1,0:T(8,128)(2,1)}, bf16[128,128]{1,0:T(8,128)(2,1)}, /*index=5*/f32[72,128]{1,0:T(8,128)}) custom-call(s32[128]{0:T(128)} %refs_0_.3, s32[128,128]{1,0:T(8,128)} %refs_1_.1, bf16[6,80]{1,0:T(8,128)(2,1)} %bitcast.8, bf16[80,96]{1,0:T(8,128)(2,1)} %refs_3_.1, ...), custom_call_target="tpu_custom_call" | custom-call | tf_op jit(solution)/shard_map/prepare/pallas_call | solution.py:156
  21.6 0.0 copy-start.7
  21.6 3.6 %collective-permute-done.3.other_ref = bf16[1024,128]{1,0:T(8,128)(2,1)S(1)} collective-permute-done((bf16[1024,128]{1,0:T(8,128)(2,1)S(1)}, bf16[1024,128]{1,0:T(8,128)(2,1)S(1)}, u32[]{:S(2)}, u32[]{:S(2)}) %collective-permute-start.3) | collective-permute-done | bytes 262176 | tf_op jit(solution)/shard_map/ppermute | solution.py:393
  25.1 0.0 copy-done.7
  25.1 0.0 copy-start.1
  25.1 0.8 %copy-done.1 = bf16[128,256]{1,0:T(8,128)(2,1)S(1)} copy-done((bf16[128,256]{1,0:T(8,128)(2,1)S(1)}, bf16[128,256]{1,0:T(8,128)(2,1)}, u32[]{:S(2)}) %copy-start.1) | copy-done | bytes 65560
  26.0 0.0 copy-start.2
  26.0 0.8 %copy-done.2 = s32[88,128]{1,0:T(8,128)S(1)} copy-done((s32[88,128]{1,0:T(8,128)S(1)}, s32[88,128]{1,0:T(8,128)}, u32[]{:S(2)}) %copy-start.2) | copy-done | bytes 45080
  26.8 0.0 copy-start.3
  26.8 0.8 %copy-done.3 = f32[72,128]{1,0:T(8,128)S(1)} copy-done((f32[72,128]{1,0:T(8,128)S(1)}, f32[72,128]{1,0:T(8,128)}, u32[]{:S(2)}) %copy-start.3) | copy-done | bytes 36888
  27.5 0.0 copy-start.4
  27.5 0.8 %copy-done.4 = bf16[128,128]{1,0:T(8,128)(2,1)S(1)} copy-done((bf16[128,128]{1,0:T(8,128)(2,1)S(1)}, bf16[128,128]{1,0:T(8,128)(2,1)}, u32[]{:S(2)}) %copy-start.4) | copy-done | bytes 32792
  28.3 0.0 copy-start.5
  28.3 0.8 %copy-done.5 = bf16[128,128]{1,0:T(8,128)(2,1)S(1)} copy-done((bf16[128,128]{1,0:T(8,128)(2,1)S(1)}, bf16[128,128]{1,0:T(8,128)(2,1)}, u32[]{:S(2)}) %copy-start.5) | copy-done | bytes 32792
  29.1 9.8 %encode.1 = (f32[24,128]{1,0:T(8,128)S(1)}, f32[24,128]{1,0:T(8,128)S(1)}) custom-call(bf16[2048,128]{1,0:T(8,128)(2,1)S(1)} %get-tuple-element.15.own_ref, bf16[1024,128]{1,0:T(8,128)(2,1)S(1)} %collective-permute-done.3.other_ref, s32[88,128]{1,0:T(8,128)S(1)} %copy-done.2, s32[16,128]{1,0:T(8,128)S(1)} %copy-done.7, bf16[128,256]{1,0:T(8,128)(2,1)S(1)} %copy-done.1, ...), custom_call_target="tpu_custom_call" | custom-call | tf_op jit(solution)/shard_map/encode/pallas_call | solution.py:337
  38.9 0.1 collective-permute-start.4
  39.0 3.7 %collective-permute-done.4 = f32[24,128]{1,0:T(8,128)S(1)} collective-permute-done((f32[24,128]{1,0:T(8,128)S(1)}, f32[24,128]{1,0:T(8,128)S(1)}, u32[]{:S(2)}, u32[]{:S(2)}) %collective-permute-start.4) | collective-permute-done | bytes 12320 | tf_op jit(solution)/shard_map/ppermute | solution.py:395
  42.6 0.6 %add.3 = f32[24,128]{1,0:T(8,128)} add(f32[24,128]{1,0:T(8,128)S(1)} %get-tuple-element.23, f32[24,128]{1,0:T(8,128)S(1)} %collective-permute-done.4) | non-fusion elementwise | flops 3072 | bytes 36864 | tf_op jit(solution)/shard_map/add | solution.py:395
Async XLA Ops:
  0.0 12.3 %copy-start.9 = (s32[2,1]{0,1:T(1,128)S(1)}, s32[2,1]{0,1:T(1,128)}, u32[]{:S(2)}) copy-start(s32[2,1]{0,1:T(1,128)} %param.16) | copy-start | bytes 28
  0.0 5.8 %collective-permute-start = (bf16[24,2048]{1,0:T(8,128)(2,1)}, bf16[24,2048]{1,0:T(8,128)(2,1)S(1)}, u32[]{:S(2)}, u32[]{:S(2)}) collective-permute-start(bf16[24,2048]{1,0:T(8,128)(2,1)} %refs_0_.2), channel_id=1, source_target_pairs={{0,1},{1,0},{2,3},{3,2},{4,5},{5,4},{6,7},{7,6},{8,9},{9,8},{10,11... | collective-permute-start | bytes 294920 | tf_op jit(solution)/shard_map/ppermute | solution.py:379
  1.6 7.7 %collective-permute-start.1 = (bf16[24,2048]{1,0:T(8,128)(2,1)}, bf16[24,2048]{1,0:T(8,128)(2,1)S(1)}, u32[]{:S(2)}, u32[]{:S(2)}) collective-permute-start(bf16[24,2048]{1,0:T(8,128)(2,1)} %refs_0_.2), channel_id=1, source_target_pairs={{0,2},{1,3},{2,0},{3,1},{4,6},{5,7},{6,4},{7,5},{8,10},{9,11},{10,... | collective-permute-start | bytes 294920 | tf_op jit(solution)/shard_map/ppermute | solution.py:379
  1.9 10.3 %collective-permute-start.2 = (bf16[24,2048]{1,0:T(8,128)(2,1)}, bf16[24,2048]{1,0:T(8,128)(2,1)S(1)}, u32[]{:S(2)}, u32[]{:S(2)}) collective-permute-start(bf16[24,2048]{1,0:T(8,128)(2,1)} %refs_0_.2), channel_id=1, source_target_pairs={{0,3},{1,2},{2,1},{3,0},{4,7},{5,6},{6,5},{7,4},{8,11},{9,10},{10,... | collective-permute-start | bytes 294920 | tf_op jit(solution)/shard_map/ppermute | solution.py:379
  12.3 0.9 %copy-start = (bf16[24,2048]{1,0:T(8,128)(2,1)S(1)}, bf16[24,2048]{1,0:T(8,128)(2,1)}, u32[]{:S(2)}) copy-start(bf16[24,2048]{1,0:T(8,128)(2,1)} %refs_0_.2) | copy-start | bytes 294916
  13.1 0.7 %copy-start.6 = (bf16[3,2048]{1,0:T(4,128)(2,1)S(1)}, bf16[3,2048]{1,0:T(4,128)(2,1)}, u32[]{:S(2)}) copy-start(bf16[3,2048]{1,0:T(4,128)(2,1)} %refs_4_.1) | copy-start | bytes 36868
  13.9 0.7 %copy-start.8 = (s32[2,1024]{1,0:T(2,128)S(1)}, s32[2,1024]{1,0:T(2,128)}, u32[]{:S(2)}) copy-start(s32[2,1024]{1,0:T(2,128)} %refs_5_.2) | copy-start | bytes 24580
  16.6 8.6 %collective-permute-start.3 = (bf16[1024,128]{1,0:T(8,128)(2,1)S(1)}, bf16[1024,128]{1,0:T(8,128)(2,1)S(1)}, u32[]{:S(2)}, u32[]{:S(2)}) collective-permute-start(bf16[1024,128]{1,0:T(8,128)(2,1)S(1)} %get-tuple-element.16), channel_id=1, source_target_pairs={{0,4},{2,6},{4,8},{5,1},{6,10},{7,3},{8,12},{9,5},{10,14},{11,7},{... | collective-permute-start | bytes 786440 | tf_op jit(solution)/shard_map/ppermute | solution.py:393
  21.6 3.6 %copy-start.7 = (s32[16,128]{1,0:T(8,128)S(1)}, s32[16,128]{1,0:T(8,128)}, u32[]{:S(2)}) copy-start(s32[16,128]{1,0:T(8,128)} %get-tuple-element.18.spots_ref) | copy-start | bytes 24580
  25.1 0.8 %copy-start.1 = (bf16[128,256]{1,0:T(8,128)(2,1)S(1)}, bf16[128,256]{1,0:T(8,128)(2,1)}, u32[]{:S(2)}) copy-start(bf16[128,256]{1,0:T(8,128)(2,1)} %get-tuple-element.19.table_w) | copy-start | bytes 196612
  26.0 0.8 %copy-start.2 = (s32[88,128]{1,0:T(8,128)S(1)}, s32[88,128]{1,0:T(8,128)}, u32[]{:S(2)}) copy-start(s32[88,128]{1,0:T(8,128)} %get-tuple-element.17.rows_ref) | copy-start | bytes 135172
  26.8 0.8 %copy-start.3 = (f32[72,128]{1,0:T(8,128)S(1)}, f32[72,128]{1,0:T(8,128)}, u32[]{:S(2)}) copy-start(f32[72,128]{1,0:T(8,128)} %get-tuple-element.22.node_pre) | copy-start | bytes 110596
  27.5 0.8 %copy-start.4 = (bf16[128,128]{1,0:T(8,128)(2,1)S(1)}, bf16[128,128]{1,0:T(8,128)(2,1)}, u32[]{:S(2)}) copy-start(bf16[128,128]{1,0:T(8,128)(2,1)} %get-tuple-element.20.hidden_w) | copy-start | bytes 98308
  28.3 0.8 %copy-start.5 = (bf16[128,128]{1,0:T(8,128)(2,1)S(1)}, bf16[128,128]{1,0:T(8,128)(2,1)}, u32[]{:S(2)}) copy-start(bf16[128,128]{1,0:T(8,128)(2,1)} %get-tuple-element.21.out_w) | copy-start | bytes 98308
  38.9 3.8 %collective-permute-start.4 = (f32[24,128]{1,0:T(8,128)S(1)}, f32[24,128]{1,0:T(8,128)S(1)}, u32[]{:S(2)}, u32[]{:S(2)}) collective-permute-start(f32[24,128]{1,0:T(8,128)S(1)} %get-tuple-element.24), channel_id=1, source_target_pairs={{0,1},{1,0},{2,3},{3,2},{4,5},{5,4},{6,7},{7,6},{8,9},{9,8},{10,11... | collective-permute-start | bytes 36872 | tf_op jit(solution)/shard_map/ppermute | solution.py:395
